TPU v7x, 32 devices: a whole 2x2x4 slice. The times are simulated.
32 devices in a mesh: gx: 4 (over z), gy: 2 (over y), gz: 4 (over x, core).
Axes of the slice: x: 2, y: 2, z: 4, core: 2. Of those that a mesh axis runs over, the one named last changes fastest.
Arguments:
- cell_counts: int32 [16, 4, 16], P('gx', 'gy', 'gz'), may hold values from 64 to 128
- grid_offset: int32 [16, 4, 16, 3, 128], P('gx', 'gy', 'gz'), may hold values from 0 to 14
- fraction: float32 [16, 4, 16, 3, 128], P('gx', 'gy', 'gz'), may hold values from 0 to 1
- species: int32 [16, 4, 16, 128], P('gx', 'gy', 'gz'), may hold values from 0 to 1
- species_density: float32 [2], replicated, may hold values from 0.01 to 0.03
- species_pair: float32 [2], replicated, may hold values from 0.05 to 0.2
- species_embed: float32 [2], replicated, may hold values from 0.5 to 2
- species_charge: float32 [2], replicated, may hold values from -3 to 3
Outputs:
- forces: float32 [16, 4, 16, 3, 128], P('gx', 'gy', 'gz')
- density: float32 [16, 4, 16, 128], P('gx', 'gy', 'gz')
Inputs may be any that keep to these rules, and one draw needn't show every extreme that they name: `cell_counts`: slots below the count hold atoms; the others are padding. `grid_offset`: an atom's stencil points lie in its own cell.
All inputs are finite; a program needn't handle non-finite values.
Results may differ from a plain program's by a relative error of at most 0.0003.
Values sent between devices are 32-bit elements; how exact they have to be, the bound alone decides.
No kernel may reach another device: no remote copies, remote signals or barrier semaphores. Data moves between devices by JAX's collectives and lax.ppermute only.
A program may use at most 128 MiB of HBM per device.

v0:
```python
import math

import jax
import jax.numpy as jnp
from jax import lax
from jax.sharding import PartitionSpec as P

NSPEC = 2
PPC = 16


EWALD_SPLIT = 0.7
COUPLING = 8.0
HIGHEST_PRECISION = lax.Precision.HIGHEST
neighbour_shifts = [
    (shift_x, shift_y, shift_z)
    for shift_x in (-1, 0, 1)
    for shift_y in (-1, 0, 1)
    for shift_z in (-1, 0, 1)
]


def padded(block, sides, width):
    for axis, dim in sides:
        count = lax.axis_size(axis)
        forward = [(i, i + 1) for i in range(count - 1)]
        forward.append((count - 1, 0))
        backward = [(target, source) for source, target in forward]
        low = lax.ppermute(
            lax.slice_in_dim(block, block.shape[dim] - width, None, axis=dim), axis, forward
        )
        high = lax.ppermute(lax.slice_in_dim(block, 0, width, axis=dim), axis, backward)
        block = jnp.concatenate([low, block, high], axis=dim)
    return block


def species_value(species, lookup_table):
    result = jnp.zeros(species.shape, jnp.float32)
    for kind_index in range(NSPEC):
        result = result + jnp.where(species == kind_index, lookup_table[kind_index], 0.0)
    return result


def stencil(offsets, fractions):
    points = lax.broadcasted_iota(jnp.int32, offsets.shape + (PPC,), offsets.ndim)
    lower_point = (points == offsets[..., None]).astype(jnp.float32)
    upper_point = (points == offsets[..., None] + 1).astype(jnp.float32)
    weights = lower_point * (1.0 - fractions[..., None]) + upper_point * fractions[..., None]
    return (weights, upper_point - lower_point)


def spread_cells(charges, weights_x, weights_y, weights_z):
    batch_size, slot_count = charges.shape
    pair_plane = (weights_y[:, :, :, None] * weights_z[:, :, None, :]).reshape(
        batch_size, slot_count, PPC * PPC
    )
    return jnp.einsum(
        "bax,bay->bxy", weights_x * charges[:, :, None], pair_plane, precision=HIGHEST_PRECISION
    )


def outer_plane(first_weights, second_weights):
    batch_size, slot_count, width_count = first_weights.shape
    return (first_weights[:, :, :, None] * second_weights[:, :, None, :]).reshape(
        batch_size, slot_count, width_count * width_count
    )


def sample_cells(blocks, charges, weights_x, weights_y, weights_z, slope_x, slope_y, slope_z):
    plain_x = jnp.einsum("bax,bxy->bay", weights_x, blocks, precision=HIGHEST_PRECISION)
    tilted_x = jnp.einsum("bax,bxy->bay", slope_x, blocks, precision=HIGHEST_PRECISION)
    force_x = -charges * jnp.sum(tilted_x * outer_plane(weights_y, weights_z), axis=2)
    force_y = -charges * jnp.sum(plain_x * outer_plane(slope_y, weights_z), axis=2)
    force_z = -charges * jnp.sum(plain_x * outer_plane(weights_y, slope_z), axis=2)
    return jnp.stack([force_x, force_y, force_z], axis=1)


def signed_modes(indices, total):
    return jnp.where(2 * indices >= total, indices - total, indices)


def green_factor(modes_x, modes_y, modes_z, length_x, length_y, length_z):
    wave_x = modes_x.astype(jnp.float32) * (2.0 * math.pi / length_x)
    wave_y = modes_y.astype(jnp.float32) * (2.0 * math.pi / length_y)
    wave_z = modes_z.astype(jnp.float32) * (2.0 * math.pi / length_z)
    squared = wave_x * wave_x + wave_y * wave_y + wave_z * wave_z
    anchor = (modes_x == 0) & (modes_y == 0) & (modes_z == 0)
    safe_square = jnp.where(anchor, 1.0, squared)
    return jnp.where(
        anchor,
        0.0,
        4.0 * math.pi * jnp.exp(-squared / (4.0 * EWALD_SPLIT * EWALD_SPLIT)) / safe_square,
    )


def dft_tables(length):
    product = lax.broadcasted_iota(jnp.int32, (length, length), 0) * lax.broadcasted_iota(
        jnp.int32, (length, length), 1
    )
    phases = (product % length).astype(jnp.float32) * (2.0 * math.pi / length)
    return (jnp.cos(phases), jnp.sin(phases))


def line_transform(real_part, imag_part, along_axis, sign_value):
    cosine_table, sine_table = dft_tables(real_part.shape[along_axis])
    real_last = jnp.moveaxis(real_part, along_axis, -1)
    imag_last = jnp.moveaxis(imag_part, along_axis, -1)
    real_cos = jnp.matmul(real_last, cosine_table, precision=HIGHEST_PRECISION)
    real_sin = jnp.matmul(real_last, sine_table, precision=HIGHEST_PRECISION)
    imag_cos = jnp.matmul(imag_last, cosine_table, precision=HIGHEST_PRECISION)
    imag_sin = jnp.matmul(imag_last, sine_table, precision=HIGHEST_PRECISION)
    new_real = real_cos - sign_value * imag_sin
    new_imag = imag_cos + sign_value * real_sin
    return (jnp.moveaxis(new_real, -1, along_axis), jnp.moveaxis(new_imag, -1, along_axis))


def pair_terms(positions, other_positions, shift_triple, not_self):
    shift_vector = jnp.asarray(shift_triple, jnp.float32)
    separation = (
        shift_vector[:, None, None] + other_positions[..., :, None, :] - positions[..., :, :, None]
    )
    squared = jnp.sum(separation * separation, axis=-3)
    weight = jnp.maximum(1.0 - squared, 0.0)
    if shift_triple == (0, 0, 0):
        weight = weight * not_self
    return (separation, weight)


def window(rows, shift_triple, cells_y, cells_z):
    return rows[
        1 + shift_triple[0],
        1 + shift_triple[1] : 1 + shift_triple[1] + cells_y,
        1 + shift_triple[2] : 1 + shift_triple[2] + cells_z,
    ]


def on_device(
    cell_counts,
    grid_offset,
    fraction,
    species,
    species_density,
    species_pair,
    species_embed,
    species_charge,
):
    cells_x, cells_y, cells_z, components, slot_count = fraction.shape
    slot_index = lax.broadcasted_iota(jnp.int32, species.shape, 3)
    alive_mask = (slot_index < cell_counts[..., None]).astype(jnp.float32)
    positions = (grid_offset.astype(jnp.float32) + 0.5 + fraction) / PPC
    density_coef = species_value(species, species_density) * alive_mask
    repulsion = species_value(species, species_pair) * alive_mask
    embedding = species_value(species, species_embed)
    charge = species_value(species, species_charge) * alive_mask
    not_self = (
        lax.broadcasted_iota(jnp.int32, (slot_count, slot_count), 0)
        != lax.broadcasted_iota(jnp.int32, (slot_count, slot_count), 1)
    ).astype(jnp.float32)
    packed_atoms = jnp.concatenate(
        [positions, density_coef[:, :, :, None, :], repulsion[:, :, :, None, :]], axis=3
    )
    extended = padded(packed_atoms, (("gx", 0), ("gy", 1), ("gz", 2)), 1)
    row_ids = jnp.arange(cells_x, dtype=jnp.int32)

    def density_row(row):
        near_rows = lax.dynamic_slice_in_dim(extended, row, 3, 0)
        own = lax.dynamic_index_in_dim(positions, row, 0, keepdims=False)
        total = jnp.zeros((cells_y, cells_z, slot_count), jnp.float32)
        for shift_triple in neighbour_shifts:
            near = window(near_rows, shift_triple, cells_y, cells_z)
            separation, weight = pair_terms(own, near[:, :, 0:3, :], shift_triple, not_self)
            total = total + jnp.sum(
                weight * weight * weight * near[:, :, 3, :][..., None, :], axis=-1
            )
        return total

    density = lax.map(density_row, row_ids) * alive_mask
    slope_embed = -embedding * alive_mask / (2.0 * jnp.sqrt(1.0 + density))
    extended_slope = padded(slope_embed, (("gx", 0), ("gy", 1), ("gz", 2)), 1)

    def force_row(row):
        near_rows = lax.dynamic_slice_in_dim(extended, row, 3, 0)
        near_slopes = lax.dynamic_slice_in_dim(extended_slope, row, 3, 0)
        own = lax.dynamic_index_in_dim(positions, row, 0, keepdims=False)
        own_rep = lax.dynamic_index_in_dim(repulsion, row, 0, keepdims=False)
        own_coef = lax.dynamic_index_in_dim(density_coef, row, 0, keepdims=False)
        own_slope = lax.dynamic_index_in_dim(slope_embed, row, 0, keepdims=False)
        total = jnp.zeros((cells_y, cells_z, 3, slot_count), jnp.float32)
        for shift_triple in neighbour_shifts:
            near = window(near_rows, shift_triple, cells_y, cells_z)
            separation, weight = pair_terms(own, near[:, :, 0:3, :], shift_triple, not_self)
            other_coef = near[:, :, 3, :][..., None, :]
            other_rep = near[:, :, 4, :][..., None, :]
            other_slope = window(near_slopes, shift_triple, cells_y, cells_z)[..., None, :]
            coefficient = -2.0 * own_rep[
                ..., :, None
            ] * other_rep * weight - 3.0 * weight * weight * (
                own_slope[..., :, None] * other_coef + other_slope * own_coef[..., :, None]
            )
            total = total + 2.0 * jnp.sum(coefficient[..., None, :, :] * separation, axis=-1)
        return total

    eam_force = lax.map(force_row, row_ids)
    flat_cells = cells_x * cells_y * cells_z

    def flatten(values):
        return values.reshape((flat_cells,) + values.shape[3:])

    stencils = [
        stencil(
            flatten(grid_offset[:, :, :, axis_index, :]), flatten(fraction[:, :, :, axis_index, :])
        )
        for axis_index in range(3)
    ]
    flat_charge = flatten(charge)
    blocks = spread_cells(flat_charge, stencils[0][0], stencils[1][0], stencils[2][0])
    charge_brick = (
        blocks.reshape(cells_x, cells_y, cells_z, PPC, PPC, PPC)
        .transpose(0, 3, 1, 4, 2, 5)
        .reshape(cells_x * PPC, cells_y * PPC, cells_z * PPC)
    )
    brick_x, brick_y, brick_z = charge_brick.shape
    length_x = brick_x * lax.axis_size("gx")
    length_y = brick_y * lax.axis_size("gy")
    depth_lines = lax.all_to_all(charge_brick, "gz", split_axis=1, concat_axis=2, tiled=True)
    quarter_y = depth_lines.shape[1]
    depth_length = depth_lines.shape[2]
    cosine_table, sine_table = dft_tables(depth_length)
    line_real = jnp.matmul(depth_lines, cosine_table, precision=HIGHEST_PRECISION)
    line_imag = -jnp.matmul(depth_lines, sine_table, precision=HIGHEST_PRECISION)
    stacked = jnp.stack([line_real, line_imag])[:, None]
    planes = lax.all_to_all(stacked, ("gx", "gy", "gz"), split_axis=4, concat_axis=1, tiled=True)
    group_size = planes.shape[1]
    rows_gx = lax.axis_size("gx")
    rest_count = group_size // rows_gx
    plane_depth = planes.shape[4]
    planes = (
        planes.reshape(2, rows_gx, rest_count, brick_x, quarter_y, plane_depth)
        .transpose(0, 5, 1, 3, 2, 4)
        .reshape(2, plane_depth, length_x, length_y)
    )
    real_part, imag_part = line_transform(planes[0], planes[1], 2, -1.0)
    real_part, imag_part = line_transform(real_part, imag_part, 1, -1.0)
    first_mode = lax.axis_index(("gx", "gy", "gz")) * plane_depth
    modes_z = signed_modes(
        first_mode + lax.broadcasted_iota(jnp.int32, (plane_depth, 1, 1), 0), depth_length
    )
    modes_x = signed_modes(lax.broadcasted_iota(jnp.int32, (1, length_x, 1), 1), length_x)
    modes_y = signed_modes(lax.broadcasted_iota(jnp.int32, (1, 1, length_y), 2), length_y)
    factor = green_factor(modes_x, modes_y, modes_z, length_x, length_y, depth_length)
    real_part, imag_part = line_transform(real_part * factor, imag_part * factor, 1, 1.0)
    real_part, imag_part = line_transform(real_part, imag_part, 2, 1.0)
    planes_return = (
        jnp.stack([real_part, imag_part])
        .reshape(2, plane_depth, rows_gx, brick_x, rest_count, quarter_y)
        .transpose(0, 2, 4, 3, 5, 1)
        .reshape(2, group_size, brick_x, quarter_y, plane_depth)
    )
    returned = lax.all_to_all(
        planes_return, ("gx", "gy", "gz"), split_axis=1, concat_axis=4, tiled=True
    )
    real_part, imag_part = (returned[0, 0], returned[1, 0])
    potential_lines = (
        jnp.matmul(real_part, cosine_table, precision=HIGHEST_PRECISION)
        - jnp.matmul(imag_part, sine_table, precision=HIGHEST_PRECISION)
    ) / (length_x * length_y * depth_length)
    potential = lax.all_to_all(potential_lines, "gz", split_axis=2, concat_axis=1, tiled=True)
    blocks_back = (
        potential.reshape(cells_x, PPC, cells_y, PPC, cells_z, PPC)
        .transpose(0, 2, 4, 1, 3, 5)
        .reshape(flat_cells, PPC, PPC * PPC)
    )
    electric = sample_cells(
        blocks_back,
        flat_charge,
        stencils[0][0],
        stencils[1][0],
        stencils[2][0],
        stencils[0][1],
        stencils[1][1],
        stencils[2][1],
    ).reshape(cells_x, cells_y, cells_z, 3, slot_count)
    forces = (eam_force + COUPLING * electric) * alive_mask[:, :, :, None, :]
    return (forces, density)


def solution(mesh):
    return jax.shard_map(
        on_device,
        mesh=mesh,
        in_specs=(
            P("gx", "gy", "gz"),
            P("gx", "gy", "gz", None, None),
            P("gx", "gy", "gz", None, None),
            P("gx", "gy", "gz", None),
            P(),
            P(),
            P(),
            P(),
        ),
        out_specs=(P("gx", "gy", "gz", None, None), P("gx", "gy", "gz", None)),
        check_vma=False,
    )
```

profile of v0, /device:TPU:1, one launch (start us, length us, event | category | flops | bytes accessed | tf_op | source)
XLA Modules:
  0.0 467.6 jit_solution(6046106370680554486)
XLA Ops:
  3.7 4.5 broadcast_multiply_fusion
  10.2 3.6 fusion.238
  13.8 2.6 reshape.1344
  16.4 6.8 %copy.257 = f32[4,2,4,16,16,16]{5,2,4,1,3,0:T(4,128)} copy(f32[4,2,4,16,16,16]{5,4,3,2,1,0:T(8,128)} %reshape.1344) | data formatting | bytes 1048576 | tf_op jit(solution)/shard_map/reshape | solution.py:218
  23.3 3.7 reshape.1345
  28.3 12.0 %all_to_all.63 = f32[4,1,32768]{2,1,0:T(1,128)S(1)} all-to-all(f32[4,1,32768]{2,1,0:T(1,128)S(1)} %reshape.1380), channel_id=1, replica_groups=mesh['gx'=4,'gy'=2,'gz'=4] {'gz'}, dimensions={0} | all-to-all | bytes 1048576 | tf_op jit(solution)/shard_map/all_to_all | solution.py:225
  48.9 2.6 copy.216
  51.5 2.4 reshape.1382
  53.9 5.7 %all-to-all-start.1 = ((f32[32,1,8192]{2,1,0:T(1,128)}), f32[32,1,8192]{2,1,0:T(1,128)S(1)}, u32[]{:S(2)}, u32[]{:S(2)}) async-start(f32[32,1,8192]{2,1,0:T(1,128)} %reshape.1382), calls=%async_computation.1 | async-start | bytes 2097152 | tf_op jit(solution)/shard_map/all_to_all | solution.py:232
  59.9 24.9 %all-to-all-done.1 = f32[32,1,8192]{2,1,0:T(1,128)S(1)} async-done(((f32[32,1,8192]{2,1,0:T(1,128)}), f32[32,1,8192]{2,1,0:T(1,128)S(1)}, u32[]{:S(2)}, u32[]{:S(2)}) %all-to-all-start.1) | async-done | bytes 1048608 | tf_op jit(solution)/shard_map/all_to_all | solution.py:232
  84.8 4.4 reduce.1
  89.2 2.4 reshape.1383
  119.7 2.3 reshape.1384
  122.1 4.6 all-to-all-start.2
  127.9 2.7 add_select_fusion.4
  134.0 13.9 %collective-permute-done = f32[1,2,4,5,128]{4,3,2,1,0:T(8,128)S(1)} collective-permute-done((f32[1,2,4,5,128]{4,3,2,1,0:T(8,128)S(1)}, f32[1,2,4,5,128]{4,3,2,1,0:T(8,128)S(1)}, u32[]{:S(2)}, u32[]{:S(2)}) %collective-permute-start) | collective-permute-done | bytes 20512 | tf_op jit(solution)/shard_map/ppermute | solution.py:29
  149.7 5.6 %copy.229 = f32[32,128,256]{2,1,0:T(8,128)} copy(f32[32,128,256]{1,2,0:T(8,128)} %bitcast.763) | data formatting | bytes 8388608 | tf_op jit(solution)/shard_map/mul | solution.py:54
  155.3 5.6 %copy.230 = f32[32,128,256]{2,1,0:T(8,128)} copy(f32[32,128,256]{1,2,0:T(8,128)} %bitcast.767) | data formatting | bytes 8388608 | tf_op jit(solution)/shard_map/mul | solution.py:64
  160.9 5.6 %copy.231 = f32[32,128,256]{2,1,0:T(8,128)} copy(f32[32,128,256]{1,2,0:T(8,128)} %bitcast.766) | data formatting | bytes 8388608 | tf_op jit(solution)/shard_map/mul | solution.py:64
  166.6 3.2 collective-permute-start.4
  171.5 2.3 collective-permute-done.5
  174.0 4.3 reduce.2
  182.0 2.6 fusion.225
  188.7 3.9 all-to-all-start.3
  192.7 87.3 %while.26 = (s32[]{:T(128)}, f32[4,2,4,128]{3,2,1,0:T(4,128)S(1)}, s32[4]{0:T(128)S(1)}, f32[6,4,6,5,128]{4,2,1,3,0:T(8,128)S(1)}, f32[4,2,4,3,128]{4,3,2,1,0:T(...) while((s32[]{:T(128)}, f32[4,2,4,128]{3,2,1,0:T(4,128)S(1)}, ...), condition=%wide.region_55.56_spmd.clone.clone.clone, body=%wide.region_0.55_spmd.sunk.clone.clone.sunk.clone | while | flops 49787912 | bytes 31814928 | solution.py:177
  200.0 5.2 %multiply_reduce_fusion.35 = (f32[2,4,128,128]{3,2,1,0:T(8,128)S(1)}, f32[2,4,128,128]{3,2,1,0:T(8,128)S(1)}, f32[2,4,128,128]{3,2,1,0:T(8,128)S(1)}, f32[2,4,12...) fusion(f32[2,4,3,128]{3,2,1,0:T(4,128)S(1)} %copy.382, ...), kind=kLoop, calls=%fused_computation.27.clone.1.clone | loop fusion | flops 18874368 | bytes 9670656 | tf_op jit(solution)/shard_map/while/body/eval_jaxpr/reduce_sum | solution.py:122
  209.8 2.5 multiply_reduce_fusion.34
  221.8 5.2 %multiply_reduce_fusion.35 = (f32[2,4,128,128]{3,2,1,0:T(8,128)S(1)}, f32[2,4,128,128]{3,2,1,0:T(8,128)S(1)}, f32[2,4,128,128]{3,2,1,0:T(8,128)S(1)}, f32[2,4,12...) fusion(f32[2,4,3,128]{3,2,1,0:T(4,128)S(1)} %copy.382, ...), kind=kLoop, calls=%fused_computation.27.clone.1.clone | loop fusion | flops 18874368 | bytes 9670656 | tf_op jit(solution)/shard_map/while/body/eval_jaxpr/reduce_sum | solution.py:122
  231.5 2.5 multiply_reduce_fusion.34
  243.6 5.2 %multiply_reduce_fusion.35 = (f32[2,4,128,128]{3,2,1,0:T(8,128)S(1)}, f32[2,4,128,128]{3,2,1,0:T(8,128)S(1)}, f32[2,4,128,128]{3,2,1,0:T(8,128)S(1)}, f32[2,4,12...) fusion(f32[2,4,3,128]{3,2,1,0:T(4,128)S(1)} %copy.382, ...), kind=kLoop, calls=%fused_computation.27.clone.1.clone | loop fusion | flops 18874368 | bytes 9670656 | tf_op jit(solution)/shard_map/while/body/eval_jaxpr/reduce_sum | solution.py:122
  253.3 2.5 multiply_reduce_fusion.34
  265.4 5.2 %multiply_reduce_fusion.35 = (f32[2,4,128,128]{3,2,1,0:T(8,128)S(1)}, f32[2,4,128,128]{3,2,1,0:T(8,128)S(1)}, f32[2,4,128,128]{3,2,1,0:T(8,128)S(1)}, f32[2,4,12...) fusion(f32[2,4,3,128]{3,2,1,0:T(4,128)S(1)} %copy.382, ...), kind=kLoop, calls=%fused_computation.27.clone.1.clone | loop fusion | flops 18874368 | bytes 9670656 | tf_op jit(solution)/shard_map/while/body/eval_jaxpr/reduce_sum | solution.py:122
  275.1 2.5 multiply_reduce_fusion.34
  279.9 2.1 reduce.3
  283.5 3.2 reshape.1348
  286.7 4.7 copy.228
  291.4 3.5 reshape.1349
  294.9 5.8 %multiply_reduce_fusion.29 = f32[32,128]{1,0:T(8,128)S(1)} fusion(f32[32,128,256]{2,1,0:T(8,128)} %copy.229, f32[32,16,256]{2,1,0:T(8,128)S(1)} %reshape.1349, s32[32,128]{1,0:T(8,128)S(1)} %bitcast.790, s32[32,128]{1,0:T(8,128)S(1)} %broadcast_add_fusion.3), kind=kOutput, calls=%fused_computation.579 | convolution fusion | flops 203747328 | bytes 4767744 | tf_op jit(solution)/shard_map/bax,bxy->bay/dot_general | solution.py:71
  300.9 6.6 %multiply_reduce_fusion.28 = (f32[32,128]{1,0:T(8,128)S(1)}, f32[32,128]{1,0:T(8,128)S(1)}) fusion(f32[32,128,256]{2,1,0:T(8,128)S(1)} %copy-done.1, f32[32,128,256]{2,1,0:T(8,128)} %copy.231, f32[32,16,256]{2,1,0:T(8,128)S(1)} %reshape.1349, f32[32,128]{1,0:T(8,128)S(1)} %bitcast.794, f32[32,128]{1,0:T(8,128)S(1)} %broadcast_subtract_fusion.2, ...), kind=kOutput, calls=%fused_computation.578 | convolution fusion | flops 205840384 | bytes 9011200 | tf_op jit(solution)/shard_map/bax,bxy->bay/dot_general | solution.py:70
  307.5 3.1 multiply_bitcast_fusion.2
  310.7 5.3 %collective-permute-start.6 = (f32[1,2,4,128]{3,2,1,0:T(4,128)S(1)}, f32[1,2,4,128]{3,2,1,0:T(4,128)S(1)}, u32[]{:S(2)}, u32[]{:S(2)}) collective-permute-start(f32[1,2,4,128]{3,2,1,0:T(4,128)S(1)} %get-tuple-element.982), channel_id=1, source_target_pairs={{0,8},{8,16},{16,24},{24,0},{1,9},{9,17},{17,25},{25,1},{2,10},{10... | collective-permute-start | bytes 12296 | tf_op jit(solution)/shard_map/ppermute | solution.py:29
  322.3 3.5 collective-permute-start.10
  326.6 2.3 collective-permute-done.11
  329.1 137.6 %while.27 = (s32[]{:T(128)}, f32[4,2,4,3,128]{4,2,1,0,3:T(4,128)S(1)}, s32[4]{0:T(128)S(1)}, f32[4,2,4,128]{3,2,1,0:T(4,128)S(1)}, f32[6,4,6,5,128]{4,2,1,3,0:T(...) while((s32[]{:T(128)}, ...), condition=%wide.region_111.112_spmd.clone.clone.clone, body=%wide.region_56.111_spmd.sunk.clone.clone.sunk.clone | while | flops 99335176 | bytes 61772524 | solution.py:203
  335.3 3.0 fusion.548
  340.1 4.6 fusion.550
  347.7 3.8 fusion.560
  353.4 4.7 %fusion.558 = (f32[2,4,3,128]{3,2,1,0:T(4,128)S(1)}, f32[2,4,3,128]{3,2,1,0:T(4,128)S(1)}, f32[2,4,3,128]{3,2,1,0:T(4,128)S(1)}, f32[2,4,3,128]{3,2,1,0:T(4,128)...) fusion(f32[2,4,128,128]{3,2,1,0:T(8,128)S(1)} %get-tuple-elemen, ...), kind=kLoop, calls=%fused_computation.265.clone.1.clone | loop fusion | flops 10589184 | bytes 4952064 | tf_op jit(solution)/shard_map/while/body/eval_jaxpr/reduce_sum | solution.py:200
  358.9 4.7 %fusion.554 = (f32[2,4,3,128]{3,2,1,0:T(4,128)S(1)}, f32[2,4,3,128]{3,2,1,0:T(4,128)S(1)}, f32[2,4,3,128]{3,2,1,0:T(4,128)S(1)}, f32[2,4,3,128]{3,2,1,0:T(4,128)...) fusion(f32[2,4,128,128]{3,2,1,0:T(8,128)S(1)} %get-tuple-elemen, ...), kind=kLoop, calls=%fused_computation.263.clone.1.clone | loop fusion | flops 10589184 | bytes 4952064 | tf_op jit(solution)/shard_map/while/body/eval_jaxpr/reduce_sum | solution.py:200
  369.7 3.0 fusion.548
  374.4 4.6 fusion.550
  382.1 3.8 fusion.560
  387.7 4.7 %fusion.558 = (f32[2,4,3,128]{3,2,1,0:T(4,128)S(1)}, f32[2,4,3,128]{3,2,1,0:T(4,128)S(1)}, f32[2,4,3,128]{3,2,1,0:T(4,128)S(1)}, f32[2,4,3,128]{3,2,1,0:T(4,128)...) fusion(f32[2,4,128,128]{3,2,1,0:T(8,128)S(1)} %get-tuple-elemen, ...), kind=kLoop, calls=%fused_computation.265.clone.1.clone | loop fusion | flops 10589184 | bytes 4952064 | tf_op jit(solution)/shard_map/while/body/eval_jaxpr/reduce_sum | solution.py:200
  393.2 4.7 %fusion.554 = (f32[2,4,3,128]{3,2,1,0:T(4,128)S(1)}, f32[2,4,3,128]{3,2,1,0:T(4,128)S(1)}, f32[2,4,3,128]{3,2,1,0:T(4,128)S(1)}, f32[2,4,3,128]{3,2,1,0:T(4,128)...) fusion(f32[2,4,128,128]{3,2,1,0:T(8,128)S(1)} %get-tuple-elemen, ...), kind=kLoop, calls=%fused_computation.263.clone.1.clone | loop fusion | flops 10589184 | bytes 4952064 | tf_op jit(solution)/shard_map/while/body/eval_jaxpr/reduce_sum | solution.py:200
  404.0 3.0 fusion.548
  408.7 4.6 fusion.550
  416.4 3.8 fusion.560
  422.1 4.7 %fusion.558 = (f32[2,4,3,128]{3,2,1,0:T(4,128)S(1)}, f32[2,4,3,128]{3,2,1,0:T(4,128)S(1)}, f32[2,4,3,128]{3,2,1,0:T(4,128)S(1)}, f32[2,4,3,128]{3,2,1,0:T(4,128)...) fusion(f32[2,4,128,128]{3,2,1,0:T(8,128)S(1)} %get-tuple-elemen, ...), kind=kLoop, calls=%fused_computation.265.clone.1.clone | loop fusion | flops 10589184 | bytes 4952064 | tf_op jit(solution)/shard_map/while/body/eval_jaxpr/reduce_sum | solution.py:200
  427.5 4.7 %fusion.554 = (f32[2,4,3,128]{3,2,1,0:T(4,128)S(1)}, f32[2,4,3,128]{3,2,1,0:T(4,128)S(1)}, f32[2,4,3,128]{3,2,1,0:T(4,128)S(1)}, f32[2,4,3,128]{3,2,1,0:T(4,128)...) fusion(f32[2,4,128,128]{3,2,1,0:T(8,128)S(1)} %get-tuple-elemen, ...), kind=kLoop, calls=%fused_computation.263.clone.1.clone | loop fusion | flops 10589184 | bytes 4952064 | tf_op jit(solution)/shard_map/while/body/eval_jaxpr/reduce_sum | solution.py:200
  438.3 3.0 fusion.548
  443.1 4.6 fusion.550
  450.7 3.8 fusion.560
  456.4 4.7 %fusion.558 = (f32[2,4,3,128]{3,2,1,0:T(4,128)S(1)}, f32[2,4,3,128]{3,2,1,0:T(4,128)S(1)}, f32[2,4,3,128]{3,2,1,0:T(4,128)S(1)}, f32[2,4,3,128]{3,2,1,0:T(4,128)...) fusion(f32[2,4,128,128]{3,2,1,0:T(8,128)S(1)} %get-tuple-elemen, ...), kind=kLoop, calls=%fused_computation.265.clone.1.clone | loop fusion | flops 10589184 | bytes 4952064 | tf_op jit(solution)/shard_map/while/body/eval_jaxpr/reduce_sum | solution.py:200
  461.9 4.7 %fusion.554 = (f32[2,4,3,128]{3,2,1,0:T(4,128)S(1)}, f32[2,4,3,128]{3,2,1,0:T(4,128)S(1)}, f32[2,4,3,128]{3,2,1,0:T(4,128)S(1)}, f32[2,4,3,128]{3,2,1,0:T(4,128)...) fusion(f32[2,4,128,128]{3,2,1,0:T(8,128)S(1)} %get-tuple-elemen, ...), kind=kLoop, calls=%fused_computation.263.clone.1.clone | loop fusion | flops 10589184 | bytes 4952064 | tf_op jit(solution)/shard_map/while/body/eval_jaxpr/reduce_sum | solution.py:200
  (877 shorter events, 150.3 us)
Async XLA Ops:
  53.9 30.9 %all-to-all-start.1 = ((f32[32,1,8192]{2,1,0:T(1,128)}), f32[32,1,8192]{2,1,0:T(1,128)S(1)}, u32[]{:S(2)}, u32[]{:S(2)}) async-start(f32[32,1,8192]{2,1,0:T(1,128)} %reshape.1382), calls=%async_computation.1 | async-start | bytes 2097152 | tf_op jit(solution)/shard_map/all_to_all | solution.py:232
  122.0 8.6 %copy-start.3 = (f32[4,2,4,3,128]{4,2,3,1,0:T(4,128)S(1)}, f32[4,2,4,3,128]{4,2,3,1,0:T(4,128)}, u32[]{:S(2)}) copy-start(f32[4,2,4,3,128]{4,2,3,1,0:T(4,128)} %param.68) | copy-start | bytes 147460
  122.1 8.6 %copy-start.4 = (s32[4,2,4,3,128]{4,2,3,1,0:T(4,128)S(1)}, s32[4,2,4,3,128]{4,2,3,1,0:T(4,128)}, u32[]{:S(2)}) copy-start(s32[4,2,4,3,128]{4,2,3,1,0:T(4,128)} %param.67) | copy-start | bytes 147460
  122.1 51.9 %all-to-all-start.2 = ((f32[32,1,8192]{2,1,0:T(1,128)}), f32[32,1,8192]{2,1,0:T(1,128)S(1)}, u32[]{:S(2)}, u32[]{:S(2)}) async-start(f32[32,1,8192]{2,1,0:T(1,128)} %reshape.1384), calls=%async_computation.2 | async-start | bytes 2097152 | tf_op jit(solution)/shard_map/all_to_all | solution.py:259
  130.7 17.2 %collective-permute-start = (f32[1,2,4,5,128]{4,3,2,1,0:T(8,128)S(1)}, f32[1,2,4,5,128]{4,3,2,1,0:T(8,128)S(1)}, u32[]{:S(2)}, u32[]{:S(2)}) collective-permute-start(f32[1,2,4,5,128]{4,3,2,1,0:T(8,128)S(1)} %get-tuple-element.966), channel_id=1, source_target_pairs={{0,8},{8,16},{16,24},{24,0},{1,9},{9,17},{17,25},{25,1},{2,10},{10... | collective-permute-start | bytes 61448 | tf_op jit(solution)/shard_map/ppermute | solution.py:29
  132.1 15.8 %collective-permute-start.1 = (f32[1,2,4,5,128]{4,3,2,1,0:T(8,128)S(1)}, f32[1,2,4,5,128]{4,3,2,1,0:T(8,128)S(1)}, u32[]{:S(2)}, u32[]{:S(2)}) collective-permute-start(f32[1,2,4,5,128]{4,3,2,1,0:T(8,128)S(1)} %get-tuple-element.967), channel_id=1, source_target_pairs={{8,0},{16,8},{24,16},{0,24},{9,1},{17,9},{25,17},{1,25},{10,2},{18... | collective-permute-start | bytes 61448 | tf_op jit(solution)/shard_map/ppermute | solution.py:32
  148.0 18.5 %collective-permute-start.2 = (f32[6,1,4,5,128]{4,3,2,1,0:T(8,128)S(1)}, f32[6,1,4,5,128]{4,3,2,1,0:T(8,128)S(1)}, u32[]{:S(2)}, u32[]{:S(2)}) collective-permute-start(f32[6,1,4,5,128]{4,3,2,1,0:T(8,128)S(1)} %get-tuple-element.964), channel_id=1, source_target_pairs={{0,4},{4,0},{1,5},{5,1},{2,6},{6,2},{3,7},{7,3},{8,12},{12,8},{9,1... | collective-permute-start | bytes 184328 | tf_op jit(solution)/shard_map/ppermute | solution.py:29
  149.6 16.9 %collective-permute-start.3 = (f32[6,1,4,5,128]{4,3,2,1,0:T(8,128)S(1)}, f32[6,1,4,5,128]{4,3,2,1,0:T(8,128)S(1)}, u32[]{:S(2)}, u32[]{:S(2)}) collective-permute-start(f32[6,1,4,5,128]{4,3,2,1,0:T(8,128)S(1)} %get-tuple-element.965), channel_id=1, source_target_pairs={{4,0},{0,4},{5,1},{1,5},{6,2},{2,6},{7,3},{3,7},{12,8},{8,12},{13,... | collective-permute-start | bytes 184328 | tf_op jit(solution)/shard_map/ppermute | solution.py:32
  160.9 8.9 %copy-start.41 = (f32[2]{0:T(128)S(1)}, f32[2]{0:T(128)}, u32[]{:S(2)}) copy-start(f32[2]{0:T(128)} %param.72) | copy-start | bytes 28
  166.6 5.0 %collective-permute-start.4 = (f32[6,4,1,5,128]{4,3,2,1,0:T(8,128)S(1)}, f32[6,4,1,5,128]{4,3,2,1,0:T(8,128)S(1)}, u32[]{:S(2)}, u32[]{:S(2)}) collective-permute-start(f32[6,4,1,5,128]{4,3,2,1,0:T(8,128)S(1)} %get-tuple-element.959), channel_id=1, source_target_pairs={{0,1},{1,2},{2,3},{3,0},{4,5},{5,6},{6,7},{7,4},{8,9},{9,10},{10,1... | collective-permute-start | bytes 184328 | tf_op jit(solution)/shard_map/ppermute | solution.py:29
  169.7 4.0 collective-permute-start.5
  188.7 91.2 %all-to-all-start.3 = ((f32[4,1,32768]{2,1,0:T(1,128)}), f32[4,1,32768]{2,1,0:T(1,128)S(1)}, u32[]{:S(2)}, u32[]{:S(2)}) async-start(f32[4,1,32768]{2,1,0:T(1,128)} %reshape.1386), calls=%async_computation.3 | async-start | bytes 1048576 | tf_op jit(solution)/shard_map/all_to_all | solution.py:267
  192.7 5.7 %copy-start.15 = (f32[3]{0:T(128)S(1)}, f32[3]{0:T(128)}, u32[]{:S(2)}) copy-start(f32[3]{0:T(128)} %get-tuple-element.2319) | copy-start | bytes 40 | tf_op jit(solution)/shard_map/while
  192.7 5.8 %copy-start.19 = (f32[3]{0:T(128)S(1)}, f32[3]{0:T(128)}, u32[]{:S(2)}) copy-start(f32[3]{0:T(128)} %get-tuple-element.2321) | copy-start | bytes 40 | tf_op jit(solution)/shard_map/while
  192.7 5.8 %copy-start.21 = (f32[3]{0:T(128)S(1)}, f32[3]{0:T(128)}, u32[]{:S(2)}) copy-start(f32[3]{0:T(128)} %get-tuple-element.2320) | copy-start | bytes 40 | tf_op jit(solution)/shard_map/while
  192.7 5.9 %copy-start.23 = (f32[3]{0:T(128)S(1)}, f32[3]{0:T(128)}, u32[]{:S(2)}) copy-start(f32[3]{0:T(128)} %get-tuple-element.2323) | copy-start | bytes 40 | tf_op jit(solution)/shard_map/while
  192.7 5.9 %copy-start.25 = (f32[3]{0:T(128)S(1)}, f32[3]{0:T(128)}, u32[]{:S(2)}) copy-start(f32[3]{0:T(128)} %get-tuple-element.2322) | copy-start | bytes 40 | tf_op jit(solution)/shard_map/while
  192.7 5.9 %copy-start.27 = (f32[3]{0:T(128)S(1)}, f32[3]{0:T(128)}, u32[]{:S(2)}) copy-start(f32[3]{0:T(128)} %get-tuple-element.2325) | copy-start | bytes 40 | tf_op jit(solution)/shard_map/while
  192.8 5.9 %copy-start.29 = (f32[3]{0:T(128)S(1)}, f32[3]{0:T(128)}, u32[]{:S(2)}) copy-start(f32[3]{0:T(128)} %get-tuple-element.2324) | copy-start | bytes 40 | tf_op jit(solution)/shard_map/while
  214.4 5.7 %copy-start.15 = (f32[3]{0:T(128)S(1)}, f32[3]{0:T(128)}, u32[]{:S(2)}) copy-start(f32[3]{0:T(128)} %get-tuple-element.2319) | copy-start | bytes 40 | tf_op jit(solution)/shard_map/while
  214.5 5.8 %copy-start.19 = (f32[3]{0:T(128)S(1)}, f32[3]{0:T(128)}, u32[]{:S(2)}) copy-start(f32[3]{0:T(128)} %get-tuple-element.2321) | copy-start | bytes 40 | tf_op jit(solution)/shard_map/while
  214.5 5.8 %copy-start.21 = (f32[3]{0:T(128)S(1)}, f32[3]{0:T(128)}, u32[]{:S(2)}) copy-start(f32[3]{0:T(128)} %get-tuple-element.2320) | copy-start | bytes 40 | tf_op jit(solution)/shard_map/while
  214.5 5.9 %copy-start.23 = (f32[3]{0:T(128)S(1)}, f32[3]{0:T(128)}, u32[]{:S(2)}) copy-start(f32[3]{0:T(128)} %get-tuple-element.2323) | copy-start | bytes 40 | tf_op jit(solution)/shard_map/while
  214.5 5.9 %copy-start.25 = (f32[3]{0:T(128)S(1)}, f32[3]{0:T(128)}, u32[]{:S(2)}) copy-start(f32[3]{0:T(128)} %get-tuple-element.2322) | copy-start | bytes 40 | tf_op jit(solution)/shard_map/while
  214.5 5.9 %copy-start.27 = (f32[3]{0:T(128)S(1)}, f32[3]{0:T(128)}, u32[]{:S(2)}) copy-start(f32[3]{0:T(128)} %get-tuple-element.2325) | copy-start | bytes 40 | tf_op jit(solution)/shard_map/while
  214.5 5.9 %copy-start.29 = (f32[3]{0:T(128)S(1)}, f32[3]{0:T(128)}, u32[]{:S(2)}) copy-start(f32[3]{0:T(128)} %get-tuple-element.2324) | copy-start | bytes 40 | tf_op jit(solution)/shard_map/while
  236.2 5.7 %copy-start.15 = (f32[3]{0:T(128)S(1)}, f32[3]{0:T(128)}, u32[]{:S(2)}) copy-start(f32[3]{0:T(128)} %get-tuple-element.2319) | copy-start | bytes 40 | tf_op jit(solution)/shard_map/while
  236.2 5.7 %copy-start.17 = (f32[3]{0:T(128)S(1)}, f32[3]{0:T(128)}, u32[]{:S(2)}) copy-start(f32[3]{0:T(128)} %get-tuple-element.2318) | copy-start | bytes 40 | tf_op jit(solution)/shard_map/while
  236.2 5.8 %copy-start.19 = (f32[3]{0:T(128)S(1)}, f32[3]{0:T(128)}, u32[]{:S(2)}) copy-start(f32[3]{0:T(128)} %get-tuple-element.2321) | copy-start | bytes 40 | tf_op jit(solution)/shard_map/while
  236.3 5.8 %copy-start.21 = (f32[3]{0:T(128)S(1)}, f32[3]{0:T(128)}, u32[]{:S(2)}) copy-start(f32[3]{0:T(128)} %get-tuple-element.2320) | copy-start | bytes 40 | tf_op jit(solution)/shard_map/while
  236.3 5.9 %copy-start.23 = (f32[3]{0:T(128)S(1)}, f32[3]{0:T(128)}, u32[]{:S(2)}) copy-start(f32[3]{0:T(128)} %get-tuple-element.2323) | copy-start | bytes 40 | tf_op jit(solution)/shard_map/while
  236.3 5.9 %copy-start.25 = (f32[3]{0:T(128)S(1)}, f32[3]{0:T(128)}, u32[]{:S(2)}) copy-start(f32[3]{0:T(128)} %get-tuple-element.2322) | copy-start | bytes 40 | tf_op jit(solution)/shard_map/while
  236.3 5.9 %copy-start.27 = (f32[3]{0:T(128)S(1)}, f32[3]{0:T(128)}, u32[]{:S(2)}) copy-start(f32[3]{0:T(128)} %get-tuple-element.2325) | copy-start | bytes 40 | tf_op jit(solution)/shard_map/while
  236.3 5.9 %copy-start.29 = (f32[3]{0:T(128)S(1)}, f32[3]{0:T(128)}, u32[]{:S(2)}) copy-start(f32[3]{0:T(128)} %get-tuple-element.2324) | copy-start | bytes 40 | tf_op jit(solution)/shard_map/while
  258.0 5.7 %copy-start.15 = (f32[3]{0:T(128)S(1)}, f32[3]{0:T(128)}, u32[]{:S(2)}) copy-start(f32[3]{0:T(128)} %get-tuple-element.2319) | copy-start | bytes 40 | tf_op jit(solution)/shard_map/while
  258.0 5.8 %copy-start.19 = (f32[3]{0:T(128)S(1)}, f32[3]{0:T(128)}, u32[]{:S(2)}) copy-start(f32[3]{0:T(128)} %get-tuple-element.2321) | copy-start | bytes 40 | tf_op jit(solution)/shard_map/while
  258.0 5.8 %copy-start.21 = (f32[3]{0:T(128)S(1)}, f32[3]{0:T(128)}, u32[]{:S(2)}) copy-start(f32[3]{0:T(128)} %get-tuple-element.2320) | copy-start | bytes 40 | tf_op jit(solution)/shard_map/while
  258.0 5.9 %copy-start.23 = (f32[3]{0:T(128)S(1)}, f32[3]{0:T(128)}, u32[]{:S(2)}) copy-start(f32[3]{0:T(128)} %get-tuple-element.2323) | copy-start | bytes 40 | tf_op jit(solution)/shard_map/while
  258.1 5.9 %copy-start.25 = (f32[3]{0:T(128)S(1)}, f32[3]{0:T(128)}, u32[]{:S(2)}) copy-start(f32[3]{0:T(128)} %get-tuple-element.2322) | copy-start | bytes 40 | tf_op jit(solution)/shard_map/while
  258.1 5.9 %copy-start.27 = (f32[3]{0:T(128)S(1)}, f32[3]{0:T(128)}, u32[]{:S(2)}) copy-start(f32[3]{0:T(128)} %get-tuple-element.2325) | copy-start | bytes 40 | tf_op jit(solution)/shard_map/while
  258.1 5.9 %copy-start.29 = (f32[3]{0:T(128)S(1)}, f32[3]{0:T(128)}, u32[]{:S(2)}) copy-start(f32[3]{0:T(128)} %get-tuple-element.2324) | copy-start | bytes 40 | tf_op jit(solution)/shard_map/while
  294.9 5.8 %copy-start.1 = (f32[32,128,256]{2,1,0:T(8,128)S(1)}, f32[32,128,256]{2,1,0:T(8,128)}, u32[]{:S(2)}) copy-start(f32[32,128,256]{2,1,0:T(8,128)} %copy.230) | copy-start | bytes 12582916
  300.7 28.2 %copy-start.7 = (f32[3]{0:T(128)S(1)}, f32[3]{0:T(128)}, u32[]{:S(2)}) copy-start(f32[3]{0:T(128)} %get-tuple-element.2445) | copy-start | bytes 40
  300.7 28.2 %copy-start.8 = (f32[3]{0:T(128)S(1)}, f32[3]{0:T(128)}, u32[]{:S(2)}) copy-start(f32[3]{0:T(128)} %get-tuple-element.2446) | copy-start | bytes 40
  300.7 28.2 %copy-start.9 = (f32[3]{0:T(128)S(1)}, f32[3]{0:T(128)}, u32[]{:S(2)}) copy-start(f32[3]{0:T(128)} %get-tuple-element.2447) | copy-start | bytes 40
  300.7 28.2 %copy-start.10 = (f32[3]{0:T(128)S(1)}, f32[3]{0:T(128)}, u32[]{:S(2)}) copy-start(f32[3]{0:T(128)} %get-tuple-element.2448) | copy-start | bytes 40
  300.8 28.2 %copy-start.11 = (f32[3]{0:T(128)S(1)}, f32[3]{0:T(128)}, u32[]{:S(2)}) copy-start(f32[3]{0:T(128)} %get-tuple-element.2449) | copy-start | bytes 40
  300.8 28.2 %copy-start.12 = (f32[3]{0:T(128)S(1)}, f32[3]{0:T(128)}, u32[]{:S(2)}) copy-start(f32[3]{0:T(128)} %get-tuple-element.2450) | copy-start | bytes 40
  300.8 28.2 %copy-start.13 = (f32[3]{0:T(128)S(1)}, f32[3]{0:T(128)}, u32[]{:S(2)}) copy-start(f32[3]{0:T(128)} %get-tuple-element.2451) | copy-start | bytes 40
  300.8 28.2 %copy-start.14 = (f32[3]{0:T(128)S(1)}, f32[3]{0:T(128)}, u32[]{:S(2)}) copy-start(f32[3]{0:T(128)} %get-tuple-element.2452) | copy-start | bytes 40
  300.8 28.2 %copy-start.16 = (f32[3]{0:T(128)S(1)}, f32[3]{0:T(128)}, u32[]{:S(2)}) copy-start(f32[3]{0:T(128)} %get-tuple-element.2453) | copy-start | bytes 40
  300.8 28.2 %copy-start.18 = (f32[3]{0:T(128)S(1)}, f32[3]{0:T(128)}, u32[]{:S(2)}) copy-start(f32[3]{0:T(128)} %get-tuple-element.2454) | copy-start | bytes 40
  300.8 28.2 %copy-start.20 = (f32[3]{0:T(128)S(1)}, f32[3]{0:T(128)}, u32[]{:S(2)}) copy-start(f32[3]{0:T(128)} %get-tuple-element.2455) | copy-start | bytes 40
  300.8 28.2 %copy-start.22 = (f32[3]{0:T(128)S(1)}, f32[3]{0:T(128)}, u32[]{:S(2)}) copy-start(f32[3]{0:T(128)} %get-tuple-element.2456) | copy-start | bytes 40
  300.9 28.2 %copy-start.24 = (f32[3]{0:T(128)S(1)}, f32[3]{0:T(128)}, u32[]{:S(2)}) copy-start(f32[3]{0:T(128)} %get-tuple-element.2457) | copy-start | bytes 40
  300.9 28.2 %copy-start.26 = (f32[3]{0:T(128)S(1)}, f32[3]{0:T(128)}, u32[]{:S(2)}) copy-start(f32[3]{0:T(128)} %get-tuple-element.2458) | copy-start | bytes 40
  300.9 28.2 %copy-start.28 = (f32[3]{0:T(128)S(1)}, f32[3]{0:T(128)}, u32[]{:S(2)}) copy-start(f32[3]{0:T(128)} %get-tuple-element.2459) | copy-start | bytes 40
  300.9 28.2 %copy-start.30 = (f32[3]{0:T(128)S(1)}, f32[3]{0:T(128)}, u32[]{:S(2)}) copy-start(f32[3]{0:T(128)} %get-tuple-element.2460) | copy-start | bytes 40
  310.7 6.0 %collective-permute-start.6 = (f32[1,2,4,128]{3,2,1,0:T(4,128)S(1)}, f32[1,2,4,128]{3,2,1,0:T(4,128)S(1)}, u32[]{:S(2)}, u32[]{:S(2)}) collective-permute-start(f32[1,2,4,128]{3,2,1,0:T(4,128)S(1)} %get-tuple-element.982), channel_id=1, source_target_pairs={{0,8},{8,16},{16,24},{24,0},{1,9},{9,17},{17,25},{25,1},{2,10},{10... | collective-permute-start | bytes 12296 | tf_op jit(solution)/shard_map/ppermute | solution.py:29
  316.0 2.5 collective-permute-start.7
  318.4 2.6 collective-permute-start.8
  319.7 2.5 collective-permute-start.9
  322.3 4.3 collective-permute-start.10
  325.8 3.1 collective-permute-start.11
  (17 other events, 82.3 us)
where the time goes:
time: 477 us; the launch traced here: 468 us
  other arithmetic  213 us (45%)
  local copies, waits for them, and re-layouts  85.4 us (18%)
  waiting for transfers between devices  50 us (10%)
  matrix products  43 us (9%)
  starting transfers between devices  32.7 us (7%)
  loops' own time  29.1 us (6%)
  blocking collectives  12 us (3%)
    reduce_sum x16, other arithmetic, force_row(): jnp.sum(coefficient[..., None, :, :] * separation, axis=-1)  71.3 us
    reduce_sum x16, other arithmetic, pair_terms(): squared = jnp.sum(separation * separation, axis=-3)  44.5 us
    sub x32, other arithmetic, force_row(): -2.0 * own_rep[..., :, None] * other_rep * weight  27.6 us
    all_to_all x1, waiting for transfers between devices, on_device(): lax.all_to_all(stacked, ('gx', 'gy', 'gz'), split_axis=4, concat_axis=1,...  24.9 us
    reduce_sum x108, other arithmetic, density_row(): jnp.sum(weight * weight * weight * near[:, :, 3, :][..., None, :], axis=-1)  23.8 us
    add x104, other arithmetic, pair_terms(): shift_vector[:, None, None] + other_positions[..., :, None, :]  18.6 us
    ppermute x6, waiting for transfers between devices, padded(): lax.ppermute(lax.slice_in_dim(block, block.shape[dim] - width, None, axis...  17.6 us
    ppermute x6, starting transfers between devices, padded(): lax.ppermute(lax.slice_in_dim(block, block.shape[dim] - width, None, axis...  16.2 us
  transfers between devices with their start and end apart: 15, of which 10 were waited for; matrix products, arithmetic and copies ran while one was open for 20% of the time, Pallas kernels for 0%

commit v1 on v0

v1 whole, which is shorter than its diff:
```python
import math

import ml_dtypes
import numpy as np

import jax
import jax.numpy as jnp
from jax import lax
from jax.experimental import pallas as pl
from jax.experimental.pallas import tpu as pltpu
from jax.sharding import PartitionSpec as P

NSPEC = 2
PPC = 16
EWALD_SPLIT = 0.7
COUPLING = 8.0
F32 = jnp.float32
BF16 = jnp.bfloat16
VMEM = pl.BlockSpec(memory_space=pltpu.VMEM)
SMEM = pl.BlockSpec(memory_space=pltpu.SMEM)
NN = (((1,), (0,)), ((), ()))
NT = (((1,), (1,)), ((), ()))
PARAMS = pltpu.CompilerParams(vmem_limit_bytes=56 * 1024 * 1024)


def split2(values):
    high = values.astype(BF16)
    return high, (values - high.astype(F32)).astype(BF16)


def split3(values):
    high = values.astype(BF16).astype(F32)
    rest = values - high
    middle = rest.astype(BF16).astype(F32)
    return high, middle, (rest - middle).astype(BF16).astype(F32)


def dot(left, right, dims):
    return lax.dot_general(left, right, dims, preferred_element_type=F32)


def dot3(left, right, dims):
    return (
        dot(left[0], right[0], dims) + dot(left[0], right[1], dims) + dot(left[1], right[0], dims)
    )


def by_kind(kind, table, column):
    result = jnp.zeros(kind.shape, F32)
    for kind_index in range(NSPEC):
        result = jnp.where(kind == float(kind_index), table[column, kind_index], result)
    return result


def real_basis(length):
    rows = np.arange(length)[:, None]
    points = np.arange(length)[None, :]
    half = length // 2
    waves = np.where(rows <= half, rows, length - rows)
    angle = 2.0 * np.pi * ((waves * points) % length) / length
    basis = np.where(rows <= half, np.cos(angle), np.sin(angle)) * math.sqrt(2.0 / length)
    basis[0] *= math.sqrt(0.5)
    basis[half] *= math.sqrt(0.5)
    return basis


def table_pair(values):
    values = values.astype(np.float32)
    high = values.astype(ml_dtypes.bfloat16)
    low = (values - high.astype(np.float32)).astype(ml_dtypes.bfloat16)
    return jnp.asarray(high), jnp.asarray(low)


def signed_modes(indices, total):
    return jnp.where(2 * indices >= total, indices - total, indices)


def green_factor(modes_x, modes_y, modes_z, length_x, length_y, length_z):
    wave_x = modes_x.astype(F32) * (2.0 * math.pi / length_x)
    wave_y = modes_y.astype(F32) * (2.0 * math.pi / length_y)
    wave_z = modes_z.astype(F32) * (2.0 * math.pi / length_z)
    squared = wave_x * wave_x + wave_y * wave_y + wave_z * wave_z
    anchor = (modes_x == 0) & (modes_y == 0) & (modes_z == 0)
    safe_square = jnp.where(anchor, 1.0, squared)
    return jnp.where(
        anchor,
        0.0,
        4.0 * math.pi * jnp.exp(-squared / (4.0 * EWALD_SPLIT * EWALD_SPLIT)) / safe_square,
    )


def chunk_transpose(tiles, chunk):
    tiles = list(tiles)
    count = len(tiles)
    width = tiles[0].shape[-1]
    lane_chunk = lax.broadcasted_iota(jnp.int32, tiles[0].shape, 1) // chunk
    bit = 1
    while bit < count:
        keep = (lane_chunk & bit) == 0
        for low in range(count):
            if low & bit:
                continue
            first, second = tiles[low], tiles[low | bit]
            tiles[low] = jnp.where(keep, first, pltpu.roll(second, bit * chunk, 1))
            tiles[low | bit] = jnp.where(keep, pltpu.roll(first, width - bit * chunk, 1), second)
        bit *= 2
    return tiles


def point_weights(offset_row, fraction_row):
    points = lax.broadcasted_iota(jnp.int32, (PPC, offset_row.shape[-1]), 0).astype(F32)
    lower = points == offset_row
    upper = points == offset_row + 1.0
    weights = jnp.where(lower, 1.0 - fraction_row, jnp.where(upper, fraction_row, 0.0))
    slopes = jnp.where(lower, -1.0, jnp.where(upper, 1.0, 0.0))
    return weights, slopes


def make_spread(parts, cells_y, cells_z, slots, lz, devices, relayout):
    columns = parts * cells_z
    modes = lz // devices
    yl = cells_y * PPC
    rows = PPC * PPC

    def kernel(atoms, table, basis_hi, basis_lo, out, plane_hi, plane_lo, line_hi, line_lo):
        line_hi[...] = jnp.zeros(line_hi.shape, BF16)
        line_lo[...] = jnp.zeros(line_lo.shape, BF16)
        basis = (basis_hi[...], basis_lo[...])
        pieces = []
        for cy in range(cells_y):
            for column in range(columns):
                cell = atoms[column // cells_z, cy, column % cells_z]
                weights = [point_weights(cell[d : d + 1], cell[3 + d : 4 + d])[0] for d in range(3)]
                along_x = weights[0] * by_kind(cell[6:7], table, 3)
                plane = jnp.concatenate(
                    [weights[1][y : y + 1] * along_x for y in range(PPC)], axis=0
                )
                lanes = pl.ds(column * slots, slots)
                points = pl.ds(column * PPC, PPC)
                plane_hi[:, lanes], plane_lo[:, lanes] = split2(plane)
                line_hi[points, lanes], line_lo[points, lanes] = split2(weights[2])
            brick = dot3(
                (plane_hi[...], plane_lo[...]), (line_hi[...], line_lo[...]), NT
            )
            pieces.append(dot3(split2(brick), basis, NT))
        if not relayout:
            for cy in range(cells_y):
                out[pl.ds(cy * rows, rows), :] = pieces[cy]
            return
        chunks = 128 // modes
        for tile in range(lz // 128):
            for group in range(yl // chunks):
                tiles = []
                for y in range(group * chunks, (group + 1) * chunks):
                    start = (y % PPC) * PPC
                    tiles.append(
                        pieces[y // PPC][start : start + PPC, tile * 128 : tile * 128 + 128]
                    )
                for chunk, value in enumerate(chunk_transpose(tiles, modes)):
                    out[tile * chunks + chunk, :, pl.ds(group * 128, 128)] = value

    if relayout:
        shape = (devices, PPC, yl * modes)
    else:
        shape = (cells_y * rows, lz)
    return pl.pallas_call(
        kernel,
        out_shape=jax.ShapeDtypeStruct(shape, F32),
        in_specs=[VMEM, SMEM, VMEM, VMEM],
        out_specs=VMEM,
        scratch_shapes=[
            pltpu.VMEM((rows, columns * slots), BF16),
            pltpu.VMEM((rows, columns * slots), BF16),
            pltpu.VMEM((lz, columns * slots), BF16),
            pltpu.VMEM((lz, columns * slots), BF16),
        ],
        compiler_params=PARAMS,
        name="spread",
    )


def make_planes(gx, gy, gz, lanes, lx, width):
    def kernel(data, x_hi, x_lo, xt_hi, xt_lo, y_hi, y_lo, green, out, grid):
        for a in range(gx):
            for b in range(gy):
                for c in range(gz):
                    grid[pl.ds((a * gz + c) * PPC, PPC), pl.ds(b * lanes, lanes)] = data[
                        (a * gy + b) * gz + c
                    ]
        along_y = (y_hi[...], y_lo[...])
        value = dot3((x_hi[...], x_lo[...]), split2(grid[...]), NN)
        value = dot3(split2(value), along_y, NT) * green[...]
        value = dot3(split2(value), along_y, NN)
        value = dot3((xt_hi[...], xt_lo[...]), split2(value), NN)
        for a in range(gx):
            for b in range(gy):
                for c in range(gz):
                    start = (a * gz + c) * PPC
                    out[(a * gy + b) * gz + c] = value[
                        start : start + PPC, b * lanes : (b + 1) * lanes
                    ]

    return pl.pallas_call(
        kernel,
        out_shape=jax.ShapeDtypeStruct((gx * gy * gz, PPC, lanes), F32),
        in_specs=[VMEM] * 8,
        out_specs=VMEM,
        scratch_shapes=[pltpu.VMEM((lx, width), F32)],
        compiler_params=PARAMS,
        name="planes",
    )


def make_sample(parts, cells_y, cells_z, slots, lz, devices, relayout):
    columns = parts * cells_z
    modes = lz // devices
    yl = cells_y * PPC
    rows = PPC * PPC

    def kernel(data, atoms, table, basis_hi, basis_lo, out, lines, line_hi, line_lo):
        if relayout:
            chunks = 128 // modes
            for tile in range(lz // 128):
                for group in range(yl // chunks):
                    tiles = [
                        data[tile * chunks + chunk, :, pl.ds(group * 128, 128)]
                        for chunk in range(chunks)
                    ]
                    for index, value in enumerate(chunk_transpose(tiles, modes)):
                        lines[
                            pl.ds((group * chunks + index) * PPC, PPC), pl.ds(tile * 128, 128)
                        ] = value
        else:
            lines[...] = data[...]
        line_hi[...] = jnp.zeros(line_hi.shape, BF16)
        line_lo[...] = jnp.zeros(line_lo.shape, BF16)
        basis = (basis_hi[...], basis_lo[...])
        for cy in range(cells_y):
            brick = split2(dot3(split2(lines[pl.ds(cy * rows, rows), :]), basis, NN))
            for column in range(columns):
                cell = atoms[column // cells_z, cy, column % cells_z]
                pairs = [point_weights(cell[d : d + 1], cell[3 + d : 4 + d]) for d in range(3)]
                (wx, sx), (wy, sy), (wz, sz) = pairs
                points = pl.ds(column * PPC, PPC)
                high, low = split2(wz)
                line_hi[column, points, pl.ds(0, slots)] = high
                line_hi[column, points, pl.ds(slots, slots)] = sz.astype(BF16)
                line_lo[column, points, :] = low
                both = dot(brick[0], line_hi[column], NN) + dot(brick[1], line_hi[column], NN)
                plain = both[:, :slots] + dot(brick[0], line_lo[column], NN)
                tilted = both[:, slots:]
                force_x = jnp.zeros((PPC, slots), F32)
                force_y = jnp.zeros((PPC, slots), F32)
                force_z = jnp.zeros((PPC, slots), F32)
                for y in range(PPC):
                    block = plain[y * PPC : (y + 1) * PPC]
                    force_x += wy[y : y + 1] * block
                    force_y += sy[y : y + 1] * block
                    force_z += wy[y : y + 1] * tilted[y * PPC : (y + 1) * PPC]
                charge = -by_kind(cell[6:7], table, 3)
                result = [
                    charge * jnp.sum(force * weight, axis=0, keepdims=True)
                    for force, weight in ((force_x, sx), (force_y, wx), (force_z, wx))
                ]
                out[column // cells_z, cy, column % cells_z] = jnp.concatenate(result, axis=0)

    return pl.pallas_call(
        kernel,
        out_shape=jax.ShapeDtypeStruct((parts, cells_y, cells_z, 3, slots), F32),
        in_specs=[VMEM, VMEM, SMEM, VMEM, VMEM],
        out_specs=VMEM,
        scratch_shapes=[
            pltpu.VMEM((cells_y * rows, lz), F32),
            pltpu.VMEM((columns, lz, 2 * slots), BF16),
            pltpu.VMEM((columns, lz, slots), BF16),
        ],
        compiler_params=PARAMS,
        name="sample",
    )


ORDER = ((0, 0), (1, 0), (0, 1), (1, 1), (2, 0), (0, 2))


def spread_pieces(values, side):
    pieces = split3(values)
    stacked = [pieces[entry[side]] for entry in ORDER]
    stacked += [jnp.zeros_like(values)] * 2
    return jnp.concatenate(stacked, axis=0)


def cell_positions(ext, x, y, sizes):
    count_x, count_y, count_z = sizes
    along_z = lax.broadcasted_iota(jnp.int32, (count_z, ext.shape[-1]), 0).astype(F32)
    pos_x = ext[x, y, :, 0, :] + (x - 0.5 * count_x)
    pos_y = ext[x, y, :, 1, :] + (y - 0.5 * count_y)
    pos_z = ext[x, y, :, 2, :] + (along_z - 0.5 * count_z)
    return (pos_x, pos_y, pos_z)


def cell_at(index, cells):
    cells_x, cells_y, cells_z = cells
    x = index // (cells_y * cells_z)
    y = (index // cells_z) % cells_y
    z = index % cells_z
    return x, y, z


def make_density(cells, slots):
    cells_x, cells_y, cells_z = cells
    sizes = (cells_x + 2, cells_y + 2, cells_z + 2)
    own = cells_x * cells_y * cells_z
    total = sizes[0] * sizes[1] * sizes[2]

    def kernel(ext, table, density, slope, feature, own_feature, right, left, sums):
        feature[...] = jnp.zeros(feature.shape, F32)
        own_feature[...] = jnp.zeros(own_feature.shape, F32)
        for x in range(sizes[0]):
            for y in range(sizes[1]):
                pos = cell_positions(ext, x, y, sizes)
                square = pos[0] * pos[0] + pos[1] * pos[1] + pos[2] * pos[2]
                scale = by_kind(ext[x, y, :, 3, :], table, 4)
                base = (x * sizes[1] + y) * sizes[2]
                here = pl.ds(base, sizes[2])
                feature[here, 0, :] = scale * (1.0 - square)
                for d in range(3):
                    feature[here, 1 + d, :] = 2.0 * scale * pos[d]
                feature[here, 4, :] = -scale
                if 1 <= x <= cells_x and 1 <= y <= cells_y:
                    there = pl.ds(((x - 1) * cells_y + y - 1) * cells_z, cells_z)
                    own_feature[there, 0, :] = jnp.ones((cells_z, slots), F32)
                    for d in range(3):
                        own_feature[there, 1 + d, :] = pos[d][1 : 1 + cells_z]
                    own_feature[there, 4, :] = square[1 : 1 + cells_z]

        def fill_right(n, carry):
            right[n] = spread_pieces(feature[n], 0).astype(BF16)
            return carry

        def fill_left(n, carry):
            left[n] = spread_pieces(own_feature[n], 1).T.astype(BF16)
            return carry

        lax.fori_loop(0, total, fill_right, 0, unroll=8)
        lax.fori_loop(0, own, fill_left, 0, unroll=4)
        same = lax.broadcasted_iota(jnp.int32, (slots, slots), 0) == lax.broadcasted_iota(
            jnp.int32, (slots, slots), 1
        )
        lane = lax.broadcasted_iota(jnp.int32, (slots, 128), 1)
        sums[...] = jnp.zeros(sums.shape, F32)
        near = [
            (dx * sizes[1] + dy) * sizes[2] + dz
            for dx in range(3)
            for dy in range(3)
            for dz in range(3)
        ]
        centre = near.pop(13)

        def one_cell(n, carry):
            x, y, z = cell_at(n, cells)
            base = (x * sizes[1] + y) * sizes[2] + z
            lhs = left[n]
            weight = jnp.maximum(dot(lhs, right[base + centre], NN), 0.0)
            weight = jnp.where(same, 0.0, weight)
            total_sum = weight * weight * weight
            for first, second in zip(near[0::2], near[1::2]):
                rhs = jnp.concatenate([right[base + first], right[base + second]], axis=1)
                weight = jnp.maximum(dot(lhs, rhs, NN), 0.0)
                cube = weight * weight * weight
                total_sum = total_sum + cube[:, :slots] + cube[:, slots:]
            column = jnp.sum(total_sum, axis=1, keepdims=True)
            sums[...] = jnp.where(lane == n, column, sums[...])
            return carry

        lax.fori_loop(0, own, one_cell, 0)
        rows = sums[...].T
        for x in range(cells_x):
            for y in range(cells_y):
                start = (x * cells_y + y) * cells_z
                kind = ext[x + 1, y + 1, :, 3, :][1 : 1 + cells_z]
                value = jnp.where(kind >= 0.0, rows[start : start + cells_z], 0.0)
                density[x, y] = value
                slope[x, y] = -by_kind(kind, table, 2) / (2.0 * jnp.sqrt(1.0 + value))

    shape = jax.ShapeDtypeStruct((cells_x, cells_y, cells_z, slots), F32)
    return pl.pallas_call(
        kernel,
        out_shape=(shape, shape),
        in_specs=[VMEM, SMEM],
        out_specs=(VMEM, VMEM),
        scratch_shapes=[
            pltpu.VMEM((total, 8, slots), F32),
            pltpu.VMEM((own, 8, slots), F32),
            pltpu.VMEM((total, 64, slots), BF16),
            pltpu.VMEM((own, slots, 64), BF16),
            pltpu.VMEM((slots, 128), F32),
        ],
        compiler_params=PARAMS,
        cost_estimate=pl.CostEstimate(
            flops=own * 27 * slots * slots * 40, bytes_accessed=total * slots * 16, transcendentals=0
        ),
        name="density",
    )


def make_force(cells, slots):
    cells_x, cells_y, cells_z = cells
    sizes = (cells_x + 2, cells_y + 2, cells_z + 2)
    own = cells_x * cells_y * cells_z
    total = sizes[0] * sizes[1] * sizes[2]
    chunk = 32

    def kernel(ext, slopes, table, out, feature, own_feature, place, right, left, both, sums):
        feature[...] = jnp.zeros(feature.shape, F32)
        own_feature[...] = jnp.zeros(own_feature.shape, F32)
        for x in range(sizes[0]):
            for y in range(sizes[1]):
                pos = cell_positions(ext, x, y, sizes)
                square = pos[0] * pos[0] + pos[1] * pos[1] + pos[2] * pos[2]
                kind = ext[x, y, :, 3, :]
                scale = by_kind(kind, table, 1)
                steep = slopes[x, y] * by_kind(kind, table, 5)
                mild = by_kind(kind, table, 6)
                here = pl.ds((x * sizes[1] + y) * sizes[2], sizes[2])
                feature[here, 0, :] = scale * (1.0 - square)
                for d in range(3):
                    feature[here, 1 + d, :] = 2.0 * scale * pos[d]
                    place[here, d, :] = pos[d]
                feature[here, 4, :] = -scale
                feature[here, 8, :] = steep
                feature[here, 9, :] = mild
                if 1 <= x <= cells_x and 1 <= y <= cells_y:
                    inner = slice(1, 1 + cells_z)
                    there = pl.ds(((x - 1) * cells_y + y - 1) * cells_z, cells_z)
                    own_feature[there, 0, :] = scale[inner]
                    for d in range(3):
                        own_feature[there, 1 + d, :] = (scale * pos[d])[inner]
                    own_feature[there, 4, :] = (scale * square)[inner]
                    own_feature[there, 8, :] = mild[inner]
                    own_feature[there, 9, :] = steep[inner]

        def fill_right(n, carry):
            values = feature[n]
            right[n, pl.ds(0, 64), :] = spread_pieces(values[0:8], 0).astype(BF16)
            right[n, pl.ds(64, 64), :] = spread_pieces(values[8:16], 0).astype(BF16)
            return carry

        def fill_left(n, carry):
            values = own_feature[n]
            left[n, :, pl.ds(0, 64)] = spread_pieces(values[0:8], 1).T.astype(BF16)
            left[n, :, pl.ds(64, 64)] = spread_pieces(values[8:16], 1).T.astype(BF16)
            return carry

        lax.fori_loop(0, total, fill_right, 0, unroll=8)
        lax.fori_loop(0, own, fill_left, 0, unroll=4)
        same = lax.broadcasted_iota(jnp.int32, (slots, slots), 0) == lax.broadcasted_iota(
            jnp.int32, (slots, slots), 1
        )
        lane = lax.broadcasted_iota(jnp.int32, (slots, 128), 1)
        sums[...] = jnp.zeros(sums.shape, F32)
        near = [
            (dx * sizes[1] + dy) * sizes[2] + dz
            for dx in range(3)
            for dy in range(3)
            for dz in range(3)
        ]
        centre = near.pop(13)
        near = [centre] + near

        def products(n, slot):
            x, y, z = cell_at(n, cells)
            base = (x * sizes[1] + y) * sizes[2] + z
            lhs = (left[n, :, pl.ds(0, 64)], left[n, :, pl.ds(64, 64)])
            for part in range(2):
                rows = pl.ds(part * 64, 64)
                value = dot(lhs[part], right[base + centre, rows, :], NN)
                if part == 0:
                    value = jnp.where(same, 0.0, value)
                both[slot, part, 0] = value
                for index in range(1, 27, 2):
                    rhs = jnp.concatenate(
                        [right[base + near[index], rows, :], right[base + near[index + 1], rows, :]],
                        axis=1,
                    )
                    value = dot(lhs[part], rhs, NN)
                    both[slot, part, index] = value[:, :slots]
                    both[slot, part, index + 1] = value[:, slots:]

        products(0, 0)

        def one_cell(n, carry):
            slot = n % 2
            x, y, z = cell_at(n, cells)
            base = (x * sizes[1] + y) * sizes[2] + z
            products(jnp.minimum(n + 1, own - 1), 1 - slot)
            for start in range(0, slots, chunk):
                rows = pl.ds(start, chunk)
                acc = [jnp.zeros((chunk, slots), F32) for _ in range(4)]
                for index in range(27):
                    weight = jnp.maximum(both[slot, 0, index, rows, :], 0.0)
                    value = (weight * both[slot, 1, index, rows, :] - 2.0) * weight
                    acc[3] = acc[3] + value
                    for d in range(3):
                        acc[d] = acc[d] + value * place[base + near[index], pl.ds(d, 1), :]
                for d in range(4):
                    column = jnp.sum(acc[d], axis=1, keepdims=True)
                    sums[d, rows, :] = jnp.where(
                        lane[start : start + chunk] == n, column, sums[d, rows, :]
                    )
            return carry

        lax.fori_loop(0, own, one_cell, 0)
        rows = [sums[d].T for d in range(4)]
        for x in range(cells_x):
            for y in range(cells_y):
                start = (x * cells_y + y) * cells_z
                stop = start + cells_z
                pos = cell_positions(ext, x + 1, y + 1, sizes)
                for d in range(3):
                    out[x, y, :, d, :] = 2.0 * (
                        rows[d][start:stop] - pos[d][1 : 1 + cells_z] * rows[3][start:stop]
                    )

    return pl.pallas_call(
        kernel,
        out_shape=jax.ShapeDtypeStruct((cells_x, cells_y, cells_z, 3, slots), F32),
        in_specs=[VMEM, VMEM, SMEM],
        out_specs=VMEM,
        scratch_shapes=[
            pltpu.VMEM((total, 16, slots), F32),
            pltpu.VMEM((own, 16, slots), F32),
            pltpu.VMEM((total, 8, slots), F32),
            pltpu.VMEM((total, 128, slots), BF16),
            pltpu.VMEM((own, slots, 128), BF16),
            pltpu.VMEM((2, 2, 27, slots, slots), F32),
            pltpu.VMEM((4, slots, 128), F32),
        ],
        compiler_params=PARAMS,
        cost_estimate=pl.CostEstimate(
            flops=own * 27 * slots * slots * 100,
            bytes_accessed=total * slots * 16,
            transcendentals=0,
        ),
        name="force",
    )


def padded(block, sides, width):
    for axis, dim in sides:
        count = lax.axis_size(axis)
        forward = [(i, (i + 1) % count) for i in range(count)]
        backward = [(target, source) for source, target in forward]
        low = lax.ppermute(
            lax.slice_in_dim(block, block.shape[dim] - width, None, axis=dim), axis, forward
        )
        high = lax.ppermute(lax.slice_in_dim(block, 0, width, axis=dim), axis, backward)
        block = jnp.concatenate([low, block, high], axis=dim)
    return block


def on_device(
    cell_counts,
    grid_offset,
    fraction,
    species,
    species_density,
    species_pair,
    species_embed,
    species_charge,
):
    cells_x, cells_y, cells_z, components, slots = fraction.shape
    cells = (cells_x, cells_y, cells_z)
    gx, gy, gz = (lax.axis_size(name) for name in ("gx", "gy", "gz"))
    devices = gx * gy * gz
    assert cells_x == gz and slots == 128
    lx, ly, lz = cells_x * gx * PPC, cells_y * gy * PPC, cells_z * gz * PPC
    assert lz % devices == 0
    modes = lz // devices
    yl = cells_y * PPC
    relayout = modes <= 128 and yl % max(1, 128 // modes) == 0

    table = jnp.stack(
        [
            species_density,
            species_pair,
            species_embed,
            species_charge,
            jnp.exp(jnp.log(species_density) * (1.0 / 3.0)),
            1.0 / (species_pair * species_pair),
            -3.0 * species_density / (species_pair * species_pair),
        ]
    )
    slot_index = lax.broadcasted_iota(jnp.int32, species.shape, 3)
    alive = slot_index < cell_counts[..., None]
    kind = jnp.where(alive, species.astype(F32), -1.0)[:, :, :, None, :]
    offsets = grid_offset.astype(F32)
    positions = (offsets + 0.5 + fraction) / PPC

    atoms = jnp.concatenate([offsets, fraction, kind, kind], axis=3)
    atoms = lax.all_to_all(atoms, "gz", split_axis=0, concat_axis=0, tiled=True)
    basis_x, basis_z = real_basis(lx), real_basis(lz)
    x_pair, xt_pair, z_pair = table_pair(basis_x), table_pair(basis_x.T), table_pair(basis_z)
    y_pair = table_pair(np.kron(real_basis(ly), np.eye(modes)))
    lines = make_spread(gz, cells_y, cells_z, slots, lz, devices, relayout)(atoms, table, *z_pair)
    if not relayout:
        lines = lines.reshape(yl, PPC, devices, modes).transpose(2, 1, 0, 3)
        lines = lines.reshape(devices, PPC, yl * modes)
    planes = lax.all_to_all(lines, ("gx", "gy", "gz"), split_axis=0, concat_axis=0, tiled=True)

    ext = padded(
        jnp.concatenate([positions, kind], axis=3), (("gz", 2), ("gy", 1), ("gx", 0)), 1
    )
    density, slope = make_density(cells, slots)(ext, table)
    slope_ext = padded(slope, (("gz", 2), ("gy", 1), ("gx", 0)), 1)

    width = ly * modes
    lane = lax.broadcasted_iota(jnp.int32, (1, width), 1)
    rank = lax.axis_index(("gx", "gy", "gz"))
    green = green_factor(
        signed_modes(lax.broadcasted_iota(jnp.int32, (lx, 1), 0), lx),
        signed_modes(lane // modes, ly),
        signed_modes(rank * modes + lane % modes, lz),
        lx,
        ly,
        lz,
    )
    planes = make_planes(gx, gy, gz, yl * modes, lx, width)(
        planes, *x_pair, *xt_pair, *y_pair, green
    )
    lines = lax.all_to_all(planes, ("gx", "gy", "gz"), split_axis=0, concat_axis=0, tiled=True)
    if not relayout:
        lines = lines.reshape(devices, PPC, yl, modes).transpose(2, 1, 0, 3)
        lines = lines.reshape(yl * PPC, lz)

    eam_force = make_force(cells, slots)(ext, slope_ext, table)

    electric = make_sample(gz, cells_y, cells_z, slots, lz, devices, relayout)(
        lines, atoms, table, *z_pair
    )
    electric = lax.all_to_all(electric, "gz", split_axis=0, concat_axis=0, tiled=True)
    forces = jnp.where(alive[:, :, :, None, :], eam_force + COUPLING * electric, 0.0)
    return (forces, density)


def solution(mesh):
    return jax.shard_map(
        on_device,
        mesh=mesh,
        in_specs=(
            P("gx", "gy", "gz"),
            P("gx", "gy", "gz", None, None),
            P("gx", "gy", "gz", None, None),
            P("gx", "gy", "gz", None),
            P(),
            P(),
            P(),
            P(),
        ),
        out_specs=(P("gx", "gy", "gz", None, None), P("gx", "gy", "gz", None)),
        check_vma=False,
    )
```

time: 477 us -> 169 us (0.35); the launches traced: 468 us -> 168 us
  other arithmetic: 213 us -> 5.3 us
  Pallas kernels: 0 us -> 101 us
  local copies, waits for them, and re-layouts: 85.4 us -> 6.26 us
  matrix products: 43 us -> 0 us
  waiting for transfers between devices: 50 us -> 20.1 us
  loops' own time: 29.1 us -> 0 us
  blocking collectives: 12 us -> 0 us
    reduce_sum x140 -> x0, other arithmetic: 140 us -> none  [the longest x16 71.3 us: force_row(): jnp.sum(coefficient[..., None, :, :] * separation, axis=-1)]
    pallas_call x0 -> x5, Pallas kernels: none -> 101 us  [the longest x1 65.3 us: on_device(): eam_force = make_force(cells, slots)(ext, slope_ext, table)]
    dot_general x23 -> x0, matrix products: 43 us -> none  [the longest x1 6.6 us: sample_cells(): jnp.einsum('bax,bxy->bay', weights_x, blocks, precision=HIGHEST_PRECISION)]
    another operation x2 -> x0, loops' own time: 29.1 us -> none  [the longest x1 15.7 us: on_device(): eam_force = lax.map(force_row, row_ids)]
    sub x36 -> x0, other arithmetic: 27.8 us -> none  [the longest x32 27.6 us: force_row(): -2.0 * own_rep[..., :, None] * other_rep * weight]
    all_to_all x3 -> x4, waiting for transfers between devices: 24.9 us -> 1.33 us  [the longest x1 1.32 us: on_device(): atoms = lax.all_to_all(atoms, 'gz', split_axis=0, concat_axis=0, tiled=True)]
    reshape x8 -> x0, local copies, waits for them, and re-layouts: 22 us -> none  [the longest x2 9.45 us: on_device(): blocks.reshape(cells_x, cells_y, cells_z, PPC, PPC, PPC)]
    add x112 -> x0, other arithmetic: 19 us -> none  [the longest x104 18.6 us: pair_terms(): shift_vector[:, None, None] + other_positions[..., :, None, :]]
  transfers between devices with their start and end apart: 15 -> 16, of which waited for: 10 -> 10; matrix products, arithmetic and copies ran while one was open for 20% -> 2% of each run, Pallas kernels for 0% -> 53%
where the time goes in v1:
time: 169 us; the launch traced here: 168 us
  Pallas kernels  101 us (60%)
  starting transfers between devices  35.3 us (21%)
  waiting for transfers between devices  20.1 us (12%)
  local copies, waits for them, and re-layouts  6.26 us (4%)
  other arithmetic  5.3 us (3%)
    pallas_call x1, Pallas kernels, on_device(): eam_force = make_force(cells, slots)(ext, slope_ext, table)  65.3 us
    pallas_call x1, Pallas kernels, on_device(): density, slope = make_density(cells, slots)(ext, table)  17.9 us
    ppermute x6, starting transfers between devices, padded(): lax.ppermute(lax.slice_in_dim(block, 0, width, axis=dim), axis, backward)  13.1 us
    ppermute x6, waiting for transfers between devices, padded(): lax.ppermute(lax.slice_in_dim(block, block.shape[dim] - width, None, axis...  9.75 us
    ppermute x6, waiting for transfers between devices, padded(): lax.ppermute(lax.slice_in_dim(block, 0, width, axis=dim), axis, backward)  9 us
    pallas_call x1, Pallas kernels, on_device(): make_spread(gz, cells_y, cells_z, slots, lz, devices, relayout)  6.7 us
    pallas_call x1, Pallas kernels, on_device(): make_sample(gz, cells_y, cells_z, slots, lz, devices, relayout)  6.36 us
    all_to_all x1, starting transfers between devices, on_device(): lax.all_to_all(lines, ('gx', 'gy', 'gz'), split_axis=0, concat_axis=0, ti...  5.71 us
  transfers between devices with their start and end apart: 16, of which 10 were waited for; matrix products, arithmetic and copies ran while one was open for 2% of the time, Pallas kernels for 53%

profile of v1, /device:TPU:1, one launch (start us, length us, event | category | flops | bytes accessed | tf_op | source)
XLA Modules:
  0.0 168.3 jit_solution(2482936554754790686)
XLA Ops:
  0.6 0.0 copy-start.6
  0.6 0.0 copy-start.5
  0.7 0.0 copy-start.4
  0.7 0.8 convert_element_type.30
  1.5 0.0 copy-done.6
  1.5 0.0 copy-done.5
  1.5 0.1 convert_select_fusion
  1.6 0.0 copy-done.4
  1.7 0.1 collective-permute-start.1
  1.7 2.6 %collective-permute-start = (f32[4,2,1,4,128]{4,3,2,1,0:T(4,128)S(1)}, f32[4,2,1,4,128]{4,3,2,1,0:T(4,128)S(1)}, u32[]{:S(2)}, u32[]{:S(2)}) collective-permute-start(f32[4,2,1,4,128]{4,3,2,1,0:T(4,128)S(1)} %get-tuple-element.18), channel_id=1, source_target_pairs={{0,1},{1,2},{2,3},{3,0},{4,5},{5,6},{6,7},{7,4},{8,9},{9,10},{10,1... | collective-permute-start | bytes 49160 | tf_op jit(solution)/shard_map/ppermute | solution.py:553
  4.4 0.7 pad_maximum_fusion.1
  5.1 3.3 %all-to-all-start = ((f32[4,2,4,8,128]{4,3,2,1,0:T(8,128)}), f32[4,2,4,8,128]{4,3,2,1,0:T(8,128)S(1)}, u32[]{:S(2)}, u32[]{:S(2)}) async-start(f32[4,2,4,8,128]{4,3,2,1,0:T(8,128)} %pad_maximum_fusion.1), calls=%async_computation | async-start | bytes 262144 | tf_op jit(solution)/shard_map/all_to_all | solution.py:600
  8.4 0.0 copy-start.7
  8.4 0.0 copy-start.8
  8.5 0.6 copy-done.7
  9.1 0.0 copy-done.8
  9.1 0.0 copy-start.10
  9.1 0.6 copy-done.9
  9.8 0.0 copy-done.10
  9.8 0.6 stack.31.table
  10.4 1.3 all-to-all-done.atoms
  11.7 0.6 copy-done.2
  12.4 6.7 %spread.1 = f32[32,16,256]{2,1,0:T(8,128)} custom-call(f32[4,2,4,8,128]{4,3,2,1,0:T(8,128)} %copy-done.2, f32[7,2]{1,0:T(8,128)} %stack.31.table, bf16[256,256]{1,0:T(8,128)(2,1)} %constant.102.clone.basis_hi.x_hi, bf16[256,256]{1,0:T(8,128)(2,1)} %constant.103.clone.basis_lo.x_lo), custom_call_target="tpu_custom_call" | custom-call | tf_op jit(solution)/shard_map/spread/pallas_call | solution.py:604
  19.1 5.7 %all-to-all-start.1 = ((f32[32,16,256]{2,1,0:T(8,128)}), f32[32,16,256]{2,1,0:T(8,128)S(1)}, u32[]{:S(2)}, u32[]{:S(2)}) async-start(f32[32,16,256]{2,1,0:T(8,128)} %spread.1), calls=%async_computation.1 | async-start | bytes 1048576 | tf_op jit(solution)/shard_map/all_to_all | solution.py:608
  24.8 0.0 collective-permute-done.1
  24.8 0.0 collective-permute-done
  24.9 1.4 collective-permute-start.3
  26.3 0.1 collective-permute-start.2
  26.4 3.4 %collective-permute-done.3 = f32[4,1,6,4,128]{4,3,2,1,0:T(4,128)S(1)} collective-permute-done((f32[4,1,6,4,128]{4,3,2,1,0:T(4,128)S(1)}, f32[4,1,6,4,128]{4,3,2,1,0:T(4,128)S(1)}, u32[]{:S(2)}, u32[]{:S(2)}) %collective-permute-start.3) | collective-permute-done | bytes 49184 | tf_op jit(solution)/shard_map/ppermute | solution.py:556
  29.8 1.8 %collective-permute-done.2 = f32[4,1,6,4,128]{4,3,2,1,0:T(4,128)S(1)} collective-permute-done((f32[4,1,6,4,128]{4,3,2,1,0:T(4,128)S(1)}, f32[4,1,6,4,128]{4,3,2,1,0:T(4,128)S(1)}, u32[]{:S(2)}, u32[]{:S(2)}) %collective-permute-start.2) | collective-permute-done | bytes 49184 | tf_op jit(solution)/shard_map/ppermute | solution.py:553
  31.7 4.6 %collective-permute-start.5 = (f32[1,4,6,4,128]{4,3,2,1,0:T(4,128)S(1)}, f32[1,4,6,4,128]{4,3,2,1,0:T(4,128)S(1)}, u32[]{:S(2)}, u32[]{:S(2)}) collective-permute-start(f32[1,4,6,4,128]{4,3,2,1,0:T(4,128)S(1)} %get-tuple-element.15), channel_id=1, source_target_pairs={{8,0},{16,8},{24,16},{0,24},{9,1},{17,9},{25,17},{1,25},{10,2},{18... | collective-permute-start | bytes 147464 | tf_op jit(solution)/shard_map/ppermute | solution.py:556
  36.3 0.0 collective-permute-start.4
  36.3 1.1 divide_select_fusion.green
  37.4 0.1 collective-permute-done.5
  37.5 3.6 %collective-permute-done.4 = f32[1,4,6,4,128]{4,3,2,1,0:T(4,128)S(1)} collective-permute-done((f32[1,4,6,4,128]{4,3,2,1,0:T(4,128)S(1)}, f32[1,4,6,4,128]{4,3,2,1,0:T(4,128)S(1)}, u32[]{:S(2)}, u32[]{:S(2)}) %collective-permute-start.4) | collective-permute-done | bytes 49184 | tf_op jit(solution)/shard_map/ppermute | solution.py:553
  41.0 0.8 pad_maximum_fusion.ext
  41.8 17.9 %density.1 = (f32[4,2,4,128]{3,2,1,0:T(4,128)}, f32[4,2,4,128]{3,2,1,0:T(4,128)}) custom-call(f32[6,4,6,4,128]{4,3,2,1,0:T(4,128)} %pad_maximum_fusion.ext, f32[7,2]{1,0:T(8,128)} %stack.31.table), custom_call_target="tpu_custom_call" | custom-call | flops 566231040 | bytes 294912 | tf_op jit(solution)/shard_map/density/pallas_call | solution.py:613
  59.8 0.0 all-to-all-done.1.data
  59.8 0.8 copy-done.1
  60.5 4.3 %planes.1 = f32[32,16,256]{2,1,0:T(8,128)} custom-call(f32[32,16,256]{2,1,0:T(8,128)} %copy-done.1, bf16[256,256]{1,0:T(8,128)(2,1)} %constant.102.clone.basis_hi.x_hi, bf16[256,256]{1,0:T(8,128)(2,1)} %constant.103.clone.basis_lo.x_lo, bf16[256,256]{1,0:T(8,128)(2,1)} %constant.104.clone.xt_hi, bf16[256,256]{1,0:T(8,128)(2,1)} %constant.105.clone.xt_lo, ...), custom_call_target="tpu_custom_call" | custom-call | tf_op jit(solution)/shard_map/planes/pallas_call | solution.py:627
  64.8 4.7 %all-to-all-start.2 = ((f32[32,16,256]{2,1,0:T(8,128)}), f32[32,16,256]{2,1,0:T(8,128)S(1)}, u32[]{:S(2)}, u32[]{:S(2)}) async-start(f32[32,16,256]{2,1,0:T(8,128)} %planes.1), calls=%async_computation.2 | async-start | bytes 1048576 | tf_op jit(solution)/shard_map/all_to_all | solution.py:630
  69.5 0.4 collective-permute-start.7
  70.0 1.3 collective-permute-start.6
  71.3 2.7 %collective-permute-done.7 = f32[4,2,1,128]{3,2,1,0:T(1,128)S(1)} collective-permute-done((f32[4,2,1,128]{3,2,1,0:T(1,128)S(1)}, f32[4,2,1,128]{3,2,1,0:T(1,128)S(1)}, u32[]{:S(2)}, u32[]{:S(2)}) %collective-permute-start.7) | collective-permute-done | bytes 4128 | tf_op jit(solution)/shard_map/ppermute | solution.py:556
  74.1 0.0 collective-permute-done.6
  74.1 1.3 collective-permute-start.9
  75.4 0.2 collective-permute-start.8
  75.6 2.0 %collective-permute-done.9 = f32[4,1,6,128]{3,2,1,0:T(8,128)S(1)} collective-permute-done((f32[4,1,6,128]{3,2,1,0:T(8,128)S(1)}, f32[4,1,6,128]{3,2,1,0:T(8,128)S(1)}, u32[]{:S(2)}, u32[]{:S(2)}) %collective-permute-start.9) | collective-permute-done | bytes 12320 | tf_op jit(solution)/shard_map/ppermute | solution.py:556
  77.6 0.9 collective-permute-done.8
  78.5 5.2 %collective-permute-start.11 = (f32[1,4,6,128]{3,2,1,0:T(8,128)S(1)}, f32[1,4,6,128]{3,2,1,0:T(8,128)S(1)}, u32[]{:S(2)}, u32[]{:S(2)}) collective-permute-start(f32[1,4,6,128]{3,2,1,0:T(8,128)S(1)} %get-tuple-element.21), channel_id=1, source_target_pairs={{8,0},{16,8},{24,16},{0,24},{9,1},{17,9},{25,17},{1,25},{10,2},{18... | collective-permute-start | bytes 36872 | tf_op jit(solution)/shard_map/ppermute | solution.py:556
  83.7 0.0 collective-permute-start.10
  83.7 0.1 iota_compare_fusion
  83.8 0.8 collective-permute-done.11
  84.6 3.5 %collective-permute-done.10 = f32[1,4,6,128]{3,2,1,0:T(8,128)S(1)} collective-permute-done((f32[1,4,6,128]{3,2,1,0:T(8,128)S(1)}, f32[1,4,6,128]{3,2,1,0:T(8,128)S(1)}, u32[]{:S(2)}, u32[]{:S(2)}) %collective-permute-start.10) | collective-permute-done | bytes 12320 | tf_op jit(solution)/shard_map/ppermute | solution.py:553
  88.1 0.7 pad_maximum_fusion.3.slopes
  88.8 0.0 all-to-all-done.2.data
  88.8 0.8 copy-done
  89.6 6.4 %sample.1 = f32[4,2,4,3,128]{4,3,2,1,0:T(4,128)} custom-call(f32[32,16,256]{2,1,0:T(8,128)} %copy-done, f32[4,2,4,8,128]{4,3,2,1,0:T(8,128)} %copy-done.2, f32[7,2]{1,0:T(8,128)} %stack.31.table, bf16[256,256]{1,0:T(8,128)(2,1)} %constant.102.clone.basis_hi.x_hi, bf16[256,256]{1,0:T(8,128)(2,1)} %constant.103.clone.basis_lo.x_lo), custom_call_target="tpu_custom_call" | custom-call | tf_op jit(solution)/shard_map/sample/pallas_call | solution.py:637
  95.9 1.5 copy.49
  97.4 4.1 %all-to-all-start.3 = ((f32[4,2,4,3,128]{4,2,3,1,0:T(4,128)}), f32[4,2,4,3,128]{4,2,3,1,0:T(4,128)S(1)}, u32[]{:S(2)}, u32[]{:S(2)}) async-start(f32[4,2,4,3,128]{4,2,3,1,0:T(4,128)} %copy.49), calls=%async_computation.3 | async-start | bytes 98304 | tf_op jit(solution)/shard_map/all_to_all | solution.py:640
  101.5 65.3 %force.1 = f32[4,2,4,3,128]{4,3,2,1,0:T(4,128)} custom-call(f32[6,4,6,4,128]{4,3,2,1,0:T(4,128)} %pad_maximum_fusion.ext, f32[6,4,6,128]{3,2,1,0:T(8,128)} %pad_maximum_fusion.3.slopes, f32[7,2]{1,0:T(8,128)} %stack.31.table), custom_call_target="tpu_custom_call" | custom-call | flops 1415577600 | bytes 294912 | tf_op jit(solution)/shard_map/force/pallas_call | solution.py:635
  166.8 0.0 all-to-all-done.3
  166.8 0.9 fusion.1
  167.7 0.6 copy.51
  (20 shorter events, 0.2 us)
Async XLA Ops:
  0.6 0.9 copy-start.6
  0.6 0.9 copy-start.5
  0.7 0.9 copy-start.4
  1.7 23.1 %collective-permute-start.1 = (f32[4,2,1,4,128]{4,3,2,1,0:T(4,128)S(1)}, f32[4,2,1,4,128]{4,3,2,1,0:T(4,128)S(1)}, u32[]{:S(2)}, u32[]{:S(2)}) collective-permute-start(f32[4,2,1,4,128]{4,3,2,1,0:T(4,128)S(1)} %get-tuple-element.19), channel_id=1, source_target_pairs={{1,0},{2,1},{3,2},{0,3},{5,4},{6,5},{7,6},{4,7},{9,8},{10,9},{11,1... | collective-permute-start | bytes 49160 | tf_op jit(solution)/shard_map/ppermute | solution.py:556
  1.7 23.1 %collective-permute-start = (f32[4,2,1,4,128]{4,3,2,1,0:T(4,128)S(1)}, f32[4,2,1,4,128]{4,3,2,1,0:T(4,128)S(1)}, u32[]{:S(2)}, u32[]{:S(2)}) collective-permute-start(f32[4,2,1,4,128]{4,3,2,1,0:T(4,128)S(1)} %get-tuple-element.18), channel_id=1, source_target_pairs={{0,1},{1,2},{2,3},{3,0},{4,5},{5,6},{6,7},{7,4},{8,9},{9,10},{10,1... | collective-permute-start | bytes 49160 | tf_op jit(solution)/shard_map/ppermute | solution.py:553
  5.1 6.6 %all-to-all-start = ((f32[4,2,4,8,128]{4,3,2,1,0:T(8,128)}), f32[4,2,4,8,128]{4,3,2,1,0:T(8,128)S(1)}, u32[]{:S(2)}, u32[]{:S(2)}) async-start(f32[4,2,4,8,128]{4,3,2,1,0:T(8,128)} %pad_maximum_fusion.1), calls=%async_computation | async-start | bytes 262144 | tf_op jit(solution)/shard_map/all_to_all | solution.py:600
  8.4 0.7 copy-start.7
  8.4 0.7 copy-start.8
  9.1 0.7 copy-start.9
  9.1 0.7 copy-start.10
  11.7 0.6 copy-start.2
  19.1 40.7 %all-to-all-start.1 = ((f32[32,16,256]{2,1,0:T(8,128)}), f32[32,16,256]{2,1,0:T(8,128)S(1)}, u32[]{:S(2)}, u32[]{:S(2)}) async-start(f32[32,16,256]{2,1,0:T(8,128)} %spread.1), calls=%async_computation.1 | async-start | bytes 1048576 | tf_op jit(solution)/shard_map/all_to_all | solution.py:608
  24.9 5.0 %collective-permute-start.3 = (f32[4,1,6,4,128]{4,3,2,1,0:T(4,128)S(1)}, f32[4,1,6,4,128]{4,3,2,1,0:T(4,128)S(1)}, u32[]{:S(2)}, u32[]{:S(2)}) collective-permute-start(f32[4,1,6,4,128]{4,3,2,1,0:T(4,128)S(1)} %get-tuple-element.17), channel_id=1, source_target_pairs={{4,0},{0,4},{5,1},{1,5},{6,2},{2,6},{7,3},{3,7},{12,8},{8,12},{13,... | collective-permute-start | bytes 147464 | tf_op jit(solution)/shard_map/ppermute | solution.py:556
  26.3 5.3 %collective-permute-start.2 = (f32[4,1,6,4,128]{4,3,2,1,0:T(4,128)S(1)}, f32[4,1,6,4,128]{4,3,2,1,0:T(4,128)S(1)}, u32[]{:S(2)}, u32[]{:S(2)}) collective-permute-start(f32[4,1,6,4,128]{4,3,2,1,0:T(4,128)S(1)} %get-tuple-element.16), channel_id=1, source_target_pairs={{0,4},{4,0},{1,5},{5,1},{2,6},{6,2},{3,7},{7,3},{8,12},{12,8},{9,1... | collective-permute-start | bytes 147464 | tf_op jit(solution)/shard_map/ppermute | solution.py:553
  31.7 5.8 %collective-permute-start.5 = (f32[1,4,6,4,128]{4,3,2,1,0:T(4,128)S(1)}, f32[1,4,6,4,128]{4,3,2,1,0:T(4,128)S(1)}, u32[]{:S(2)}, u32[]{:S(2)}) collective-permute-start(f32[1,4,6,4,128]{4,3,2,1,0:T(4,128)S(1)} %get-tuple-element.15), channel_id=1, source_target_pairs={{8,0},{16,8},{24,16},{0,24},{9,1},{17,9},{25,17},{1,25},{10,2},{18... | collective-permute-start | bytes 147464 | tf_op jit(solution)/shard_map/ppermute | solution.py:556
  36.3 4.7 %collective-permute-start.4 = (f32[1,4,6,4,128]{4,3,2,1,0:T(4,128)S(1)}, f32[1,4,6,4,128]{4,3,2,1,0:T(4,128)S(1)}, u32[]{:S(2)}, u32[]{:S(2)}) collective-permute-start(f32[1,4,6,4,128]{4,3,2,1,0:T(4,128)S(1)} %get-tuple-element.14), channel_id=1, source_target_pairs={{0,8},{8,16},{16,24},{24,0},{1,9},{9,17},{17,25},{25,1},{2,10},{10... | collective-permute-start | bytes 147464 | tf_op jit(solution)/shard_map/ppermute | solution.py:553
  59.8 0.8 copy-start.1
  64.8 4.7 %copy-start.3 = (f32[4,2,4,128]{3,2,1,0:T(4,128)S(1)}, f32[4,2,4,128]{3,2,1,0:T(4,128)}, u32[]{:S(2)}) copy-start(f32[4,2,4,128]{3,2,1,0:T(4,128)} %get-tuple-element.4) | copy-start | bytes 49156
  64.8 24.0 %all-to-all-start.2 = ((f32[32,16,256]{2,1,0:T(8,128)}), f32[32,16,256]{2,1,0:T(8,128)S(1)}, u32[]{:S(2)}, u32[]{:S(2)}) async-start(f32[32,16,256]{2,1,0:T(8,128)} %planes.1), calls=%async_computation.2 | async-start | bytes 1048576 | tf_op jit(solution)/shard_map/all_to_all | solution.py:630
  69.5 4.5 %collective-permute-start.7 = (f32[4,2,1,128]{3,2,1,0:T(1,128)S(1)}, f32[4,2,1,128]{3,2,1,0:T(1,128)S(1)}, u32[]{:S(2)}, u32[]{:S(2)}) collective-permute-start(f32[4,2,1,128]{3,2,1,0:T(1,128)S(1)} %get-tuple-element.28), channel_id=1, source_target_pairs={{1,0},{2,1},{3,2},{0,3},{5,4},{6,5},{7,6},{4,7},{9,8},{10,9},{11,1... | collective-permute-start | bytes 12296 | tf_op jit(solution)/shard_map/ppermute | solution.py:556
  70.0 4.1 %collective-permute-start.6 = (f32[4,2,1,128]{3,2,1,0:T(1,128)S(1)}, f32[4,2,1,128]{3,2,1,0:T(1,128)S(1)}, u32[]{:S(2)}, u32[]{:S(2)}) collective-permute-start(f32[4,2,1,128]{3,2,1,0:T(1,128)S(1)} %get-tuple-element.27), channel_id=1, source_target_pairs={{0,1},{1,2},{2,3},{3,0},{4,5},{5,6},{6,7},{7,4},{8,9},{9,10},{10,1... | collective-permute-start | bytes 12296 | tf_op jit(solution)/shard_map/ppermute | solution.py:553
  74.1 3.5 %collective-permute-start.9 = (f32[4,1,6,128]{3,2,1,0:T(8,128)S(1)}, f32[4,1,6,128]{3,2,1,0:T(8,128)S(1)}, u32[]{:S(2)}, u32[]{:S(2)}) collective-permute-start(f32[4,1,6,128]{3,2,1,0:T(8,128)S(1)} %get-tuple-element.26), channel_id=1, source_target_pairs={{4,0},{0,4},{5,1},{1,5},{6,2},{2,6},{7,3},{3,7},{12,8},{8,12},{13,... | collective-permute-start | bytes 36872 | tf_op jit(solution)/shard_map/ppermute | solution.py:556
  75.4 3.1 %collective-permute-start.8 = (f32[4,1,6,128]{3,2,1,0:T(8,128)S(1)}, f32[4,1,6,128]{3,2,1,0:T(8,128)S(1)}, u32[]{:S(2)}, u32[]{:S(2)}) collective-permute-start(f32[4,1,6,128]{3,2,1,0:T(8,128)S(1)} %get-tuple-element.25), channel_id=1, source_target_pairs={{0,4},{4,0},{1,5},{5,1},{2,6},{6,2},{3,7},{7,3},{8,12},{12,8},{9,1... | collective-permute-start | bytes 36872 | tf_op jit(solution)/shard_map/ppermute | solution.py:553
  78.5 6.1 %collective-permute-start.11 = (f32[1,4,6,128]{3,2,1,0:T(8,128)S(1)}, f32[1,4,6,128]{3,2,1,0:T(8,128)S(1)}, u32[]{:S(2)}, u32[]{:S(2)}) collective-permute-start(f32[1,4,6,128]{3,2,1,0:T(8,128)S(1)} %get-tuple-element.21), channel_id=1, source_target_pairs={{8,0},{16,8},{24,16},{0,24},{9,1},{17,9},{25,17},{1,25},{10,2},{18... | collective-permute-start | bytes 36872 | tf_op jit(solution)/shard_map/ppermute | solution.py:556
  83.7 4.4 %collective-permute-start.10 = (f32[1,4,6,128]{3,2,1,0:T(8,128)S(1)}, f32[1,4,6,128]{3,2,1,0:T(8,128)S(1)}, u32[]{:S(2)}, u32[]{:S(2)}) collective-permute-start(f32[1,4,6,128]{3,2,1,0:T(8,128)S(1)} %get-tuple-element.20), channel_id=1, source_target_pairs={{0,8},{8,16},{16,24},{24,0},{1,9},{9,17},{17,25},{25,1},{2,10},{10... | collective-permute-start | bytes 36872 | tf_op jit(solution)/shard_map/ppermute | solution.py:553
  88.8 0.8 copy-start
  97.4 69.4 %all-to-all-start.3 = ((f32[4,2,4,3,128]{4,2,3,1,0:T(4,128)}), f32[4,2,4,3,128]{4,2,3,1,0:T(4,128)S(1)}, u32[]{:S(2)}, u32[]{:S(2)}) async-start(f32[4,2,4,3,128]{4,2,3,1,0:T(4,128)} %copy.49), calls=%async_computation.3 | async-start | bytes 98304 | tf_op jit(solution)/shard_map/all_to_all | solution.py:640

commit v2 on v1

--- a/solution.py
+++ b/solution.py
@@ -9,6 +9,7 @@
 from jax.experimental import pallas as pl
 from jax.experimental.pallas import tpu as pltpu
 from jax.sharding import PartitionSpec as P
+
 
 NSPEC = 2
 PPC = 16
@@ -217,7 +218,9 @@
     yl = cells_y * PPC
     rows = PPC * PPC
 
-    def kernel(data, atoms, table, basis_hi, basis_lo, out, lines, line_hi, line_lo):
+    def kernel(
+        data, atoms, short, dens, table, basis_hi, basis_lo, out, lines, line_hi, line_lo
+    ):
         if relayout:
             chunks = 128 // modes
             for tile in range(lz // 128):
@@ -257,17 +260,23 @@
                     force_x += wy[y : y + 1] * block
                     force_y += sy[y : y + 1] * block
                     force_z += wy[y : y + 1] * tilted[y * PPC : (y + 1) * PPC]
-                charge = -by_kind(cell[6:7], table, 3)
+                charge = -COUPLING * by_kind(cell[6:7], table, 3)
+                here = pl.ds(column, 1)
                 result = [
                     charge * jnp.sum(force * weight, axis=0, keepdims=True)
-                    for force, weight in ((force_x, sx), (force_y, wx), (force_z, wx))
+                    + short[d, cy, here, :]
+                    for d, (force, weight) in enumerate(
+                        ((force_x, sx), (force_y, wx), (force_z, wx))
+                    )
                 ]
+                result = [jnp.where(cell[6:7] >= 0.0, value, 0.0) for value in result]
+                result.append(dens[cy, here, :])
                 out[column // cells_z, cy, column % cells_z] = jnp.concatenate(result, axis=0)
 
     return pl.pallas_call(
         kernel,
-        out_shape=jax.ShapeDtypeStruct((parts, cells_y, cells_z, 3, slots), F32),
-        in_specs=[VMEM, VMEM, SMEM, VMEM, VMEM],
+        out_shape=jax.ShapeDtypeStruct((parts, cells_y, cells_z, 4, slots), F32),
+        in_specs=[VMEM, VMEM, VMEM, VMEM, SMEM, VMEM, VMEM],
         out_specs=VMEM,
         scratch_shapes=[
             pltpu.VMEM((cells_y * rows, lz), F32),
@@ -279,120 +288,114 @@
     )
 
 
-ORDER = ((0, 0), (1, 0), (0, 1), (1, 1), (2, 0), (0, 2))
-
-
-def spread_pieces(values, side):
+WIDE = ((0, 0), (1, 0), (0, 1), (1, 1), (2, 0), (0, 2))
+SHORT = WIDE[:4]
+
+
+def piece_rows(values, order, side):
     pieces = split3(values)
-    stacked = [pieces[entry[side]] for entry in ORDER]
-    stacked += [jnp.zeros_like(values)] * 2
-    return jnp.concatenate(stacked, axis=0)
-
-
-def cell_positions(ext, x, y, sizes):
-    count_x, count_y, count_z = sizes
-    along_z = lax.broadcasted_iota(jnp.int32, (count_z, ext.shape[-1]), 0).astype(F32)
-    pos_x = ext[x, y, :, 0, :] + (x - 0.5 * count_x)
-    pos_y = ext[x, y, :, 1, :] + (y - 0.5 * count_y)
-    pos_z = ext[x, y, :, 2, :] + (along_z - 0.5 * count_z)
-    return (pos_x, pos_y, pos_z)
-
-
-def cell_at(index, cells):
-    cells_x, cells_y, cells_z = cells
-    x = index // (cells_y * cells_z)
-    y = (index // cells_z) % cells_y
-    z = index % cells_z
-    return x, y, z
-
-
-def make_density(cells, slots):
-    cells_x, cells_y, cells_z = cells
-    sizes = (cells_x + 2, cells_y + 2, cells_z + 2)
-    own = cells_x * cells_y * cells_z
-    total = sizes[0] * sizes[1] * sizes[2]
-
-    def kernel(ext, table, density, slope, feature, own_feature, right, left, sums):
+    return jnp.concatenate([pieces[entry[side]] for entry in order], axis=0)
+
+
+def channel(block, y, nz, index):
+    return block[pl.ds(y * nz * 4 + index, nz, stride=4), :]
+
+
+def row_positions(block, x, y, sy, nz):
+    pos_x = channel(block, y, nz, 0) + (x - 1.0)
+    pos_y = channel(block, y, nz, 1) + (y - 0.5 * (sy - 1))
+    return pos_x, pos_y, channel(block, y, nz, 2)
+
+
+def same_slot(slots):
+    return lax.broadcasted_iota(jnp.int32, (slots, slots), 0) == lax.broadcasted_iota(
+        jnp.int32, (slots, slots), 1
+    )
+
+
+def make_density(cells_y, nz, slots):
+    sy = cells_y + 2
+    own = cells_y * nz
+    total = 3 * sy * nz
+
+    def kernel(low, mid, high, table, density, slope, feature, own_feature, right, left, sums):
         feature[...] = jnp.zeros(feature.shape, F32)
         own_feature[...] = jnp.zeros(own_feature.shape, F32)
-        for x in range(sizes[0]):
-            for y in range(sizes[1]):
-                pos = cell_positions(ext, x, y, sizes)
+        for x, block in enumerate((low, mid, high)):
+            for y in range(sy):
+                pos = row_positions(block, x, y, sy, nz)
                 square = pos[0] * pos[0] + pos[1] * pos[1] + pos[2] * pos[2]
-                scale = by_kind(ext[x, y, :, 3, :], table, 4)
-                base = (x * sizes[1] + y) * sizes[2]
-                here = pl.ds(base, sizes[2])
-                feature[here, 0, :] = scale * (1.0 - square)
+                scale = by_kind(channel(block, y, nz, 3), table, 4)
+                base = (x * sy + y) * nz * 8
+                feature[pl.ds(base, nz, stride=8), :] = scale * (1.0 - square)
                 for d in range(3):
-                    feature[here, 1 + d, :] = 2.0 * scale * pos[d]
-                feature[here, 4, :] = -scale
-                if 1 <= x <= cells_x and 1 <= y <= cells_y:
-                    there = pl.ds(((x - 1) * cells_y + y - 1) * cells_z, cells_z)
-                    own_feature[there, 0, :] = jnp.ones((cells_z, slots), F32)
-                    for d in range(3):
-                        own_feature[there, 1 + d, :] = pos[d][1 : 1 + cells_z]
-                    own_feature[there, 4, :] = square[1 : 1 + cells_z]
+                    feature[pl.ds(base + 1 + d, nz, stride=8), :] = 2.0 * scale * pos[d]
+                feature[pl.ds(base + 4, nz, stride=8), :] = -scale
+                if x == 1 and 1 <= y <= cells_y:
+                    for dz in range(3):
+                        across = pos[2] - (dz - 1.0)
+                        square = pos[0] * pos[0] + pos[1] * pos[1] + across * across
+                        base = (dz * own + (y - 1) * nz) * 8
+                        rows = (jnp.ones_like(square), pos[0], pos[1], across, square)
+                        for k, value in enumerate(rows):
+                            own_feature[pl.ds(base + k, nz, stride=8), :] = value
 
         def fill_right(n, carry):
-            right[n] = spread_pieces(feature[n], 0).astype(BF16)
+            right[n] = piece_rows(feature[pl.ds(n * 8, 8), :], WIDE, 0).astype(BF16)
             return carry
 
         def fill_left(n, carry):
-            left[n] = spread_pieces(own_feature[n], 1).T.astype(BF16)
+            left[n] = piece_rows(own_feature[pl.ds(n * 8, 8), :], WIDE, 1).T.astype(BF16)
             return carry
 
         lax.fori_loop(0, total, fill_right, 0, unroll=8)
-        lax.fori_loop(0, own, fill_left, 0, unroll=4)
-        same = lax.broadcasted_iota(jnp.int32, (slots, slots), 0) == lax.broadcasted_iota(
-            jnp.int32, (slots, slots), 1
-        )
+        lax.fori_loop(0, 3 * own, fill_left, 0, unroll=8)
+        same = same_slot(slots)
         lane = lax.broadcasted_iota(jnp.int32, (slots, 128), 1)
         sums[...] = jnp.zeros(sums.shape, F32)
-        near = [
-            (dx * sizes[1] + dy) * sizes[2] + dz
-            for dx in range(3)
-            for dy in range(3)
-            for dz in range(3)
-        ]
-        centre = near.pop(13)
 
         def one_cell(n, carry):
-            x, y, z = cell_at(n, cells)
-            base = (x * sizes[1] + y) * sizes[2] + z
-            lhs = left[n]
-            weight = jnp.maximum(dot(lhs, right[base + centre], NN), 0.0)
+            y, z = n // nz, n % nz
+            weight = jnp.maximum(dot(left[own + n], right[(sy + y + 1) * nz + z], NN), 0.0)
             weight = jnp.where(same, 0.0, weight)
             total_sum = weight * weight * weight
-            for first, second in zip(near[0::2], near[1::2]):
-                rhs = jnp.concatenate([right[base + first], right[base + second]], axis=1)
-                weight = jnp.maximum(dot(lhs, rhs, NN), 0.0)
-                cube = weight * weight * weight
-                total_sum = total_sum + cube[:, :slots] + cube[:, slots:]
+            for dz in range(3):
+                zz = (z + (dz - 1 + nz)) % nz
+                lhs = left[dz * own + n]
+                near = [(dx * sy + y + dy) * nz + zz for dx in range(3) for dy in range(3)]
+                if dz == 1:
+                    near.pop(4)
+                while near:
+                    pair, near = near[:2], near[2:]
+                    rhs = [right[index] for index in pair]
+                    rhs = jnp.concatenate(rhs, axis=1) if len(rhs) > 1 else rhs[0]
+                    weight = jnp.maximum(dot(lhs, rhs, NN), 0.0)
+                    cube = weight * weight * weight
+                    for part in range(len(pair)):
+                        total_sum = total_sum + cube[:, part * slots : (part + 1) * slots]
             column = jnp.sum(total_sum, axis=1, keepdims=True)
             sums[...] = jnp.where(lane == n, column, sums[...])
             return carry
 
-        lax.fori_loop(0, own, one_cell, 0)
+        lax.fori_loop(0, own, one_cell, 0, unroll=2)
         rows = sums[...].T
-        for x in range(cells_x):
-            for y in range(cells_y):
-                start = (x * cells_y + y) * cells_z
-                kind = ext[x + 1, y + 1, :, 3, :][1 : 1 + cells_z]
-                value = jnp.where(kind >= 0.0, rows[start : start + cells_z], 0.0)
-                density[x, y] = value
-                slope[x, y] = -by_kind(kind, table, 2) / (2.0 * jnp.sqrt(1.0 + value))
-
-    shape = jax.ShapeDtypeStruct((cells_x, cells_y, cells_z, slots), F32)
+        for y in range(cells_y):
+            kind = channel(mid, y + 1, nz, 3)
+            value = jnp.where(kind >= 0.0, rows[y * nz : (y + 1) * nz], 0.0)
+            density[y] = value
+            slope[y] = -by_kind(kind, table, 2) / (2.0 * jnp.sqrt(1.0 + value))
+
+    shape = jax.ShapeDtypeStruct((cells_y, nz, slots), F32)
     return pl.pallas_call(
         kernel,
         out_shape=(shape, shape),
-        in_specs=[VMEM, SMEM],
+        in_specs=[VMEM, VMEM, VMEM, SMEM],
         out_specs=(VMEM, VMEM),
         scratch_shapes=[
-            pltpu.VMEM((total, 8, slots), F32),
-            pltpu.VMEM((own, 8, slots), F32),
-            pltpu.VMEM((total, 64, slots), BF16),
-            pltpu.VMEM((own, slots, 64), BF16),
+            pltpu.VMEM((total * 8, slots), F32),
+            pltpu.VMEM((3 * own * 8, slots), F32),
+            pltpu.VMEM((total, 48, slots), BF16),
+            pltpu.VMEM((3 * own, slots, 48), BF16),
             pltpu.VMEM((slots, 128), F32),
         ],
         compiler_params=PARAMS,
@@ -403,136 +406,130 @@
     )
 
 
-def make_force(cells, slots):
-    cells_x, cells_y, cells_z = cells
-    sizes = (cells_x + 2, cells_y + 2, cells_z + 2)
-    own = cells_x * cells_y * cells_z
-    total = sizes[0] * sizes[1] * sizes[2]
-    chunk = 32
-
-    def kernel(ext, slopes, table, out, feature, own_feature, place, right, left, both, sums):
-        feature[...] = jnp.zeros(feature.shape, F32)
-        own_feature[...] = jnp.zeros(own_feature.shape, F32)
-        for x in range(sizes[0]):
-            for y in range(sizes[1]):
-                pos = cell_positions(ext, x, y, sizes)
+def make_force(cells_y, nz, slots):
+    sy = cells_y + 2
+    own = cells_y * nz
+    total = 3 * sy * nz
+    chunk = 64
+
+    def kernel(
+        low, mid, high, slope_low, slope_mid, slope_high, table, out,
+        feature, extra, own_feature, own_extra, place, right, right_extra, left, left_extra,
+        sums,
+    ):
+        for ref in (feature, extra, own_feature, own_extra):
+            ref[...] = jnp.zeros(ref.shape, F32)
+        blocks = zip((low, mid, high), (slope_low, slope_mid, slope_high))
+        for x, (block, slopes) in enumerate(blocks):
+            for y in range(sy):
+                pos = row_positions(block, x, y, sy, nz)
                 square = pos[0] * pos[0] + pos[1] * pos[1] + pos[2] * pos[2]
-                kind = ext[x, y, :, 3, :]
+                kind = channel(block, y, nz, 3)
                 scale = by_kind(kind, table, 1)
-                steep = slopes[x, y] * by_kind(kind, table, 5)
+                steep = slopes[y] * by_kind(kind, table, 5)
                 mild = by_kind(kind, table, 6)
-                here = pl.ds((x * sizes[1] + y) * sizes[2], sizes[2])
-                feature[here, 0, :] = scale * (1.0 - square)
+                base = (x * sy + y) * nz * 8
+                feature[pl.ds(base, nz, stride=8), :] = scale * (1.0 - square)
                 for d in range(3):
-                    feature[here, 1 + d, :] = 2.0 * scale * pos[d]
-                    place[here, d, :] = pos[d]
-                feature[here, 4, :] = -scale
-                feature[here, 8, :] = steep
-                feature[here, 9, :] = mild
-                if 1 <= x <= cells_x and 1 <= y <= cells_y:
-                    inner = slice(1, 1 + cells_z)
-                    there = pl.ds(((x - 1) * cells_y + y - 1) * cells_z, cells_z)
-                    own_feature[there, 0, :] = scale[inner]
-                    for d in range(3):
-                        own_feature[there, 1 + d, :] = (scale * pos[d])[inner]
-                    own_feature[there, 4, :] = (scale * square)[inner]
-                    own_feature[there, 8, :] = mild[inner]
-                    own_feature[there, 9, :] = steep[inner]
+                    feature[pl.ds(base + 1 + d, nz, stride=8), :] = 2.0 * scale * pos[d]
+                    place[pl.ds(base + d, nz, stride=8), :] = pos[d]
+                feature[pl.ds(base + 4, nz, stride=8), :] = -scale
+                extra[pl.ds(base, nz, stride=8), :] = steep
+                extra[pl.ds(base + 1, nz, stride=8), :] = mild
+                if x == 1 and 1 <= y <= cells_y:
+                    base = (y - 1) * nz * 8
+                    own_extra[pl.ds(base, nz, stride=8), :] = mild
+                    own_extra[pl.ds(base + 1, nz, stride=8), :] = steep
+                    for dz in range(3):
+                        across = pos[2] - (dz - 1.0)
+                        square = pos[0] * pos[0] + pos[1] * pos[1] + across * across
+                        base = (dz * own + (y - 1) * nz) * 8
+                        rows = (1.0, pos[0], pos[1], across, square)
+                        for k, value in enumerate(rows):
+                            own_feature[pl.ds(base + k, nz, stride=8), :] = scale * value
 
         def fill_right(n, carry):
-            values = feature[n]
-            right[n, pl.ds(0, 64), :] = spread_pieces(values[0:8], 0).astype(BF16)
-            right[n, pl.ds(64, 64), :] = spread_pieces(values[8:16], 0).astype(BF16)
+            rows = pl.ds(n * 8, 8)
+            right[n] = piece_rows(feature[rows, :], WIDE, 0).astype(BF16)
+            right_extra[n] = piece_rows(extra[rows, :], SHORT, 0).astype(BF16)
             return carry
 
         def fill_left(n, carry):
-            values = own_feature[n]
-            left[n, :, pl.ds(0, 64)] = spread_pieces(values[0:8], 1).T.astype(BF16)
-            left[n, :, pl.ds(64, 64)] = spread_pieces(values[8:16], 1).T.astype(BF16)
+            left[n] = piece_rows(own_feature[pl.ds(n * 8, 8), :], WIDE, 1).T.astype(BF16)
             return carry
 
+        def fill_left_extra(n, carry):
+            left_extra[n] = piece_rows(own_extra[pl.ds(n * 8, 8), :], SHORT, 1).T.astype(BF16)
+            return carry
+
         lax.fori_loop(0, total, fill_right, 0, unroll=8)
-        lax.fori_loop(0, own, fill_left, 0, unroll=4)
-        same = lax.broadcasted_iota(jnp.int32, (slots, slots), 0) == lax.broadcasted_iota(
-            jnp.int32, (slots, slots), 1
-        )
+        lax.fori_loop(0, 3 * own, fill_left, 0, unroll=8)
+        lax.fori_loop(0, own, fill_left_extra, 0, unroll=8)
+        same = same_slot(slots)
         lane = lax.broadcasted_iota(jnp.int32, (slots, 128), 1)
         sums[...] = jnp.zeros(sums.shape, F32)
-        near = [
-            (dx * sizes[1] + dy) * sizes[2] + dz
-            for dx in range(3)
-            for dy in range(3)
-            for dz in range(3)
-        ]
-        centre = near.pop(13)
-        near = [centre] + near
-
-        def products(n, slot):
-            x, y, z = cell_at(n, cells)
-            base = (x * sizes[1] + y) * sizes[2] + z
-            lhs = (left[n, :, pl.ds(0, 64)], left[n, :, pl.ds(64, 64)])
-            for part in range(2):
-                rows = pl.ds(part * 64, 64)
-                value = dot(lhs[part], right[base + centre, rows, :], NN)
-                if part == 0:
-                    value = jnp.where(same, 0.0, value)
-                both[slot, part, 0] = value
-                for index in range(1, 27, 2):
-                    rhs = jnp.concatenate(
-                        [right[base + near[index], rows, :], right[base + near[index + 1], rows, :]],
-                        axis=1,
-                    )
-                    value = dot(lhs[part], rhs, NN)
-                    both[slot, part, index] = value[:, :slots]
-                    both[slot, part, index + 1] = value[:, slots:]
-
-        products(0, 0)
 
         def one_cell(n, carry):
-            slot = n % 2
-            x, y, z = cell_at(n, cells)
-            base = (x * sizes[1] + y) * sizes[2] + z
-            products(jnp.minimum(n + 1, own - 1), 1 - slot)
+            y, z = n // nz, n % nz
             for start in range(0, slots, chunk):
                 rows = pl.ds(start, chunk)
-                acc = [jnp.zeros((chunk, slots), F32) for _ in range(4)]
-                for index in range(27):
-                    weight = jnp.maximum(both[slot, 0, index, rows, :], 0.0)
-                    value = (weight * both[slot, 1, index, rows, :] - 2.0) * weight
-                    acc[3] = acc[3] + value
-                    for d in range(3):
-                        acc[d] = acc[d] + value * place[base + near[index], pl.ds(d, 1), :]
+                lhs_extra = left_extra[n, rows, :]
+                parts = [jnp.zeros((chunk, slots), F32) for _ in range(4)]
+                for dz in range(3):
+                    zz = (z + (dz - 1 + nz)) % nz
+                    lhs = left[dz * own + n, rows, :]
+                    near = [(dx * sy + y + dy) * nz + zz for dx in range(3) for dy in range(3)]
+                    if dz == 1:
+                        near.append(near.pop(4))
+                    for index in range(0, 9, 2):
+                        pair = near[index : index + 2]
+                        rhs = [right[cell] for cell in pair]
+                        rhs_extra = [right_extra[cell] for cell in pair]
+                        if len(pair) > 1:
+                            rhs = [jnp.concatenate(rhs, axis=1)]
+                            rhs_extra = [jnp.concatenate(rhs_extra, axis=1)]
+                        weight = jnp.maximum(dot(lhs, rhs[0], NN), 0.0)
+                        if dz == 1 and index == 8:
+                            weight = jnp.where(same[start : start + chunk], 0.0, weight)
+                        value = (weight * dot(lhs_extra, rhs_extra[0], NN) - 2.0) * weight
+                        for k, cell in enumerate(pair):
+                            tile = value[:, k * slots : (k + 1) * slots]
+                            parts[3] = parts[3] + tile
+                            for d in range(3):
+                                there = place[pl.ds(cell * 8 + d, 1), :]
+                                if d == 2 and dz != 1:
+                                    there = there + (dz - 1.0)
+                                parts[d] = parts[d] + tile * there
                 for d in range(4):
-                    column = jnp.sum(acc[d], axis=1, keepdims=True)
+                    column = jnp.sum(parts[d], axis=1, keepdims=True)
                     sums[d, rows, :] = jnp.where(
                         lane[start : start + chunk] == n, column, sums[d, rows, :]
                     )
             return carry
 
-        lax.fori_loop(0, own, one_cell, 0)
+        lax.fori_loop(0, own, one_cell, 0, unroll=2)
         rows = [sums[d].T for d in range(4)]
-        for x in range(cells_x):
-            for y in range(cells_y):
-                start = (x * cells_y + y) * cells_z
-                stop = start + cells_z
-                pos = cell_positions(ext, x + 1, y + 1, sizes)
-                for d in range(3):
-                    out[x, y, :, d, :] = 2.0 * (
-                        rows[d][start:stop] - pos[d][1 : 1 + cells_z] * rows[3][start:stop]
-                    )
+        for y in range(cells_y):
+            pos = row_positions(mid, 1, y + 1, sy, nz)
+            part = slice(y * nz, (y + 1) * nz)
+            for d in range(3):
+                out[d, y] = 2.0 * (rows[d][part] - pos[d] * rows[3][part])
 
     return pl.pallas_call(
         kernel,
-        out_shape=jax.ShapeDtypeStruct((cells_x, cells_y, cells_z, 3, slots), F32),
-        in_specs=[VMEM, VMEM, SMEM],
+        out_shape=jax.ShapeDtypeStruct((3, cells_y, nz, slots), F32),
+        in_specs=[VMEM] * 6 + [SMEM],
         out_specs=VMEM,
         scratch_shapes=[
-            pltpu.VMEM((total, 16, slots), F32),
-            pltpu.VMEM((own, 16, slots), F32),
-            pltpu.VMEM((total, 8, slots), F32),
-            pltpu.VMEM((total, 128, slots), BF16),
-            pltpu.VMEM((own, slots, 128), BF16),
-            pltpu.VMEM((2, 2, 27, slots, slots), F32),
+            pltpu.VMEM((total * 8, slots), F32),
+            pltpu.VMEM((total * 8, slots), F32),
+            pltpu.VMEM((3 * own * 8, slots), F32),
+            pltpu.VMEM((own * 8, slots), F32),
+            pltpu.VMEM((total * 8, slots), F32),
+            pltpu.VMEM((total, 48, slots), BF16),
+            pltpu.VMEM((total, 32, slots), BF16),
+            pltpu.VMEM((3 * own, slots, 48), BF16),
+            pltpu.VMEM((own, slots, 32), BF16),
             pltpu.VMEM((4, slots, 128), F32),
         ],
         compiler_params=PARAMS,
@@ -545,17 +542,24 @@
     )
 
 
-def padded(block, sides, width):
-    for axis, dim in sides:
-        count = lax.axis_size(axis)
-        forward = [(i, (i + 1) % count) for i in range(count)]
-        backward = [(target, source) for source, target in forward]
-        low = lax.ppermute(
-            lax.slice_in_dim(block, block.shape[dim] - width, None, axis=dim), axis, forward
-        )
-        high = lax.ppermute(lax.slice_in_dim(block, 0, width, axis=dim), axis, backward)
-        block = jnp.concatenate([low, block, high], axis=dim)
-    return block
+def shifted(axis, count):
+    up = [(i, (i + 1) % count) for i in range(count)]
+    down = [(target, source) for source, target in up]
+    return lambda part: lax.ppermute(part, axis, up), lambda part: lax.ppermute(part, axis, down)
+
+
+def halo(block, gx, gy, gz):
+    up, down = shifted("gy", gy)
+    if gy == 2 and block.shape[0] == 2:
+        other = up(block)
+        low, high = other[-1:], other[:1]
+    else:
+        low, high = up(block[-1:]), down(block[:1])
+    middle = jnp.concatenate([low, block, high], axis=0)
+    up, down = shifted(("gx", "gz"), gx * gz)
+    low = up(middle)
+    high = down(middle)
+    return low, middle, high
 
 
 def on_device(
@@ -568,8 +572,7 @@
     species_embed,
     species_charge,
 ):
-    cells_x, cells_y, cells_z, components, slots = fraction.shape
-    cells = (cells_x, cells_y, cells_z)
+    cells_x, cells_y, cells_z, _, slots = fraction.shape
     gx, gy, gz = (lax.axis_size(name) for name in ("gx", "gy", "gz"))
     devices = gx * gy * gz
     assert cells_x == gz and slots == 128
@@ -594,24 +597,26 @@
     alive = slot_index < cell_counts[..., None]
     kind = jnp.where(alive, species.astype(F32), -1.0)[:, :, :, None, :]
     offsets = grid_offset.astype(F32)
-    positions = (offsets + 0.5 + fraction) / PPC
 
     atoms = jnp.concatenate([offsets, fraction, kind, kind], axis=3)
     atoms = lax.all_to_all(atoms, "gz", split_axis=0, concat_axis=0, tiled=True)
     basis_x, basis_z = real_basis(lx), real_basis(lz)
     x_pair, xt_pair, z_pair = table_pair(basis_x), table_pair(basis_x.T), table_pair(basis_z)
     y_pair = table_pair(np.kron(real_basis(ly), np.eye(modes)))
-    lines = make_spread(gz, cells_y, cells_z, slots, lz, devices, relayout)(atoms, table, *z_pair)
+    spread = make_spread(gz, cells_y, cells_z, slots, lz, devices, relayout)
+    lines = spread(atoms, table, *z_pair)
     if not relayout:
         lines = lines.reshape(yl, PPC, devices, modes).transpose(2, 1, 0, 3)
         lines = lines.reshape(devices, PPC, yl * modes)
     planes = lax.all_to_all(lines, ("gx", "gy", "gz"), split_axis=0, concat_axis=0, tiled=True)
 
-    ext = padded(
-        jnp.concatenate([positions, kind], axis=3), (("gz", 2), ("gy", 1), ("gx", 0)), 1
-    )
-    density, slope = make_density(cells, slots)(ext, table)
-    slope_ext = padded(slope, (("gz", 2), ("gy", 1), ("gx", 0)), 1)
+    nz = gz * cells_z
+    place = (atoms[:, :, :, 0:3] + 0.5 + atoms[:, :, :, 3:6]) / PPC - 0.5
+    place = jnp.concatenate([place, atoms[:, :, :, 6:7]], axis=3)
+    place = place.transpose(1, 0, 2, 3, 4).reshape(cells_y, nz, 4, slots)
+    near = [part.reshape((cells_y + 2) * nz * 4, slots) for part in halo(place, gx, gy, gz)]
+    density, slope = make_density(cells_y, nz, slots)(*near, table)
+    near_slopes = halo(slope, gx, gy, gz)
 
     width = ly * modes
     lane = lax.broadcasted_iota(jnp.int32, (1, width), 1)
@@ -632,14 +637,12 @@
         lines = lines.reshape(devices, PPC, yl, modes).transpose(2, 1, 0, 3)
         lines = lines.reshape(yl * PPC, lz)
 
-    eam_force = make_force(cells, slots)(ext, slope_ext, table)
-
-    electric = make_sample(gz, cells_y, cells_z, slots, lz, devices, relayout)(
-        lines, atoms, table, *z_pair
-    )
-    electric = lax.all_to_all(electric, "gz", split_axis=0, concat_axis=0, tiled=True)
-    forces = jnp.where(alive[:, :, :, None, :], eam_force + COUPLING * electric, 0.0)
-    return (forces, density)
+    short = make_force(cells_y, nz, slots)(*near, *near_slopes, table)
+    result = make_sample(gz, cells_y, cells_z, slots, lz, devices, relayout)(
+        lines, atoms, short, density, table, *z_pair
+    )
+    result = lax.all_to_all(result, "gz", split_axis=0, concat_axis=0, tiled=True)
+    return (result[:, :, :, 0:3], result[:, :, :, 3])
 
 
 def solution(mesh):

time: 169 us -> 143 us (0.85)
  Pallas kernels: 101 us -> 66.8 us
  blocking collectives: 0 us -> 11.8 us
  starting transfers between devices: 35.3 us -> 27 us
  other arithmetic: 5.3 us -> 2.04 us
  waiting for transfers between devices: 20.1 us -> 23.2 us
  local copies, waits for them, and re-layouts: 6.26 us -> 9.35 us
    pallas_call x3, Pallas kernels: 89.9 us -> 56.1 us  [the longest x1 34.4 us: on_device(): short = make_force(cells_y, nz, slots)(*near, *near_slopes, table)]
    all_to_all x1, waiting for transfers between devices: 0.01 us -> 12.5 us  [on_device(): lax.all_to_all(lines, ('gx', 'gy', 'gz'), split_axis=0, concat_axis=0, ti...]
    all_to_all x0 -> x1, blocking collectives: none -> 11.8 us  [on_device(): lax.all_to_all(result, 'gz', split_axis=0, concat_axis=0, tiled=True)]
    ppermute x12 -> x6, waiting for transfers between devices: 18.8 us -> 8.43 us  [the longest x4 5.42 us: shifted(): lax.ppermute(part, axis, up)]
    ppermute x12 -> x6, starting transfers between devices: 17.4 us -> 13 us  [the longest x2 7.56 us: shifted(): lax.ppermute(part, axis, down)]
    all_to_all x1 -> x0, starting transfers between devices: 4.13 us -> none  [on_device(): lax.all_to_all(electric, 'gz', split_axis=0, concat_axis=0, tiled=True)]
    unnamed x23 -> x32, local copies, waits for them, and re-layouts: 4.16 us -> 5.93 us
  transfers between devices with their start and end apart: 16 -> 9, of which waited for: 10 -> 7; matrix products, arithmetic and copies ran while one was open for 2% -> 3% of each run, Pallas kernels for 53% -> 38%
where the time goes in v2:
time: 143 us; the launch traced here: 141 us
  Pallas kernels  66.8 us (47%)
  starting transfers between devices  27 us (19%)
  waiting for transfers between devices  23.2 us (16%)
  blocking collectives  11.8 us (8%)
  local copies, waits for them, and re-layouts  9.35 us (7%)
  other arithmetic  2.04 us (1%)
    pallas_call x1, Pallas kernels, on_device(): short = make_force(cells_y, nz, slots)(*near, *near_slopes, table)  34.4 us
    pallas_call x1, Pallas kernels, on_device(): density, slope = make_density(cells_y, nz, slots)(*near, table)  15.1 us
    all_to_all x1, waiting for transfers between devices, on_device(): lax.all_to_all(lines, ('gx', 'gy', 'gz'), split_axis=0, concat_axis=0, ti...  12.5 us
    all_to_all x1, blocking collectives, on_device(): lax.all_to_all(result, 'gz', split_axis=0, concat_axis=0, tiled=True)  11.8 us
    ppermute x2, starting transfers between devices, shifted(): lax.ppermute(part, axis, down)  7.56 us
    pallas_call x1, Pallas kernels, on_device(): lines = spread(atoms, table, *z_pair)  6.69 us
    pallas_call x1, Pallas kernels, on_device(): make_sample(gz, cells_y, cells_z, slots, lz, devices, relayout)  6.41 us
    all_to_all x1, starting transfers between devices, on_device(): lax.all_to_all(lines, ('gx', 'gy', 'gz'), split_axis=0, concat_axis=0, ti...  6.24 us
  transfers between devices with their start and end apart: 9, of which 7 were waited for; matrix products, arithmetic and copies ran while one was open for 3% of the time, Pallas kernels for 38%

profile of v2, /device:TPU:1, one launch (start us, length us, event | category | flops | bytes accessed | tf_op | source)
XLA Modules:
  0.0 141.1 jit_solution(8696786663138421366)
XLA Ops:
  0.6 0.0 copy-start.4
  0.6 0.8 copy.54
  1.5 0.0 copy-done.4
  1.5 0.0 copy-start.6
  1.5 0.0 copy-start.8
  1.6 0.7 copy-done.6
  2.2 0.0 copy-done.8
  2.2 0.1 convert_select_fusion
  2.3 0.7 pad_maximum_fusion
  3.0 0.0 copy-start.9
  3.0 0.0 copy-start.10
  3.0 4.4 %all-to-all-start = ((f32[4,2,4,8,128]{4,3,2,1,0:T(8,128)}), f32[4,2,4,8,128]{4,3,2,1,0:T(8,128)S(1)}, u32[]{:S(2)}, u32[]{:S(2)}) async-start(f32[4,2,4,8,128]{4,3,2,1,0:T(8,128)} %pad_maximum_fusion), calls=%async_computation | async-start | bytes 262144 | tf_op jit(solution)/shard_map/all_to_all | solution.py:602
  7.4 0.0 copy-done.9
  7.4 0.0 copy-done.10
  7.4 0.0 copy-start.11
  7.4 0.0 copy-start.12
  7.4 0.6 copy-done.11
  8.1 0.0 copy-done.12
  8.1 0.6 stack.31.table
  8.7 2.3 %all-to-all-done.atoms = f32[4,2,4,8,128]{4,3,2,1,0:T(8,128)S(1)} async-done(((f32[4,2,4,8,128]{4,3,2,1,0:T(8,128)}), f32[4,2,4,8,128]{4,3,2,1,0:T(8,128)S(1)}, u32[]{:S(2)}, u32[]{:S(2)}) %all-to-all-start) | async-done | bytes 131104 | tf_op jit(solution)/shard_map/all_to_all | solution.py:602
  11.0 0.0 copy-start
  11.0 0.7 copy-done
  11.6 6.7 %spread.1 = f32[32,16,256]{2,1,0:T(8,128)} custom-call(f32[4,2,4,8,128]{4,3,2,1,0:T(8,128)} %copy-done, f32[7,2]{1,0:T(8,128)} %stack.31.table, bf16[256,256]{1,0:T(8,128)(2,1)} %constant.102.clone.basis_hi.x_hi, bf16[256,256]{1,0:T(8,128)(2,1)} %constant.103.clone.basis_lo.x_lo), custom_call_target="tpu_custom_call" | custom-call | tf_op jit(solution)/shard_map/spread/pallas_call | solution.py:607
  18.3 0.0 copy-start.1
  18.3 6.2 %all-to-all-start.1 = ((f32[32,16,256]{2,1,0:T(8,128)}), f32[32,16,256]{2,1,0:T(8,128)S(1)}, u32[]{:S(2)}, u32[]{:S(2)}) async-start(f32[32,16,256]{2,1,0:T(8,128)} %spread.1), calls=%async_computation.1 | async-start | bytes 1048576 | tf_op jit(solution)/shard_map/all_to_all | solution.py:611
  24.6 0.0 copy-done.1
  24.8 1.4 %collective-permute-start = (f32[2,16,4,128]{3,1,2,0:T(8,128)S(1)}, f32[2,16,4,128]{3,1,2,0:T(8,128)S(1)}, u32[]{:S(2)}, u32[]{:S(2)}) collective-permute-start(f32[2,16,4,128]{3,1,2,0:T(8,128)S(1)} %bitcast.20), channel_id=1, source_target_pairs={{0,4},{4,0},{1,5},{5,1},{2,6},{6,2},{3,7},{7,3},{8,12},{12,8},{9,1... | collective-permute-start | bytes 196616 | tf_op jit(solution)/shard_map/ppermute | solution.py:548
  26.2 1.1 divide_select_fusion.green
  27.3 12.5 %all-to-all-done.1.data = f32[32,16,256]{2,1,0:T(8,128)S(1)} async-done(((f32[32,16,256]{2,1,0:T(8,128)}), f32[32,16,256]{2,1,0:T(8,128)S(1)}, u32[]{:S(2)}, u32[]{:S(2)}) %all-to-all-start.1) | async-done | bytes 524320 | tf_op jit(solution)/shard_map/all_to_all | solution.py:611
  39.8 0.0 copy-start.3
  39.8 0.8 copy-done.3
  40.6 4.2 %planes.1 = f32[32,16,256]{2,1,0:T(8,128)} custom-call(f32[32,16,256]{2,1,0:T(8,128)} %copy-done.3, bf16[256,256]{1,0:T(8,128)(2,1)} %constant.102.clone.basis_hi.x_hi, bf16[256,256]{1,0:T(8,128)(2,1)} %constant.103.clone.basis_lo.x_lo, bf16[256,256]{1,0:T(8,128)(2,1)} %constant.104.clone.xt_hi, bf16[256,256]{1,0:T(8,128)(2,1)} %constant.105.clone.xt_lo, ...), custom_call_target="tpu_custom_call" | custom-call | tf_op jit(solution)/shard_map/planes/pallas_call | solution.py:632
  44.9 3.4 %all-to-all-start.2 = ((f32[32,16,256]{2,1,0:T(8,128)}), f32[32,16,256]{2,1,0:T(8,128)S(1)}, u32[]{:S(2)}, u32[]{:S(2)}) async-start(f32[32,16,256]{2,1,0:T(8,128)} %planes.1), calls=%async_computation.2 | async-start | bytes 1048576 | tf_op jit(solution)/shard_map/all_to_all | solution.py:635
  48.2 0.0 collective-permute-done
  48.3 1.7 %collective-permute-start.1 = (f32[4,16,4,128]{3,1,2,0:T(8,128)S(1)}, f32[4,16,4,128]{3,1,2,0:T(8,128)S(1)}, u32[]{:S(2)}, u32[]{:S(2)}) collective-permute-start(f32[4,16,4,128]{3,1,2,0:T(8,128)S(1)} %pad_maximum_fusion.1), channel_id=1, source_target_pairs={{0,1},{1,2},{2,3},{3,8},{8,9},{9,10},{10,11},{11,16},{16,17},{17,1... | collective-permute-start | bytes 393224 | tf_op jit(solution)/shard_map/ppermute | solution.py:548
  50.0 0.0 collective-permute-start.2
  50.0 0.7 copy.57
  50.7 3.1 %collective-permute-done.1 = f32[4,16,4,128]{3,1,2,0:T(8,128)S(1)} collective-permute-done((f32[4,16,4,128]{3,1,2,0:T(8,128)S(1)}, f32[4,16,4,128]{3,1,2,0:T(8,128)S(1)}, u32[]{:S(2)}, u32[]{:S(2)}) %collective-permute-start.1) | collective-permute-done | bytes 131104 | tf_op jit(solution)/shard_map/ppermute | solution.py:548
  53.7 0.7 copy.56
  54.4 2.6 %collective-permute-done.2 = f32[4,16,4,128]{3,1,2,0:T(8,128)S(1)} collective-permute-done((f32[4,16,4,128]{3,1,2,0:T(8,128)S(1)}, f32[4,16,4,128]{3,1,2,0:T(8,128)S(1)}, u32[]{:S(2)}, u32[]{:S(2)}) %collective-permute-start.2) | collective-permute-done | bytes 131104 | tf_op jit(solution)/shard_map/ppermute | solution.py:548
  57.0 0.7 copy.58
  57.8 15.1 %density.1 = (f32[2,16,128]{2,1,0:T(8,128)}, f32[2,16,128]{2,1,0:T(8,128)}) custom-call(f32[256,128]{1,0:T(8,128)} %bitcast.24, f32[256,128]{1,0:T(8,128)} %bitcast.22, f32[256,128]{1,0:T(8,128)} %bitcast.26, f32[7,2]{1,0:T(8,128)} %stack.31.table), custom_call_target="tpu_custom_call" | custom-call | flops 566231040 | bytes 393216 | tf_op jit(solution)/shard_map/density/pallas_call | solution.py:618
  72.8 0.0 copy-start.7
  72.8 0.9 collective-permute-start.3
  73.7 1.9 %collective-permute-done.3 = f32[2,16,128]{2,1,0:T(8,128)S(1)} collective-permute-done((f32[2,16,128]{2,1,0:T(8,128)}, f32[2,16,128]{2,1,0:T(8,128)S(1)}, u32[]{:S(2)}, u32[]{:S(2)}) %collective-permute-start.3) | collective-permute-done | bytes 16416 | tf_op jit(solution)/shard_map/ppermute | solution.py:548
  75.6 0.0 copy-done.7
  75.6 0.0 copy-start.5
  75.6 1.5 %collective-permute-start.4 = (f32[4,16,128]{2,1,0:T(8,128)S(1)}, f32[4,16,128]{2,1,0:T(8,128)S(1)}, u32[]{:S(2)}, u32[]{:S(2)}) collective-permute-start(f32[4,16,128]{2,1,0:T(8,128)S(1)} %pad_maximum_fusion.2.slope_mid), channel_id=1, source_target_pairs={{0,1},{1,2},{2,3},{3,8},{8,9},{9,10},{10,11},{11,16},{16,17},{17,1... | collective-permute-start | bytes 98312 | tf_op jit(solution)/shard_map/ppermute | solution.py:548
  77.1 7.6 %collective-permute-start.5 = (f32[4,16,128]{2,1,0:T(8,128)S(1)}, f32[4,16,128]{2,1,0:T(8,128)S(1)}, u32[]{:S(2)}, u32[]{:S(2)}) collective-permute-start(f32[4,16,128]{2,1,0:T(8,128)S(1)} %pad_maximum_fusion.2.slope_mid), channel_id=1, source_target_pairs={{1,0},{2,1},{3,2},{8,3},{9,8},{10,9},{11,10},{16,11},{17,16},{18,1... | collective-permute-start | bytes 98312 | tf_op jit(solution)/shard_map/ppermute | solution.py:548
  84.7 0.5 collective-permute-done.4.slope_low
  85.1 0.0 copy-start.13
  85.1 0.4 collective-permute-done.5.slope_high
  85.5 0.0 copy-done.5
  85.5 0.2 copy-done.13
  85.7 0.0 copy-start.14
  85.7 0.6 copy-done.14
  86.4 34.4 %force.1.short = f32[3,2,16,128]{3,2,1,0:T(8,128)} custom-call(f32[256,128]{1,0:T(8,128)} %bitcast.25, f32[256,128]{1,0:T(8,128)} %bitcast.23, f32[256,128]{1,0:T(8,128)} %bitcast.27, f32[4,16,128]{2,1,0:T(8,128)} %copy-done.13, f32[4,16,128]{2,1,0:T(8,128)} %copy-done.5, f32[4,16,128]{2,1,0:T(8,128)} %copy-done.14, f32[7,2]{1,0:T(8,128)} %stack.31.table), custom_call_target="tpu_custom_call" | custom-call | flops 1415577600 | bytes 393216 | tf_op jit(solution)/shard_map/force/pallas_call | solution.py:640
  120.7 0.0 all-to-all-done.2.data
  120.7 0.0 copy-start.2
  120.7 0.8 copy-done.2
  121.5 6.4 %sample.1 = f32[4,2,4,4,128]{4,3,2,1,0:T(4,128)} custom-call(f32[32,16,256]{2,1,0:T(8,128)} %copy-done.2, f32[4,2,4,8,128]{4,3,2,1,0:T(8,128)} %copy-done, f32[3,2,16,128]{3,2,1,0:T(8,128)} %force.1.short, f32[2,16,128]{2,1,0:T(8,128)} %get-tuple-element.5.dens, f32[7,2]{1,0:T(8,128)} %stack.31.table, bf16[256,256]{1,0:T(8,128)(2,1)} %constant.102.clone.basis_hi.x_hi, ...), custom_call_target="tpu_custom_call" | custom-call | tf_op jit(solution)/shard_map/sample/pallas_call | solution.py:641
  128.0 11.8 %all_to_all.20 = f32[4,2,4,4,128]{4,3,2,1,0:T(4,128)S(1)} all-to-all(f32[4,2,4,4,128]{4,3,2,1,0:T(4,128)} %sample.1), channel_id=1, replica_groups=mesh['gx'=4,'gy'=2,'gz'=4] {'gz'}, dimensions={0} | all-to-all | bytes 131072 | tf_op jit(solution)/shard_map/all_to_all | solution.py:644
  139.8 0.6 copy.59
  140.4 0.6 slice.44
  (15 shorter events, 0.2 us)
Async XLA Ops:
  0.6 0.8 copy-start.4
  1.5 0.7 copy-start.6
  1.5 0.7 copy-start.8
  3.0 4.4 %copy-start.9 = (f32[2]{0:T(128)S(1)}, f32[2]{0:T(128)}, u32[]{:S(2)}) copy-start(f32[2]{0:T(128)} %param.20) | copy-start | bytes 28
  3.0 4.4 %copy-start.10 = (f32[2]{0:T(128)S(1)}, f32[2]{0:T(128)}, u32[]{:S(2)}) copy-start(f32[2]{0:T(128)} %param.21) | copy-start | bytes 28
  3.0 7.9 %all-to-all-start = ((f32[4,2,4,8,128]{4,3,2,1,0:T(8,128)}), f32[4,2,4,8,128]{4,3,2,1,0:T(8,128)S(1)}, u32[]{:S(2)}, u32[]{:S(2)}) async-start(f32[4,2,4,8,128]{4,3,2,1,0:T(8,128)} %pad_maximum_fusion), calls=%async_computation | async-start | bytes 262144 | tf_op jit(solution)/shard_map/all_to_all | solution.py:602
  7.4 0.7 copy-start.11
  7.4 0.7 copy-start.12
  11.0 0.7 copy-start
  18.3 6.3 %copy-start.1 = (f32[4,2,4,8,128]{4,3,2,1,0:T(8,128)S(1)}, f32[4,2,4,8,128]{4,3,2,1,0:T(8,128)}, u32[]{:S(2)}) copy-start(f32[4,2,4,8,128]{4,3,2,1,0:T(8,128)} %copy-done) | copy-start | bytes 393220
  18.3 21.5 %all-to-all-start.1 = ((f32[32,16,256]{2,1,0:T(8,128)}), f32[32,16,256]{2,1,0:T(8,128)S(1)}, u32[]{:S(2)}, u32[]{:S(2)}) async-start(f32[32,16,256]{2,1,0:T(8,128)} %spread.1), calls=%async_computation.1 | async-start | bytes 1048576 | tf_op jit(solution)/shard_map/all_to_all | solution.py:611
  24.8 23.5 %collective-permute-start = (f32[2,16,4,128]{3,1,2,0:T(8,128)S(1)}, f32[2,16,4,128]{3,1,2,0:T(8,128)S(1)}, u32[]{:S(2)}, u32[]{:S(2)}) collective-permute-start(f32[2,16,4,128]{3,1,2,0:T(8,128)S(1)} %bitcast.20), channel_id=1, source_target_pairs={{0,4},{4,0},{1,5},{5,1},{2,6},{6,2},{3,7},{7,3},{8,12},{12,8},{9,1... | collective-permute-start | bytes 196616 | tf_op jit(solution)/shard_map/ppermute | solution.py:548
  39.8 0.8 copy-start.3
  44.9 75.9 %all-to-all-start.2 = ((f32[32,16,256]{2,1,0:T(8,128)}), f32[32,16,256]{2,1,0:T(8,128)S(1)}, u32[]{:S(2)}, u32[]{:S(2)}) async-start(f32[32,16,256]{2,1,0:T(8,128)} %planes.1), calls=%async_computation.2 | async-start | bytes 1048576 | tf_op jit(solution)/shard_map/all_to_all | solution.py:635
  48.3 5.5 %collective-permute-start.1 = (f32[4,16,4,128]{3,1,2,0:T(8,128)S(1)}, f32[4,16,4,128]{3,1,2,0:T(8,128)S(1)}, u32[]{:S(2)}, u32[]{:S(2)}) collective-permute-start(f32[4,16,4,128]{3,1,2,0:T(8,128)S(1)} %pad_maximum_fusion.1), channel_id=1, source_target_pairs={{0,1},{1,2},{2,3},{3,8},{8,9},{9,10},{10,11},{11,16},{16,17},{17,1... | collective-permute-start | bytes 393224 | tf_op jit(solution)/shard_map/ppermute | solution.py:548
  50.0 7.1 %collective-permute-start.2 = (f32[4,16,4,128]{3,1,2,0:T(8,128)S(1)}, f32[4,16,4,128]{3,1,2,0:T(8,128)S(1)}, u32[]{:S(2)}, u32[]{:S(2)}) collective-permute-start(f32[4,16,4,128]{3,1,2,0:T(8,128)S(1)} %pad_maximum_fusion.1), channel_id=1, source_target_pairs={{1,0},{2,1},{3,2},{8,3},{9,8},{10,9},{11,10},{16,11},{17,16},{18,1... | collective-permute-start | bytes 393224 | tf_op jit(solution)/shard_map/ppermute | solution.py:548
  72.8 2.8 %copy-start.7 = (f32[2,16,128]{2,1,0:T(8,128)S(1)}, f32[2,16,128]{2,1,0:T(8,128)}, u32[]{:S(2)}) copy-start(f32[2,16,128]{2,1,0:T(8,128)} %get-tuple-element.4) | copy-start | bytes 49156
  72.8 2.8 %collective-permute-start.3 = (f32[2,16,128]{2,1,0:T(8,128)}, f32[2,16,128]{2,1,0:T(8,128)S(1)}, u32[]{:S(2)}, u32[]{:S(2)}) collective-permute-start(f32[2,16,128]{2,1,0:T(8,128)} %get-tuple-element.4), channel_id=1, source_target_pairs={{0,4},{4,0},{1,5},{5,1},{2,6},{6,2},{3,7},{7,3},{8,12},{12,8},{9,1... | collective-permute-start | bytes 49160 | tf_op jit(solution)/shard_map/ppermute | solution.py:548
  75.6 9.9 %copy-start.5 = (f32[4,16,128]{2,1,0:T(8,128)}, f32[4,16,128]{2,1,0:T(8,128)S(1)}, u32[]{:S(2)}) copy-start(f32[4,16,128]{2,1,0:T(8,128)S(1)} %pad_maximum_fusion.2.slope_mid) | copy-start | bytes 98308
  75.6 9.5 %collective-permute-start.4 = (f32[4,16,128]{2,1,0:T(8,128)S(1)}, f32[4,16,128]{2,1,0:T(8,128)S(1)}, u32[]{:S(2)}, u32[]{:S(2)}) collective-permute-start(f32[4,16,128]{2,1,0:T(8,128)S(1)} %pad_maximum_fusion.2.slope_mid), channel_id=1, source_target_pairs={{0,1},{1,2},{2,3},{3,8},{8,9},{9,10},{10,11},{11,16},{16,17},{17,1... | collective-permute-start | bytes 98312 | tf_op jit(solution)/shard_map/ppermute | solution.py:548
  77.1 8.4 %collective-permute-start.5 = (f32[4,16,128]{2,1,0:T(8,128)S(1)}, f32[4,16,128]{2,1,0:T(8,128)S(1)}, u32[]{:S(2)}, u32[]{:S(2)}) collective-permute-start(f32[4,16,128]{2,1,0:T(8,128)S(1)} %pad_maximum_fusion.2.slope_mid), channel_id=1, source_target_pairs={{1,0},{2,1},{3,2},{8,3},{9,8},{10,9},{11,10},{16,11},{17,16},{18,1... | collective-permute-start | bytes 98312 | tf_op jit(solution)/shard_map/ppermute | solution.py:548
  85.1 0.6 copy-start.13
  85.7 0.6 copy-start.14
  120.7 0.8 copy-start.2

commit v3 on v2

--- a/solution.py
+++ b/solution.py
@@ -19,9 +19,14 @@
 BF16 = jnp.bfloat16
 VMEM = pl.BlockSpec(memory_space=pltpu.VMEM)
 SMEM = pl.BlockSpec(memory_space=pltpu.SMEM)
+ANY = pl.BlockSpec(memory_space=pl.ANY)
 NN = (((1,), (0,)), ((), ()))
 NT = (((1,), (1,)), ((), ()))
 PARAMS = pltpu.CompilerParams(vmem_limit_bytes=56 * 1024 * 1024)
+
+
+def near_core(values):
+    return pltpu.with_memory_space_constraint(values, pltpu.VMEM)
 
 
 def split2(values):
@@ -46,10 +51,10 @@
     )
 
 
-def by_kind(kind, table, column):
-    result = jnp.zeros(kind.shape, F32)
+def by_kind(kind, table, empty=0.0):
+    result = jnp.full(kind.shape, empty, F32)
     for kind_index in range(NSPEC):
-        result = jnp.where(kind == float(kind_index), table[column, kind_index], result)
+        result = jnp.where(kind == float(kind_index), table[kind_index], result)
     return result
 
 
@@ -69,25 +74,11 @@
     values = values.astype(np.float32)
     high = values.astype(ml_dtypes.bfloat16)
     low = (values - high.astype(np.float32)).astype(ml_dtypes.bfloat16)
-    return jnp.asarray(high), jnp.asarray(low)
+    return jnp.asarray(np.stack([high, low]))
 
 
 def signed_modes(indices, total):
     return jnp.where(2 * indices >= total, indices - total, indices)
-
-
-def green_factor(modes_x, modes_y, modes_z, length_x, length_y, length_z):
-    wave_x = modes_x.astype(F32) * (2.0 * math.pi / length_x)
-    wave_y = modes_y.astype(F32) * (2.0 * math.pi / length_y)
-    wave_z = modes_z.astype(F32) * (2.0 * math.pi / length_z)
-    squared = wave_x * wave_x + wave_y * wave_y + wave_z * wave_z
-    anchor = (modes_x == 0) & (modes_y == 0) & (modes_z == 0)
-    safe_square = jnp.where(anchor, 1.0, squared)
-    return jnp.where(
-        anchor,
-        0.0,
-        4.0 * math.pi * jnp.exp(-squared / (4.0 * EWALD_SPLIT * EWALD_SPLIT)) / safe_square,
-    )
 
 
 def chunk_transpose(tiles, chunk):
@@ -123,41 +114,58 @@
     yl = cells_y * PPC
     rows = PPC * PPC
 
-    def kernel(atoms, table, basis_hi, basis_lo, out, plane_hi, plane_lo, line_hi, line_lo):
+    tiles = lz // 128
+    reach = columns // tiles
+
+    def kernel(atoms, table, basis_any, out, plane, line_hi, line_lo, basis_ref, sem):
+        fetch = pltpu.make_async_copy(basis_any, basis_ref, sem)
+        fetch.start()
         line_hi[...] = jnp.zeros(line_hi.shape, BF16)
         line_lo[...] = jnp.zeros(line_lo.shape, BF16)
-        basis = (basis_hi[...], basis_lo[...])
         pieces = []
         for cy in range(cells_y):
-            for column in range(columns):
-                cell = atoms[column // cells_z, cy, column % cells_z]
-                weights = [point_weights(cell[d : d + 1], cell[3 + d : 4 + d])[0] for d in range(3)]
-                along_x = weights[0] * by_kind(cell[6:7], table, 3)
-                plane = jnp.concatenate(
-                    [weights[1][y : y + 1] * along_x for y in range(PPC)], axis=0
+            brick = []
+            for tile in range(tiles):
+                for place in range(reach):
+                    column = tile * reach + place
+                    cell = atoms[column // cells_z, cy, :, column % cells_z, :]
+                    weights = [
+                        point_weights(cell[d : d + 1], cell[3 + d : 4 + d])[0] for d in range(3)
+                    ]
+                    along_x = weights[0] * by_kind(cell[6:7], table)
+                    value = jnp.concatenate(
+                        [weights[1][y : y + 1] * along_x for y in range(PPC)], axis=0
+                    )
+                    lanes = pl.ds(place * slots, slots)
+                    points = pl.ds(place * PPC, PPC)
+                    high, low = split2(value)
+                    plane[tile, pl.ds(0, rows), lanes] = high
+                    plane[tile, pl.ds(rows, rows), lanes] = low
+                    high, low = split2(weights[2])
+                    line_hi[tile, points, lanes] = high
+                    line_lo[tile, points, lanes] = low
+                wide = dot(plane[tile], line_hi[tile], NT)
+                brick.append(
+                    wide[:rows] + wide[rows:] + dot(plane[tile, pl.ds(0, rows), :], line_lo[tile], NT)
                 )
-                lanes = pl.ds(column * slots, slots)
-                points = pl.ds(column * PPC, PPC)
-                plane_hi[:, lanes], plane_lo[:, lanes] = split2(plane)
-                line_hi[points, lanes], line_lo[points, lanes] = split2(weights[2])
-            brick = dot3(
-                (plane_hi[...], plane_lo[...]), (line_hi[...], line_lo[...]), NT
-            )
-            pieces.append(dot3(split2(brick), basis, NT))
+            if cy == 0:
+                fetch.wait()
+            brick = jnp.concatenate(brick, axis=1)
+            pieces.append(dot3(split2(brick), (basis_ref[0], basis_ref[1]), NT))
         if not relayout:
             for cy in range(cells_y):
                 out[pl.ds(cy * rows, rows), :] = pieces[cy]
             return
         chunks = 128 // modes
-        for tile in range(lz // 128):
+        for tile in range(tiles):
             for group in range(yl // chunks):
-                tiles = []
+                parts = []
                 for y in range(group * chunks, (group + 1) * chunks):
                     start = (y % PPC) * PPC
-                    tiles.append(
+                    parts.append(
                         pieces[y // PPC][start : start + PPC, tile * 128 : tile * 128 + 128]
                     )
-                for chunk, value in enumerate(chunk_transpose(tiles, modes)):
+                for chunk, value in enumerate(chunk_transpose(parts, modes)):
                     out[tile * chunks + chunk, :, pl.ds(group * 128, 128)] = value
 
     if relayout:
@@ -166,33 +174,57 @@
         shape = (cells_y * rows, lz)
     return pl.pallas_call(
         kernel,
-        out_shape=jax.ShapeDtypeStruct(shape, F32),
-        in_specs=[VMEM, SMEM, VMEM, VMEM],
+        out_shape=pltpu.VMEM(shape, F32),
+        in_specs=[VMEM, SMEM, ANY],
         out_specs=VMEM,
         scratch_shapes=[
-            pltpu.VMEM((rows, columns * slots), BF16),
-            pltpu.VMEM((rows, columns * slots), BF16),
-            pltpu.VMEM((lz, columns * slots), BF16),
-            pltpu.VMEM((lz, columns * slots), BF16),
+            pltpu.VMEM((tiles, 2 * rows, reach * slots), BF16),
+            pltpu.VMEM((tiles, 128, reach * slots), BF16),
+            pltpu.VMEM((tiles, 128, reach * slots), BF16),
+            pltpu.VMEM((2, lz, lz), BF16),
+            pltpu.SemaphoreType.DMA(()),
         ],
         compiler_params=PARAMS,
         name="spread",
     )
 
 
-def make_planes(gx, gy, gz, lanes, lx, width):
-    def kernel(data, x_hi, x_lo, xt_hi, xt_lo, y_hi, y_lo, green, out, grid):
+def make_planes(gx, gy, gz, lanes, lx, ly, lz):
+    modes = lz // (gx * gy * gz)
+    width = ly * modes
+    sharp = -1.0 / (4.0 * EWALD_SPLIT * EWALD_SPLIT)
+
+    def wave_square(indices, length):
+        return jnp.square(signed_modes(indices, length).astype(F32) * (2.0 * math.pi / length))
+
+    def kernel(rank, data, x_any, xt_any, y_any, out, grid, x_ref, xt_ref, y_ref, sems):
+        fetches = [
+            pltpu.make_async_copy(source, target, sems.at[index])
+            for index, (source, target) in enumerate(
+                ((x_any, x_ref), (y_any, y_ref), (xt_any, xt_ref))
+            )
+        ]
+        for fetch in fetches:
+            fetch.start()
         for a in range(gx):
             for b in range(gy):
                 for c in range(gz):
                     grid[pl.ds((a * gz + c) * PPC, PPC), pl.ds(b * lanes, lanes)] = data[
                         (a * gy + b) * gz + c
                     ]
-        along_y = (y_hi[...], y_lo[...])
-        value = dot3((x_hi[...], x_lo[...]), split2(grid[...]), NN)
-        value = dot3(split2(value), along_y, NT) * green[...]
-        value = dot3(split2(value), along_y, NN)
-        value = dot3((xt_hi[...], xt_lo[...]), split2(value), NN)
+        lane = lax.broadcasted_iota(jnp.int32, (1, width), 1)
+        across = wave_square(lane // modes, ly) + wave_square(rank[0] * modes + lane % modes, lz)
+        along = wave_square(lax.broadcasted_iota(jnp.int32, (lx, 1), 0), lx)
+        squared = along + across
+        factor = (4.0 * math.pi * jnp.exp(along * sharp)) * jnp.exp(across * sharp)
+        green = jnp.where(squared == 0.0, 0.0, factor / jnp.where(squared == 0.0, 1.0, squared))
+        fetches[0].wait()
+        value = dot3((x_ref[0], x_ref[1]), split2(grid[...]), NN)
+        fetches[1].wait()
+        value = dot3(split2(value), (y_ref[0], y_ref[1]), NT) * green
+        value = dot3(split2(value), (y_ref[0], y_ref[1]), NN)
+        fetches[2].wait()
+        value = dot3((xt_ref[0], xt_ref[1]), split2(value), NN)
         for a in range(gx):
             for b in range(gy):
                 for c in range(gz):
@@ -203,10 +235,16 @@
 
     return pl.pallas_call(
         kernel,
-        out_shape=jax.ShapeDtypeStruct((gx * gy * gz, PPC, lanes), F32),
-        in_specs=[VMEM] * 8,
+        out_shape=pltpu.VMEM((gx * gy * gz, PPC, lanes), F32),
+        in_specs=[SMEM, VMEM, ANY, ANY, ANY],
         out_specs=VMEM,
-        scratch_shapes=[pltpu.VMEM((lx, width), F32)],
+        scratch_shapes=[
+            pltpu.VMEM((lx, width), F32),
+            pltpu.VMEM((2, lx, lx), BF16),
+            pltpu.VMEM((2, lx, lx), BF16),
+            pltpu.VMEM((2, width, width), BF16),
+            pltpu.SemaphoreType.DMA((3,)),
+        ],
         compiler_params=PARAMS,
         name="planes",
     )
@@ -218,9 +256,13 @@
     yl = cells_y * PPC
     rows = PPC * PPC
 
+    reach = columns * 128 // lz
+
     def kernel(
-        data, atoms, short, dens, table, basis_hi, basis_lo, out, lines, line_hi, line_lo
+        data, atoms, short, dens, table, basis_any, out, lines, line, basis_ref, sem
     ):
+        fetch = pltpu.make_async_copy(basis_any, basis_ref, sem)
+        fetch.start()
         if relayout:
             chunks = 128 // modes
             for tile in range(lz // 128):
@@ -235,23 +277,28 @@
                         ] = value
         else:
             lines[...] = data[...]
-        line_hi[...] = jnp.zeros(line_hi.shape, BF16)
-        line_lo[...] = jnp.zeros(line_lo.shape, BF16)
-        basis = (basis_hi[...], basis_lo[...])
+        line[...] = jnp.zeros(line.shape, BF16)
+        fetch.wait()
         for cy in range(cells_y):
-            brick = split2(dot3(split2(lines[pl.ds(cy * rows, rows), :]), basis, NN))
+            brick = dot3(
+                split2(lines[pl.ds(cy * rows, rows), :]), (basis_ref[0], basis_ref[1]), NN
+            )
             for column in range(columns):
-                cell = atoms[column // cells_z, cy, column % cells_z]
+                if column % reach == 0:
+                    start = column // reach * 128
+                    high, low = split2(brick[:, start : start + 128])
+                    wide = jnp.concatenate([high, low, high], axis=1)
+                cell = atoms[column // cells_z, cy, :, column % cells_z, :]
                 pairs = [point_weights(cell[d : d + 1], cell[3 + d : 4 + d]) for d in range(3)]
                 (wx, sx), (wy, sy), (wz, sz) = pairs
-                points = pl.ds(column * PPC, PPC)
+                first = column % reach * PPC
                 high, low = split2(wz)
-                line_hi[column, points, pl.ds(0, slots)] = high
-                line_hi[column, points, pl.ds(slots, slots)] = sz.astype(BF16)
-                line_lo[column, points, :] = low
-                both = dot(brick[0], line_hi[column], NN) + dot(brick[1], line_hi[column], NN)
-                plain = both[:, :slots] + dot(brick[0], line_lo[column], NN)
-                tilted = both[:, slots:]
+                both = jnp.concatenate([high, sz.astype(BF16)], axis=1)
+                line[column, pl.ds(first, PPC), :] = both
+                line[column, pl.ds(128 + first, PPC), :] = both
+                line[column, pl.ds(256 + first, PPC), pl.ds(0, slots)] = low
+                both = dot(wide, line[column], NN)
+                plain, tilted = both[:, :slots], both[:, slots:]
                 force_x = jnp.zeros((PPC, slots), F32)
                 force_y = jnp.zeros((PPC, slots), F32)
                 force_z = jnp.zeros((PPC, slots), F32)
@@ -260,7 +307,7 @@
                     force_x += wy[y : y + 1] * block
                     force_y += sy[y : y + 1] * block
                     force_z += wy[y : y + 1] * tilted[y * PPC : (y + 1) * PPC]
-                charge = -COUPLING * by_kind(cell[6:7], table, 3)
+                charge = -COUPLING * by_kind(cell[6:7], table)
                 here = pl.ds(column, 1)
                 result = [
                     charge * jnp.sum(force * weight, axis=0, keepdims=True)
@@ -271,17 +318,18 @@
                 ]
                 result = [jnp.where(cell[6:7] >= 0.0, value, 0.0) for value in result]
                 result.append(dens[cy, here, :])
-                out[column // cells_z, cy, column % cells_z] = jnp.concatenate(result, axis=0)
+                out[column // cells_z, cy, :, column % cells_z, :] = jnp.concatenate(result, axis=0)
 
     return pl.pallas_call(
         kernel,
-        out_shape=jax.ShapeDtypeStruct((parts, cells_y, cells_z, 4, slots), F32),
-        in_specs=[VMEM, VMEM, VMEM, VMEM, SMEM, VMEM, VMEM],
+        out_shape=pltpu.VMEM((parts, cells_y, 4, cells_z, slots), F32),
+        in_specs=[VMEM, VMEM, VMEM, VMEM, SMEM, ANY],
         out_specs=VMEM,
         scratch_shapes=[
             pltpu.VMEM((cells_y * rows, lz), F32),
-            pltpu.VMEM((columns, lz, 2 * slots), BF16),
-            pltpu.VMEM((columns, lz, slots), BF16),
+            pltpu.VMEM((columns, 384, 2 * slots), BF16),
+            pltpu.VMEM((2, lz, lz), BF16),
+            pltpu.SemaphoreType.DMA(()),
         ],
         compiler_params=PARAMS,
         name="sample",
@@ -298,7 +346,7 @@
 
 
 def channel(block, y, nz, index):
-    return block[pl.ds(y * nz * 4 + index, nz, stride=4), :]
+    return block[pl.ds((y * 4 + index) * nz, nz), :]
 
 
 def row_positions(block, x, y, sy, nz):
@@ -318,14 +366,18 @@
     own = cells_y * nz
     total = 3 * sy * nz
 
-    def kernel(low, mid, high, table, density, slope, feature, own_feature, right, left, sums):
+    def kernel(
+        low, mid, high, electrons, embed, density, slope, feature, own_feature, right, left, sums
+    ):
         feature[...] = jnp.zeros(feature.shape, F32)
         own_feature[...] = jnp.zeros(own_feature.shape, F32)
         for x, block in enumerate((low, mid, high)):
             for y in range(sy):
                 pos = row_positions(block, x, y, sy, nz)
                 square = pos[0] * pos[0] + pos[1] * pos[1] + pos[2] * pos[2]
-                scale = by_kind(channel(block, y, nz, 3), table, 4)
+                kind = channel(block, y, nz, 3)
+                scale = jnp.exp(jnp.log(by_kind(kind, electrons, 1.0)) * (1.0 / 3.0))
+                scale = jnp.where(kind >= 0.0, scale, 0.0)
                 base = (x * sy + y) * nz * 8
                 feature[pl.ds(base, nz, stride=8), :] = scale * (1.0 - square)
                 for d in range(3):
@@ -377,19 +429,21 @@
             sums[...] = jnp.where(lane == n, column, sums[...])
             return carry
 
-        lax.fori_loop(0, own, one_cell, 0, unroll=2)
+        lax.fori_loop(0, own, one_cell, 0, unroll=4)
         rows = sums[...].T
         for y in range(cells_y):
             kind = channel(mid, y + 1, nz, 3)
             value = jnp.where(kind >= 0.0, rows[y * nz : (y + 1) * nz], 0.0)
             density[y] = value
-            slope[y] = -by_kind(kind, table, 2) / (2.0 * jnp.sqrt(1.0 + value))
-
-    shape = jax.ShapeDtypeStruct((cells_y, nz, slots), F32)
+            slope[pl.ds(y * nz, nz), :] = -by_kind(kind, embed) / (2.0 * jnp.sqrt(1.0 + value))
+
     return pl.pallas_call(
         kernel,
-        out_shape=(shape, shape),
-        in_specs=[VMEM, VMEM, VMEM, SMEM],
+        out_shape=(
+            pltpu.VMEM((cells_y, nz, slots), F32),
+            pltpu.VMEM((own, slots), F32),
+        ),
+        in_specs=[VMEM, VMEM, VMEM, SMEM, SMEM],
         out_specs=(VMEM, VMEM),
         scratch_shapes=[
             pltpu.VMEM((total * 8, slots), F32),
@@ -413,7 +467,7 @@
     chunk = 64
 
     def kernel(
-        low, mid, high, slope_low, slope_mid, slope_high, table, out,
+        low, mid, high, slope_low, slope_mid, slope_high, electrons, repel, out,
         feature, extra, own_feature, own_extra, place, right, right_extra, left, left_extra,
         sums,
     ):
@@ -425,9 +479,11 @@
                 pos = row_positions(block, x, y, sy, nz)
                 square = pos[0] * pos[0] + pos[1] * pos[1] + pos[2] * pos[2]
                 kind = channel(block, y, nz, 3)
-                scale = by_kind(kind, table, 1)
-                steep = slopes[y] * by_kind(kind, table, 5)
-                mild = by_kind(kind, table, 6)
+                scale = by_kind(kind, repel)
+                inverse = 1.0 / by_kind(kind, repel, 1.0)
+                inverse = inverse * inverse
+                steep = slopes[pl.ds(y * nz, nz), :] * inverse
+                mild = -3.0 * by_kind(kind, electrons) * inverse
                 base = (x * sy + y) * nz * 8
                 feature[pl.ds(base, nz, stride=8), :] = scale * (1.0 - square)
                 for d in range(3):
@@ -507,7 +563,7 @@
                     )
             return carry
 
-        lax.fori_loop(0, own, one_cell, 0, unroll=2)
+        lax.fori_loop(0, own, one_cell, 0, unroll=4)
         rows = [sums[d].T for d in range(4)]
         for y in range(cells_y):
             pos = row_positions(mid, 1, y + 1, sy, nz)
@@ -517,8 +573,8 @@
 
     return pl.pallas_call(
         kernel,
-        out_shape=jax.ShapeDtypeStruct((3, cells_y, nz, slots), F32),
-        in_specs=[VMEM] * 6 + [SMEM],
+        out_shape=pltpu.VMEM((3, cells_y, nz, slots), F32),
+        in_specs=[VMEM] * 6 + [SMEM, SMEM],
         out_specs=VMEM,
         scratch_shapes=[
             pltpu.VMEM((total * 8, slots), F32),
@@ -548,13 +604,13 @@
     return lambda part: lax.ppermute(part, axis, up), lambda part: lax.ppermute(part, axis, down)
 
 
-def halo(block, gx, gy, gz):
+def halo(block, rows, gx, gy, gz):
     up, down = shifted("gy", gy)
-    if gy == 2 and block.shape[0] == 2:
+    if gy == 2 and block.shape[0] == 2 * rows:
         other = up(block)
-        low, high = other[-1:], other[:1]
+        low, high = other[-rows:], other[:rows]
     else:
-        low, high = up(block[-1:]), down(block[:1])
+        low, high = up(block[-rows:]), down(block[:rows])
     middle = jnp.concatenate([low, block, high], axis=0)
     up, down = shifted(("gx", "gz"), gx * gz)
     low = up(middle)
@@ -582,67 +638,56 @@
     yl = cells_y * PPC
     relayout = modes <= 128 and yl % max(1, 128 // modes) == 0
 
-    table = jnp.stack(
-        [
-            species_density,
-            species_pair,
-            species_embed,
-            species_charge,
-            jnp.exp(jnp.log(species_density) * (1.0 / 3.0)),
-            1.0 / (species_pair * species_pair),
-            -3.0 * species_density / (species_pair * species_pair),
-        ]
-    )
     slot_index = lax.broadcasted_iota(jnp.int32, species.shape, 3)
     alive = slot_index < cell_counts[..., None]
-    kind = jnp.where(alive, species.astype(F32), -1.0)[:, :, :, None, :]
-    offsets = grid_offset.astype(F32)
-
-    atoms = jnp.concatenate([offsets, fraction, kind, kind], axis=3)
+    kind = jnp.where(alive, species.astype(F32), -1.0)[:, :, None]
+
+    atoms = jnp.concatenate(
+        [
+            grid_offset.astype(F32).transpose(0, 1, 3, 2, 4),
+            fraction.transpose(0, 1, 3, 2, 4),
+            kind,
+        ],
+        axis=2,
+    )
     atoms = lax.all_to_all(atoms, "gz", split_axis=0, concat_axis=0, tiled=True)
     basis_x, basis_z = real_basis(lx), real_basis(lz)
     x_pair, xt_pair, z_pair = table_pair(basis_x), table_pair(basis_x.T), table_pair(basis_z)
     y_pair = table_pair(np.kron(real_basis(ly), np.eye(modes)))
     spread = make_spread(gz, cells_y, cells_z, slots, lz, devices, relayout)
-    lines = spread(atoms, table, *z_pair)
+    lines = spread(near_core(atoms), species_charge, z_pair)
     if not relayout:
         lines = lines.reshape(yl, PPC, devices, modes).transpose(2, 1, 0, 3)
         lines = lines.reshape(devices, PPC, yl * modes)
     planes = lax.all_to_all(lines, ("gx", "gy", "gz"), split_axis=0, concat_axis=0, tiled=True)
 
     nz = gz * cells_z
-    place = (atoms[:, :, :, 0:3] + 0.5 + atoms[:, :, :, 3:6]) / PPC - 0.5
-    place = jnp.concatenate([place, atoms[:, :, :, 6:7]], axis=3)
-    place = place.transpose(1, 0, 2, 3, 4).reshape(cells_y, nz, 4, slots)
-    near = [part.reshape((cells_y + 2) * nz * 4, slots) for part in halo(place, gx, gy, gz)]
-    density, slope = make_density(cells_y, nz, slots)(*near, table)
-    near_slopes = halo(slope, gx, gy, gz)
-
-    width = ly * modes
-    lane = lax.broadcasted_iota(jnp.int32, (1, width), 1)
-    rank = lax.axis_index(("gx", "gy", "gz"))
-    green = green_factor(
-        signed_modes(lax.broadcasted_iota(jnp.int32, (lx, 1), 0), lx),
-        signed_modes(lane // modes, ly),
-        signed_modes(rank * modes + lane % modes, lz),
-        lx,
-        ly,
-        lz,
-    )
-    planes = make_planes(gx, gy, gz, yl * modes, lx, width)(
-        planes, *x_pair, *xt_pair, *y_pair, green
+    place = (atoms[:, :, 0:3] + 0.5 + atoms[:, :, 3:6]) / PPC - 0.5
+    place = jnp.concatenate([place, atoms[:, :, 6:7]], axis=2)
+    place = place.transpose(1, 2, 0, 3, 4).reshape(cells_y * 4 * nz, slots)
+    near = halo(place, nz * 4, gx, gy, gz)
+    density, slope = make_density(cells_y, nz, slots)(
+        *map(near_core, near), species_density, species_embed
+    )
+    near_slopes = halo(slope, nz, gx, gy, gz)
+
+    rank = lax.axis_index(("gx", "gy", "gz")).astype(jnp.int32).reshape(1)
+    planes = make_planes(gx, gy, gz, yl * modes, lx, ly, lz)(
+        rank, near_core(planes), x_pair, xt_pair, y_pair
     )
     lines = lax.all_to_all(planes, ("gx", "gy", "gz"), split_axis=0, concat_axis=0, tiled=True)
     if not relayout:
         lines = lines.reshape(devices, PPC, yl, modes).transpose(2, 1, 0, 3)
         lines = lines.reshape(yl * PPC, lz)
 
-    short = make_force(cells_y, nz, slots)(*near, *near_slopes, table)
+    short = make_force(cells_y, nz, slots)(
+        *map(near_core, near), *map(near_core, near_slopes), species_density, species_pair
+    )
     result = make_sample(gz, cells_y, cells_z, slots, lz, devices, relayout)(
-        lines, atoms, short, density, table, *z_pair
+        near_core(lines), near_core(atoms), near_core(short), near_core(density), species_charge, z_pair
     )
     result = lax.all_to_all(result, "gz", split_axis=0, concat_axis=0, tiled=True)
-    return (result[:, :, :, 0:3], result[:, :, :, 3])
+    return (result[:, :, 0:3].transpose(0, 1, 3, 2, 4), result[:, :, 3])
 
 
 def solution(mesh):

time: 143 us -> 125 us (0.87)
  Pallas kernels: 66.8 us -> 58 us
  local copies, waits for them, and re-layouts: 9.35 us -> 1.27 us
  blocking collectives: 11.8 us -> 18 us
  starting transfers between devices: 27 us -> 21.4 us
    all_to_all x0 -> x1, blocking collectives: none -> 7.48 us  [on_device(): atoms = lax.all_to_all(atoms, 'gz', split_axis=0, concat_axis=0, tiled=True)]
    pallas_call x4, Pallas kernels: 60.4 us -> 52.9 us  [the longest x1 32.2 us: on_device(): make_force(cells_y, nz, slots)]
    unnamed x32 -> x6, local copies, waits for them, and re-layouts: 5.93 us -> 0.01 us
    all_to_all x1 -> x0, starting transfers between devices: 4.38 us -> none  [on_device(): atoms = lax.all_to_all(atoms, 'gz', split_axis=0, concat_axis=0, tiled=True)]
    all_to_all x1 -> x0, waiting for transfers between devices: 2.25 us -> none  [on_device(): atoms = lax.all_to_all(atoms, 'gz', split_axis=0, concat_axis=0, tiled=True)]
  transfers between devices with their start and end apart: 9 -> 8, of which waited for: 7 -> 6; matrix products, arithmetic and copies ran while one was open for 3% -> 0% of each run, Pallas kernels for 38% -> 39%
where the time goes in v3:
time: 125 us; the launch traced here: 124 us
  Pallas kernels  58 us (46%)
  waiting for transfers between devices  23.3 us (19%)
  starting transfers between devices  21.4 us (17%)
  blocking collectives  18 us (14%)
  local copies, waits for them, and re-layouts  1.27 us (1%)
    pallas_call x1, Pallas kernels, on_device(): make_force(cells_y, nz, slots)  32.2 us
    all_to_all x1, waiting for transfers between devices, on_device(): lax.all_to_all(lines, ('gx', 'gy', 'gz'), split_axis=0, concat_axis=0, ti...  13.7 us
    pallas_call x1, Pallas kernels, on_device(): make_density(cells_y, nz, slots)  12.3 us
    all_to_all x1, blocking collectives, on_device(): lax.all_to_all(result, 'gz', split_axis=0, concat_axis=0, tiled=True)  10.6 us
    ppermute x2, starting transfers between devices, shifted(): lax.ppermute(part, axis, down)  7.55 us
    all_to_all x1, blocking collectives, on_device(): atoms = lax.all_to_all(atoms, 'gz', split_axis=0, concat_axis=0, tiled=True)  7.48 us
    ppermute x4, waiting for transfers between devices, shifted(): lax.ppermute(part, axis, up)  5.92 us
    all_to_all x1, starting transfers between devices, on_device(): lax.all_to_all(lines, ('gx', 'gy', 'gz'), split_axis=0, concat_axis=0, ti...  5.67 us
  transfers between devices with their start and end apart: 8, of which 6 were waited for; matrix products, arithmetic and copies ran while one was open for 0% of the time, Pallas kernels for 39%

profile of v3, /device:TPU:1, one launch (start us, length us, event | category | flops | bytes accessed | tf_op | source)
XLA Modules:
  0.0 123.9 jit_solution(17390279266391473838)
XLA Ops:
  0.6 0.0 copy-start.1
  0.6 0.0 copy-start.2
  0.7 0.0 copy-start
  0.7 0.8 convert_bitcast_fusion
  1.5 0.0 copy-done.1
  1.5 0.0 copy-done.2
  1.5 0.1 select_bitcast_fusion
  1.6 0.0 copy-done
  1.6 7.5 %all_to_all.20.atoms = f32[4,2,7,4,128]{4,3,2,1,0:T(4,128)S(1)} all-to-all(f32[4,2,7,4,128]{4,3,2,1,0:T(4,128)S(1)} %pad_maximum_fusion.1), channel_id=1, replica_groups=mesh['gx'=4,'gy'=2,'gz'=4] {'gz'}, dimensions={0} | all-to-all | bytes 229376 | tf_op jit(solution)/shard_map/all_to_all | solution.py:653
  9.1 4.8 %spread.1 = f32[32,16,256]{2,1,0:T(8,128)} custom-call(f32[4,2,7,4,128]{4,3,2,1,0:T(4,128)S(1)} %all_to_all.20.atoms, f32[2]{0:T(128)} %table.3, bf16[2,256,256]{2,1,0:T(8,128)(2,1)} %constant.31.clone.basis_any.x_any), custom_call_target="tpu_custom_call" | custom-call | tf_op jit(solution)/shard_map/spread/pallas_call | solution.py:658
  13.9 5.7 %all-to-all-start.1 = ((f32[32,16,256]{2,1,0:T(8,128)}), f32[32,16,256]{2,1,0:T(8,128)S(1)}, u32[]{:S(2)}, u32[]{:S(2)}) async-start(f32[32,16,256]{2,1,0:T(8,128)} %spread.1), calls=%async_computation.1 | async-start | bytes 1048576 | tf_op jit(solution)/shard_map/all_to_all | solution.py:662
  19.7 1.4 %collective-permute-start = (f32[128,128]{1,0:T(8,128)S(1)}, f32[128,128]{1,0:T(8,128)S(1)}, u32[]{:S(2)}, u32[]{:S(2)}) collective-permute-start(f32[128,128]{1,0:T(8,128)S(1)} %bitcast.13), channel_id=1, source_target_pairs={{0,4},{4,0},{1,5},{5,1},{2,6},{6,2},{3,7},{7,3},{8,12},{12,8},{9,1... | collective-permute-start | bytes 196616 | tf_op jit(solution)/shard_map/ppermute | solution.py:604
  21.1 13.7 %all-to-all-done.1.data = f32[32,16,256]{2,1,0:T(8,128)S(1)} async-done(((f32[32,16,256]{2,1,0:T(8,128)}), f32[32,16,256]{2,1,0:T(8,128)S(1)}, u32[]{:S(2)}, u32[]{:S(2)}) %all-to-all-start.1) | async-done | bytes 524320 | tf_op jit(solution)/shard_map/all_to_all | solution.py:662
  34.8 3.6 %planes.1 = f32[32,16,256]{2,1,0:T(8,128)} custom-call(s32[1]{0:T(128)} %bitcast.rank, f32[32,16,256]{2,1,0:T(8,128)S(1)} %all-to-all-done.1.data, bf16[2,256,256]{2,1,0:T(8,128)(2,1)} %constant.31.clone.basis_any.x_any, bf16[2,256,256]{2,1,0:T(8,128)(2,1)} %constant.32.clone.xt_any, bf16[2,512,512]{2,1,0:T(8,128)(2,1)} %constant.33.clone.y_any), custom_call_target="tpu_custom_call" | custom-call | tf_op jit(solution)/shard_map/planes/pallas_call | solution.py:675
  38.5 3.4 %all-to-all-start.2 = ((f32[32,16,256]{2,1,0:T(8,128)}), f32[32,16,256]{2,1,0:T(8,128)S(1)}, u32[]{:S(2)}, u32[]{:S(2)}) async-start(f32[32,16,256]{2,1,0:T(8,128)} %planes.1), calls=%async_computation.2 | async-start | bytes 1048576 | tf_op jit(solution)/shard_map/all_to_all | solution.py:678
  41.8 0.0 collective-permute-done
  41.9 1.7 %collective-permute-start.1 = (f32[256,128]{1,0:T(8,128)S(1)}, f32[256,128]{1,0:T(8,128)S(1)}, u32[]{:S(2)}, u32[]{:S(2)}) collective-permute-start(f32[256,128]{1,0:T(8,128)S(1)} %pad_maximum_fusion.mid), channel_id=1, source_target_pairs={{0,1},{1,2},{2,3},{3,8},{8,9},{9,10},{10,11},{11,16},{16,17},{17,1... | collective-permute-start | bytes 393224 | tf_op jit(solution)/shard_map/ppermute | solution.py:604
  43.6 0.0 collective-permute-start.2
  43.6 3.8 %collective-permute-done.1.low = f32[256,128]{1,0:T(8,128)S(1)} collective-permute-done((f32[256,128]{1,0:T(8,128)S(1)}, f32[256,128]{1,0:T(8,128)S(1)}, u32[]{:S(2)}, u32[]{:S(2)}) %collective-permute-start.1) | collective-permute-done | bytes 131104 | tf_op jit(solution)/shard_map/ppermute | solution.py:604
  47.3 3.3 %collective-permute-done.2.high = f32[256,128]{1,0:T(8,128)S(1)} collective-permute-done((f32[256,128]{1,0:T(8,128)S(1)}, f32[256,128]{1,0:T(8,128)S(1)}, u32[]{:S(2)}, u32[]{:S(2)}) %collective-permute-start.2) | collective-permute-done | bytes 131104 | tf_op jit(solution)/shard_map/ppermute | solution.py:604
  50.7 12.3 %density.1 = (f32[2,16,128]{2,1,0:T(8,128)S(1)}, f32[32,128]{1,0:T(8,128)S(1)}) custom-call(f32[256,128]{1,0:T(8,128)S(1)} %collective-permute-done.1.low, f32[256,128]{1,0:T(8,128)S(1)} %pad_maximum_fusion.mid, f32[256,128]{1,0:T(8,128)S(1)} %collective-permute-done.2.high, f32[2]{0:T(128)} %electrons.3, f32[2]{0:T(128)} %embed.1), custom_call_target="tpu_custom_call" | custom-call | flops 566231040 | bytes 393216 | tf_op jit(solution)/shard_map/density/pallas_call | solution.py:669
  63.0 1.0 collective-permute-start.3
  64.0 1.7 %collective-permute-done.3 = f32[32,128]{1,0:T(8,128)S(1)} collective-permute-done((f32[32,128]{1,0:T(8,128)S(1)}, f32[32,128]{1,0:T(8,128)S(1)}, u32[]{:S(2)}, u32[]{:S(2)}) %collective-permute-start.3) | collective-permute-done | bytes 16416 | tf_op jit(solution)/shard_map/ppermute | solution.py:604
  65.7 0.7 collective-permute-start.4
  66.4 7.5 %collective-permute-start.5 = (f32[64,128]{1,0:T(8,128)S(1)}, f32[64,128]{1,0:T(8,128)S(1)}, u32[]{:S(2)}, u32[]{:S(2)}) collective-permute-start(f32[64,128]{1,0:T(8,128)S(1)} %pad_maximum_fusion.2.slope_mid), channel_id=1, source_target_pairs={{1,0},{2,1},{3,2},{8,3},{9,8},{10,9},{11,10},{16,11},{17,16},{18,1... | collective-permute-start | bytes 98312 | tf_op jit(solution)/shard_map/ppermute | solution.py:604
  73.9 0.5 collective-permute-done.4.slope_low
  74.4 0.4 collective-permute-done.5.slope_high
  74.8 32.2 %force.1.short = f32[3,2,16,128]{3,2,1,0:T(8,128)S(1)} custom-call(f32[256,128]{1,0:T(8,128)S(1)} %collective-permute-done.1.low, f32[256,128]{1,0:T(8,128)S(1)} %pad_maximum_fusion.mid, f32[256,128]{1,0:T(8,128)S(1)} %collective-permute-done.2.high, f32[64,128]{1,0:T(8,128)S(1)} %collective-permute-done.4.slope_low, ...), custom_call_target="tpu_custom_call" | custom-call | flops 1415577600 | bytes 393216 | tf_op jit(solution)/shard_map/force/pallas_call | solution.py:683
  107.0 0.0 all-to-all-done.2.data
  107.0 5.1 %sample.1 = f32[4,2,4,4,128]{4,3,2,1,0:T(4,128)S(1)} custom-call(f32[32,16,256]{2,1,0:T(8,128)S(1)} %all-to-all-done.2.data, f32[4,2,7,4,128]{4,3,2,1,0:T(4,128)S(1)} %all_to_all.20.atoms, f32[3,2,16,128]{3,2,1,0:T(8,128)S(1)} %force.1.short, f32[2,16,128]{2,1,0:T(8,128)S(1)} %get-tuple-element.5.dens, f32[2]{0:T(128)} %table.3, ...), custom_call_target="tpu_custom_call" | custom-call | tf_op jit(solution)/shard_map/sample/pallas_call | solution.py:686
  112.1 10.6 %all_to_all.21 = f32[4,2,4,4,128]{4,3,2,1,0:T(4,128)S(1)} all-to-all(f32[4,2,4,4,128]{4,3,2,1,0:T(4,128)S(1)} %sample.1), channel_id=1, replica_groups=mesh['gx'=4,'gy'=2,'gz'=4] {'gz'}, dimensions={0} | all-to-all | bytes 131072 | tf_op jit(solution)/shard_map/all_to_all | solution.py:689
  122.7 0.6 slice_bitcast_fusion
  123.3 0.6 slice_bitcast_fusion.1
  (9 shorter events, 0.1 us)
Async XLA Ops:
  0.6 0.9 copy-start.1
  0.6 0.9 copy-start.2
  0.7 0.9 copy-start
  13.9 20.9 %all-to-all-start.1 = ((f32[32,16,256]{2,1,0:T(8,128)}), f32[32,16,256]{2,1,0:T(8,128)S(1)}, u32[]{:S(2)}, u32[]{:S(2)}) async-start(f32[32,16,256]{2,1,0:T(8,128)} %spread.1), calls=%async_computation.1 | async-start | bytes 1048576 | tf_op jit(solution)/shard_map/all_to_all | solution.py:662
  19.7 22.2 %collective-permute-start = (f32[128,128]{1,0:T(8,128)S(1)}, f32[128,128]{1,0:T(8,128)S(1)}, u32[]{:S(2)}, u32[]{:S(2)}) collective-permute-start(f32[128,128]{1,0:T(8,128)S(1)} %bitcast.13), channel_id=1, source_target_pairs={{0,4},{4,0},{1,5},{5,1},{2,6},{6,2},{3,7},{7,3},{8,12},{12,8},{9,1... | collective-permute-start | bytes 196616 | tf_op jit(solution)/shard_map/ppermute | solution.py:604
  38.5 68.5 %all-to-all-start.2 = ((f32[32,16,256]{2,1,0:T(8,128)}), f32[32,16,256]{2,1,0:T(8,128)S(1)}, u32[]{:S(2)}, u32[]{:S(2)}) async-start(f32[32,16,256]{2,1,0:T(8,128)} %planes.1), calls=%async_computation.2 | async-start | bytes 1048576 | tf_op jit(solution)/shard_map/all_to_all | solution.py:678
  41.9 5.5 %collective-permute-start.1 = (f32[256,128]{1,0:T(8,128)S(1)}, f32[256,128]{1,0:T(8,128)S(1)}, u32[]{:S(2)}, u32[]{:S(2)}) collective-permute-start(f32[256,128]{1,0:T(8,128)S(1)} %pad_maximum_fusion.mid), channel_id=1, source_target_pairs={{0,1},{1,2},{2,3},{3,8},{8,9},{9,10},{10,11},{11,16},{16,17},{17,1... | collective-permute-start | bytes 393224 | tf_op jit(solution)/shard_map/ppermute | solution.py:604
  43.6 7.1 %collective-permute-start.2 = (f32[256,128]{1,0:T(8,128)S(1)}, f32[256,128]{1,0:T(8,128)S(1)}, u32[]{:S(2)}, u32[]{:S(2)}) collective-permute-start(f32[256,128]{1,0:T(8,128)S(1)} %pad_maximum_fusion.mid), channel_id=1, source_target_pairs={{1,0},{2,1},{3,2},{8,3},{9,8},{10,9},{11,10},{16,11},{17,16},{18,1... | collective-permute-start | bytes 393224 | tf_op jit(solution)/shard_map/ppermute | solution.py:604
  63.0 2.7 %collective-permute-start.3 = (f32[32,128]{1,0:T(8,128)S(1)}, f32[32,128]{1,0:T(8,128)S(1)}, u32[]{:S(2)}, u32[]{:S(2)}) collective-permute-start(f32[32,128]{1,0:T(8,128)S(1)} %get-tuple-element.4), channel_id=1, source_target_pairs={{0,4},{4,0},{1,5},{5,1},{2,6},{6,2},{3,7},{7,3},{8,12},{12,8},{9,1... | collective-permute-start | bytes 49160 | tf_op jit(solution)/shard_map/ppermute | solution.py:604
  65.7 8.7 %collective-permute-start.4 = (f32[64,128]{1,0:T(8,128)S(1)}, f32[64,128]{1,0:T(8,128)S(1)}, u32[]{:S(2)}, u32[]{:S(2)}) collective-permute-start(f32[64,128]{1,0:T(8,128)S(1)} %pad_maximum_fusion.2.slope_mid), channel_id=1, source_target_pairs={{0,1},{1,2},{2,3},{3,8},{8,9},{9,10},{10,11},{11,16},{16,17},{17,1... | collective-permute-start | bytes 98312 | tf_op jit(solution)/shard_map/ppermute | solution.py:604
  66.4 8.4 %collective-permute-start.5 = (f32[64,128]{1,0:T(8,128)S(1)}, f32[64,128]{1,0:T(8,128)S(1)}, u32[]{:S(2)}, u32[]{:S(2)}) collective-permute-start(f32[64,128]{1,0:T(8,128)S(1)} %pad_maximum_fusion.2.slope_mid), channel_id=1, source_target_pairs={{1,0},{2,1},{3,2},{8,3},{9,8},{10,9},{11,10},{16,11},{17,16},{18,1... | collective-permute-start | bytes 98312 | tf_op jit(solution)/shard_map/ppermute | solution.py:604

commit v4 on v3

--- a/solution.py
+++ b/solution.py
@@ -45,10 +45,15 @@
     return lax.dot_general(left, right, dims, preferred_element_type=F32)
 
 
+def stack2(values):
+    high, low = split2(values)
+    return jnp.concatenate([high, low], axis=0)
+
+
 def dot3(left, right, dims):
-    return (
-        dot(left[0], right[0], dims) + dot(left[0], right[1], dims) + dot(left[1], right[0], dims)
-    )
+    rows = left.shape[0] // 2
+    wide = dot(left, right[0], dims)
+    return wide[:rows] + wide[rows:] + dot(left[:rows], right[1], dims)
 
 
 def by_kind(kind, table, empty=0.0):
@@ -117,11 +122,10 @@
     tiles = lz // 128
     reach = columns // tiles
 
-    def kernel(atoms, table, basis_any, out, plane, line_hi, line_lo, basis_ref, sem):
+    def kernel(atoms, table, basis_any, out, plane, line, basis_ref, sem):
         fetch = pltpu.make_async_copy(basis_any, basis_ref, sem)
         fetch.start()
-        line_hi[...] = jnp.zeros(line_hi.shape, BF16)
-        line_lo[...] = jnp.zeros(line_lo.shape, BF16)
+        line[...] = jnp.zeros(line.shape, BF16)
         pieces = []
         for cy in range(cells_y):
             brick = []
@@ -137,21 +141,19 @@
                         [weights[1][y : y + 1] * along_x for y in range(PPC)], axis=0
                     )
                     lanes = pl.ds(place * slots, slots)
-                    points = pl.ds(place * PPC, PPC)
                     high, low = split2(value)
                     plane[tile, pl.ds(0, rows), lanes] = high
                     plane[tile, pl.ds(rows, rows), lanes] = low
                     high, low = split2(weights[2])
-                    line_hi[tile, points, lanes] = high
-                    line_lo[tile, points, lanes] = low
-                wide = dot(plane[tile], line_hi[tile], NT)
-                brick.append(
-                    wide[:rows] + wide[rows:] + dot(plane[tile, pl.ds(0, rows), :], line_lo[tile], NT)
-                )
+                    line[tile, pl.ds(place * PPC, PPC), lanes] = high
+                    line[tile, pl.ds(128 + place * PPC, PPC), lanes] = low
+                wide = dot(plane[tile], line[tile], NT)
+                wide = wide[:rows] + wide[rows:]
+                brick.append(wide[:, :128] + wide[:, 128:])
             if cy == 0:
                 fetch.wait()
             brick = jnp.concatenate(brick, axis=1)
-            pieces.append(dot3(split2(brick), (basis_ref[0], basis_ref[1]), NT))
+            pieces.append(dot3(stack2(brick), (basis_ref[0], basis_ref[1]), NT))
         if not relayout:
             for cy in range(cells_y):
                 out[pl.ds(cy * rows, rows), :] = pieces[cy]
@@ -179,8 +181,7 @@
         out_specs=VMEM,
         scratch_shapes=[
             pltpu.VMEM((tiles, 2 * rows, reach * slots), BF16),
-            pltpu.VMEM((tiles, 128, reach * slots), BF16),
-            pltpu.VMEM((tiles, 128, reach * slots), BF16),
+            pltpu.VMEM((tiles, 256, reach * slots), BF16),
             pltpu.VMEM((2, lz, lz), BF16),
             pltpu.SemaphoreType.DMA(()),
         ],
@@ -219,12 +220,12 @@
         factor = (4.0 * math.pi * jnp.exp(along * sharp)) * jnp.exp(across * sharp)
         green = jnp.where(squared == 0.0, 0.0, factor / jnp.where(squared == 0.0, 1.0, squared))
         fetches[0].wait()
-        value = dot3((x_ref[0], x_ref[1]), split2(grid[...]), NN)
+        value = dot3(x_ref[...], split2(grid[...]), NN)
         fetches[1].wait()
-        value = dot3(split2(value), (y_ref[0], y_ref[1]), NT) * green
-        value = dot3(split2(value), (y_ref[0], y_ref[1]), NN)
+        value = dot3(stack2(value), (y_ref[0], y_ref[1]), NT) * green
+        value = dot3(stack2(value), (y_ref[0], y_ref[1]), NN)
         fetches[2].wait()
-        value = dot3((xt_ref[0], xt_ref[1]), split2(value), NN)
+        value = dot3(xt_ref[...], split2(value), NN)
         for a in range(gx):
             for b in range(gy):
                 for c in range(gz):
@@ -240,8 +241,8 @@
         out_specs=VMEM,
         scratch_shapes=[
             pltpu.VMEM((lx, width), F32),
-            pltpu.VMEM((2, lx, lx), BF16),
-            pltpu.VMEM((2, lx, lx), BF16),
+            pltpu.VMEM((2 * lx, lx), BF16),
+            pltpu.VMEM((2 * lx, lx), BF16),
             pltpu.VMEM((2, width, width), BF16),
             pltpu.SemaphoreType.DMA((3,)),
         ],
@@ -281,13 +282,24 @@
         fetch.wait()
         for cy in range(cells_y):
             brick = dot3(
-                split2(lines[pl.ds(cy * rows, rows), :]), (basis_ref[0], basis_ref[1]), NN
+                stack2(lines[pl.ds(cy * rows, rows), :]), (basis_ref[0], basis_ref[1]), NN
             )
             for column in range(columns):
                 if column % reach == 0:
                     start = column // reach * 128
-                    high, low = split2(brick[:, start : start + 128])
-                    wide = jnp.concatenate([high, low, high], axis=1)
+                    value = brick[:, start : start + 128]
+                    high = value.astype(BF16)
+                    left_half = lax.broadcasted_iota(jnp.int32, value.shape, 1) < 64
+                    top = high.astype(F32)
+                    swapped = pltpu.roll(value - top, 64, 1)
+                    wides = [
+                        jnp.concatenate([half.astype(BF16), high], axis=1)
+                        for half in (
+                            jnp.where(left_half, top, swapped),
+                            jnp.where(left_half, swapped, top),
+                        )
+                    ]
+                wide = wides[column % reach * 2 // reach]
                 cell = atoms[column // cells_z, cy, :, column % cells_z, :]
                 pairs = [point_weights(cell[d : d + 1], cell[3 + d : 4 + d]) for d in range(3)]
                 (wx, sx), (wy, sy), (wz, sz) = pairs
@@ -295,8 +307,8 @@
                 high, low = split2(wz)
                 both = jnp.concatenate([high, sz.astype(BF16)], axis=1)
                 line[column, pl.ds(first, PPC), :] = both
-                line[column, pl.ds(128 + first, PPC), :] = both
-                line[column, pl.ds(256 + first, PPC), pl.ds(0, slots)] = low
+                line[column, pl.ds((first + 64) % 128, PPC), :] = both
+                line[column, pl.ds(128 + first, PPC), pl.ds(0, slots)] = low
                 both = dot(wide, line[column], NN)
                 plain, tilted = both[:, :slots], both[:, slots:]
                 force_x = jnp.zeros((PPC, slots), F32)
@@ -327,7 +339,7 @@
         out_specs=VMEM,
         scratch_shapes=[
             pltpu.VMEM((cells_y * rows, lz), F32),
-            pltpu.VMEM((columns, 384, 2 * slots), BF16),
+            pltpu.VMEM((columns, 256, 2 * slots), BF16),
             pltpu.VMEM((2, lz, lz), BF16),
             pltpu.SemaphoreType.DMA(()),
         ],
@@ -336,13 +348,49 @@
     )
 
 
-WIDE = ((0, 0), (1, 0), (0, 1), (1, 1), (2, 0), (0, 2))
-SHORT = WIDE[:4]
-
-
-def piece_rows(values, order, side):
-    pieces = split3(values)
-    return jnp.concatenate([pieces[entry[side]] for entry in order], axis=0)
+RIGHT = ((0, 0), (1, 0), (1, 0), (2, 0))
+LEFT = ((0, 1), (0, 1), (1, 2), (0, 2))
+
+
+def clear_spare(ref):
+    count = ref.shape[1] // 8
+    for tile in (1, 3):
+        ref[tile, pl.ds(7, count, stride=8), :] = jnp.zeros((count, ref.shape[2]), F32)
+
+
+def store_five(ref, first, count, values, order):
+    pieces = [split3(value) for value in values]
+    for tile, (main, third) in enumerate(order):
+        rows = [pieces[index][main] for index in range(5)]
+        rows += [pieces[index][third] for index in ((3, 4) if tile % 2 else (0, 1, 2))]
+        for row, value in enumerate(rows):
+            ref[tile, pl.ds(first * 8 + row, count, stride=8), :] = value
+
+
+def five_rows(ref, cell):
+    tiles = [ref[tile, pl.ds(cell * 8, 8), :] for tile in range(4)]
+    return jnp.concatenate(tiles, axis=0).astype(BF16)
+
+
+def fill(feature, own_feature, right, left):
+    def fill_right(n, carry):
+        right[n] = five_rows(feature, n)
+        return carry
+
+    def fill_left(n, carry):
+        left[n] = five_rows(own_feature, n).T
+        return carry
+
+    lax.fori_loop(0, right.shape[0], fill_right, 0, unroll=8)
+    lax.fori_loop(0, left.shape[0], fill_left, 0, unroll=8)
+
+
+def two_rows(values, side):
+    high = values.astype(BF16).astype(F32)
+    rest = values - high
+    row = lax.broadcasted_iota(jnp.int32, values.shape, 0)
+    pick = row < 4 if side else row % 4 < 2
+    return jnp.concatenate([jnp.where(pick, high, rest), jnp.zeros_like(values)], axis=0)
 
 
 def channel(block, y, nz, index):
@@ -369,8 +417,8 @@
     def kernel(
         low, mid, high, electrons, embed, density, slope, feature, own_feature, right, left, sums
     ):
-        feature[...] = jnp.zeros(feature.shape, F32)
-        own_feature[...] = jnp.zeros(own_feature.shape, F32)
+        clear_spare(feature)
+        clear_spare(own_feature)
         for x, block in enumerate((low, mid, high)):
             for y in range(sy):
                 pos = row_positions(block, x, y, sy, nz)
@@ -378,30 +426,17 @@
                 kind = channel(block, y, nz, 3)
                 scale = jnp.exp(jnp.log(by_kind(kind, electrons, 1.0)) * (1.0 / 3.0))
                 scale = jnp.where(kind >= 0.0, scale, 0.0)
-                base = (x * sy + y) * nz * 8
-                feature[pl.ds(base, nz, stride=8), :] = scale * (1.0 - square)
-                for d in range(3):
-                    feature[pl.ds(base + 1 + d, nz, stride=8), :] = 2.0 * scale * pos[d]
-                feature[pl.ds(base + 4, nz, stride=8), :] = -scale
+                double = 2.0 * scale
+                values = [scale * (1.0 - square)] + [double * pos[d] for d in range(3)] + [-scale]
+                store_five(feature, (x * sy + y) * nz, nz, values, RIGHT)
                 if x == 1 and 1 <= y <= cells_y:
                     for dz in range(3):
                         across = pos[2] - (dz - 1.0)
                         square = pos[0] * pos[0] + pos[1] * pos[1] + across * across
-                        base = (dz * own + (y - 1) * nz) * 8
-                        rows = (jnp.ones_like(square), pos[0], pos[1], across, square)
-                        for k, value in enumerate(rows):
-                            own_feature[pl.ds(base + k, nz, stride=8), :] = value
-
-        def fill_right(n, carry):
-            right[n] = piece_rows(feature[pl.ds(n * 8, 8), :], WIDE, 0).astype(BF16)
-            return carry
-
-        def fill_left(n, carry):
-            left[n] = piece_rows(own_feature[pl.ds(n * 8, 8), :], WIDE, 1).T.astype(BF16)
-            return carry
-
-        lax.fori_loop(0, total, fill_right, 0, unroll=8)
-        lax.fori_loop(0, 3 * own, fill_left, 0, unroll=8)
+                        values = [jnp.ones_like(square), pos[0], pos[1], across, square]
+                        store_five(own_feature, dz * own + (y - 1) * nz, nz, values, LEFT)
+
+        fill(feature, own_feature, right, left)
         same = same_slot(slots)
         lane = lax.broadcasted_iota(jnp.int32, (slots, 128), 1)
         sums[...] = jnp.zeros(sums.shape, F32)
@@ -446,10 +481,10 @@
         in_specs=[VMEM, VMEM, VMEM, SMEM, SMEM],
         out_specs=(VMEM, VMEM),
         scratch_shapes=[
-            pltpu.VMEM((total * 8, slots), F32),
-            pltpu.VMEM((3 * own * 8, slots), F32),
-            pltpu.VMEM((total, 48, slots), BF16),
-            pltpu.VMEM((3 * own, slots, 48), BF16),
+            pltpu.VMEM((4, total * 8, slots), F32),
+            pltpu.VMEM((4, 3 * own * 8, slots), F32),
+            pltpu.VMEM((total, 32, slots), BF16),
+            pltpu.VMEM((3 * own, slots, 32), BF16),
             pltpu.VMEM((slots, 128), F32),
         ],
         compiler_params=PARAMS,
@@ -464,15 +499,14 @@
     sy = cells_y + 2
     own = cells_y * nz
     total = 3 * sy * nz
-    chunk = 64
+    chunk = 8
 
     def kernel(
         low, mid, high, slope_low, slope_mid, slope_high, electrons, repel, out,
-        feature, extra, own_feature, own_extra, place, right, right_extra, left, left_extra,
-        sums,
+        feature, extra, own_feature, own_extra, place, right, right_extra, left, left_extra, acc, sums,
     ):
-        for ref in (feature, extra, own_feature, own_extra):
-            ref[...] = jnp.zeros(ref.shape, F32)
+        clear_spare(feature)
+        clear_spare(own_feature)
         blocks = zip((low, mid, high), (slope_low, slope_mid, slope_high))
         for x, (block, slopes) in enumerate(blocks):
             for y in range(sy):
@@ -484,42 +518,37 @@
                 inverse = inverse * inverse
                 steep = slopes[pl.ds(y * nz, nz), :] * inverse
                 mild = -3.0 * by_kind(kind, electrons) * inverse
-                base = (x * sy + y) * nz * 8
-                feature[pl.ds(base, nz, stride=8), :] = scale * (1.0 - square)
+                double = 2.0 * scale
+                values = [scale * (1.0 - square)] + [double * pos[d] for d in range(3)] + [-scale]
+                cell = (x * sy + y) * nz
+                store_five(feature, cell, nz, values, RIGHT)
                 for d in range(3):
-                    feature[pl.ds(base + 1 + d, nz, stride=8), :] = 2.0 * scale * pos[d]
-                    place[pl.ds(base + d, nz, stride=8), :] = pos[d]
-                feature[pl.ds(base + 4, nz, stride=8), :] = -scale
-                extra[pl.ds(base, nz, stride=8), :] = steep
-                extra[pl.ds(base + 1, nz, stride=8), :] = mild
+                    place[pl.ds(cell * 8 + d, nz, stride=8), :] = pos[d]
+                for k in range(8):
+                    extra[pl.ds(cell * 8 + k, nz, stride=8), :] = mild if k % 2 else steep
                 if x == 1 and 1 <= y <= cells_y:
-                    base = (y - 1) * nz * 8
-                    own_extra[pl.ds(base, nz, stride=8), :] = mild
-                    own_extra[pl.ds(base + 1, nz, stride=8), :] = steep
+                    cell = (y - 1) * nz
+                    for k in range(8):
+                        own_extra[pl.ds(cell * 8 + k, nz, stride=8), :] = steep if k % 2 else mild
                     for dz in range(3):
                         across = pos[2] - (dz - 1.0)
                         square = pos[0] * pos[0] + pos[1] * pos[1] + across * across
-                        base = (dz * own + (y - 1) * nz) * 8
-                        rows = (1.0, pos[0], pos[1], across, square)
-                        for k, value in enumerate(rows):
-                            own_feature[pl.ds(base + k, nz, stride=8), :] = scale * value
-
-        def fill_right(n, carry):
-            rows = pl.ds(n * 8, 8)
-            right[n] = piece_rows(feature[rows, :], WIDE, 0).astype(BF16)
-            right_extra[n] = piece_rows(extra[rows, :], SHORT, 0).astype(BF16)
+                        values = [scale] + [
+                            scale * value for value in (pos[0], pos[1], across, square)
+                        ]
+                        store_five(own_feature, dz * own + cell, nz, values, LEFT)
+
+        fill(feature, own_feature, right, left)
+
+        def fill_right_extra(n, carry):
+            right_extra[n] = two_rows(extra[pl.ds(n * 8, 8), :], 0).astype(BF16)
             return carry
 
-        def fill_left(n, carry):
-            left[n] = piece_rows(own_feature[pl.ds(n * 8, 8), :], WIDE, 1).T.astype(BF16)
+        def fill_left_extra(n, carry):
+            left_extra[n] = two_rows(own_extra[pl.ds(n * 8, 8), :], 1).astype(BF16).T
             return carry
 
-        def fill_left_extra(n, carry):
-            left_extra[n] = piece_rows(own_extra[pl.ds(n * 8, 8), :], SHORT, 1).T.astype(BF16)
-            return carry
-
-        lax.fori_loop(0, total, fill_right, 0, unroll=8)
-        lax.fori_loop(0, 3 * own, fill_left, 0, unroll=8)
+        lax.fori_loop(0, total, fill_right_extra, 0, unroll=8)
         lax.fori_loop(0, own, fill_left_extra, 0, unroll=8)
         same = same_slot(slots)
         lane = lax.broadcasted_iota(jnp.int32, (slots, 128), 1)
@@ -527,40 +556,48 @@
 
         def one_cell(n, carry):
             y, z = n // nz, n % nz
-            for start in range(0, slots, chunk):
-                rows = pl.ds(start, chunk)
-                lhs_extra = left_extra[n, rows, :]
-                parts = [jnp.zeros((chunk, slots), F32) for _ in range(4)]
-                for dz in range(3):
-                    zz = (z + (dz - 1 + nz)) % nz
-                    lhs = left[dz * own + n, rows, :]
-                    near = [(dx * sy + y + dy) * nz + zz for dx in range(3) for dy in range(3)]
-                    if dz == 1:
-                        near.append(near.pop(4))
-                    for index in range(0, 9, 2):
-                        pair = near[index : index + 2]
-                        rhs = [right[cell] for cell in pair]
-                        rhs_extra = [right_extra[cell] for cell in pair]
-                        if len(pair) > 1:
-                            rhs = [jnp.concatenate(rhs, axis=1)]
-                            rhs_extra = [jnp.concatenate(rhs_extra, axis=1)]
-                        weight = jnp.maximum(dot(lhs, rhs[0], NN), 0.0)
-                        if dz == 1 and index == 8:
-                            weight = jnp.where(same[start : start + chunk], 0.0, weight)
-                        value = (weight * dot(lhs_extra, rhs_extra[0], NN) - 2.0) * weight
-                        for k, cell in enumerate(pair):
-                            tile = value[:, k * slots : (k + 1) * slots]
-                            parts[3] = parts[3] + tile
-                            for d in range(3):
-                                there = place[pl.ds(cell * 8 + d, 1), :]
-                                if d == 2 and dz != 1:
-                                    there = there + (dz - 1.0)
-                                parts[d] = parts[d] + tile * there
-                for d in range(4):
-                    column = jnp.sum(parts[d], axis=1, keepdims=True)
-                    sums[d, rows, :] = jnp.where(
-                        lane[start : start + chunk] == n, column, sums[d, rows, :]
-                    )
+            lhs_extra = left_extra[n]
+            first = True
+            for dz in range(3):
+                zz = (z + (dz - 1 + nz)) % nz
+                lhs = left[dz * own + n]
+                near = [(dx * sy + y + dy) * nz + zz for dx in range(3) for dy in range(3)]
+                if dz == 1:
+                    near.append(near.pop(4))
+                for index in range(0, 9, 2):
+                    pair = near[index : index + 2]
+                    rhs = [right[cell] for cell in pair]
+                    rhs_extra = [right_extra[cell] for cell in pair]
+                    if len(pair) > 1:
+                        rhs = [jnp.concatenate(rhs, axis=1)]
+                        rhs_extra = [jnp.concatenate(rhs_extra, axis=1)]
+                    weight = jnp.maximum(dot(lhs, rhs[0], NN), 0.0)
+                    if dz == 1 and index == 8:
+                        weight = jnp.where(same, 0.0, weight)
+                    value = (weight * dot(lhs_extra, rhs_extra[0], NN) - 2.0) * weight
+                    there = [
+                        [place[pl.ds(cell * 8 + d, 1), :] for d in range(3)] for cell in pair
+                    ]
+                    if dz != 1:
+                        there = [[x, y_, z_ + (dz - 1.0)] for x, y_, z_ in there]
+                    for start in range(0, slots, chunk):
+                        rows = pl.ds(start, chunk)
+                        tiles = [
+                            value[start : start + chunk, k * slots : (k + 1) * slots]
+                            for k in range(len(pair))
+                        ]
+                        sums_of = [
+                            [tile * there[k][d] for k, tile in enumerate(tiles)] for d in range(3)
+                        ] + [tiles]
+                        for d in range(4):
+                            part = sums_of[d][0]
+                            for more in sums_of[d][1:]:
+                                part = part + more
+                            acc[d, rows, :] = part if first else acc[d, rows, :] + part
+                    first = False
+            for d in range(4):
+                column = jnp.sum(acc[d], axis=1, keepdims=True)
+                sums[d] = jnp.where(lane == n, column, sums[d])
             return carry
 
         lax.fori_loop(0, own, one_cell, 0, unroll=4)
@@ -577,15 +614,16 @@
         in_specs=[VMEM] * 6 + [SMEM, SMEM],
         out_specs=VMEM,
         scratch_shapes=[
+            pltpu.VMEM((4, total * 8, slots), F32),
             pltpu.VMEM((total * 8, slots), F32),
-            pltpu.VMEM((total * 8, slots), F32),
-            pltpu.VMEM((3 * own * 8, slots), F32),
+            pltpu.VMEM((4, 3 * own * 8, slots), F32),
             pltpu.VMEM((own * 8, slots), F32),
             pltpu.VMEM((total * 8, slots), F32),
-            pltpu.VMEM((total, 48, slots), BF16),
             pltpu.VMEM((total, 32, slots), BF16),
-            pltpu.VMEM((3 * own, slots, 48), BF16),
-            pltpu.VMEM((own, slots, 32), BF16),
+            pltpu.VMEM((total, 16, slots), BF16),
+            pltpu.VMEM((3 * own, slots, 32), BF16),
+            pltpu.VMEM((own, slots, 16), BF16),
+            pltpu.VMEM((4, slots, slots), F32),
             pltpu.VMEM((4, slots, 128), F32),
         ],
         compiler_params=PARAMS,
@@ -673,16 +711,15 @@
 
     rank = lax.axis_index(("gx", "gy", "gz")).astype(jnp.int32).reshape(1)
     planes = make_planes(gx, gy, gz, yl * modes, lx, ly, lz)(
-        rank, near_core(planes), x_pair, xt_pair, y_pair
+        rank, near_core(planes), x_pair.reshape(2 * lx, lx), xt_pair.reshape(2 * lx, lx), y_pair
     )
     lines = lax.all_to_all(planes, ("gx", "gy", "gz"), split_axis=0, concat_axis=0, tiled=True)
     if not relayout:
         lines = lines.reshape(devices, PPC, yl, modes).transpose(2, 1, 0, 3)
         lines = lines.reshape(yl * PPC, lz)
 
-    short = make_force(cells_y, nz, slots)(
-        *map(near_core, near), *map(near_core, near_slopes), species_density, species_pair
-    )
+    operands = (*near, *near_slopes)
+    short = make_force(cells_y, nz, slots)(*map(near_core, operands), species_density, species_pair)
     result = make_sample(gz, cells_y, cells_z, slots, lz, devices, relayout)(
         near_core(lines), near_core(atoms), near_core(short), near_core(density), species_charge, z_pair
     )

time: 125 us -> 123 us (0.984)
  Pallas kernels: 58 us -> 55.9 us
    pallas_call x1, Pallas kernels: 32.2 us -> 30.7 us  [on_device(): make_force(cells_y, nz, slots)]
where the time goes in v4:
time: 123 us; the launch traced here: 122 us
  Pallas kernels  55.9 us (45%)
  waiting for transfers between devices  23.4 us (19%)
  starting transfers between devices  21.4 us (17%)
  blocking collectives  18 us (15%)
  local copies, waits for them, and re-layouts  1.27 us (1%)
    pallas_call x1, Pallas kernels, on_device(): make_force(cells_y, nz, slots)  30.7 us
    all_to_all x1, waiting for transfers between devices, on_device(): lax.all_to_all(lines, ('gx', 'gy', 'gz'), split_axis=0, concat_axis=0, ti...  13.7 us
    pallas_call x1, Pallas kernels, on_device(): make_density(cells_y, nz, slots)  12.6 us
    all_to_all x1, blocking collectives, on_device(): lax.all_to_all(result, 'gz', split_axis=0, concat_axis=0, tiled=True)  10.6 us
    ppermute x2, starting transfers between devices, shifted(): lax.ppermute(part, axis, down)  7.55 us
    all_to_all x1, blocking collectives, on_device(): atoms = lax.all_to_all(atoms, 'gz', split_axis=0, concat_axis=0, tiled=True)  7.48 us
    ppermute x4, waiting for transfers between devices, shifted(): lax.ppermute(part, axis, up)  5.94 us
    all_to_all x1, starting transfers between devices, on_device(): lax.all_to_all(lines, ('gx', 'gy', 'gz'), split_axis=0, concat_axis=0, ti...  5.67 us
  transfers between devices with their start and end apart: 8, of which 6 were waited for; matrix products, arithmetic and copies ran while one was open for 0% of the time, Pallas kernels for 39%

profile of v4, /device:TPU:1, one launch (start us, length us, event | category | flops | bytes accessed | tf_op | source)
XLA Modules:
  0.0 121.8 jit_solution(12122935112518378648)
XLA Ops:
  0.6 0.0 copy-start.1
  0.6 0.0 copy-start.2
  0.7 0.0 copy-start
  0.7 0.8 convert_bitcast_fusion
  1.5 0.0 copy-done.1
  1.5 0.0 copy-done.2
  1.5 0.1 select_bitcast_fusion
  1.6 0.0 copy-done
  1.6 7.5 %all_to_all.20.atoms = f32[4,2,7,4,128]{4,3,2,1,0:T(4,128)S(1)} all-to-all(f32[4,2,7,4,128]{4,3,2,1,0:T(4,128)S(1)} %pad_maximum_fusion.1), channel_id=1, replica_groups=mesh['gx'=4,'gy'=2,'gz'=4] {'gz'}, dimensions={0} | all-to-all | bytes 229376 | tf_op jit(solution)/shard_map/all_to_all | solution.py:691
  9.1 4.2 %spread.1 = f32[32,16,256]{2,1,0:T(8,128)} custom-call(f32[4,2,7,4,128]{4,3,2,1,0:T(4,128)S(1)} %all_to_all.20.atoms, f32[2]{0:T(128)} %table.3, bf16[2,256,256]{2,1,0:T(8,128)(2,1)} %constant.31.clone.basis_any), custom_call_target="tpu_custom_call" | custom-call | tf_op jit(solution)/shard_map/spread/pallas_call | solution.py:696
  13.4 5.7 %all-to-all-start.1 = ((f32[32,16,256]{2,1,0:T(8,128)}), f32[32,16,256]{2,1,0:T(8,128)S(1)}, u32[]{:S(2)}, u32[]{:S(2)}) async-start(f32[32,16,256]{2,1,0:T(8,128)} %spread.1), calls=%async_computation.1 | async-start | bytes 1048576 | tf_op jit(solution)/shard_map/all_to_all | solution.py:700
  19.1 1.4 %collective-permute-start = (f32[128,128]{1,0:T(8,128)S(1)}, f32[128,128]{1,0:T(8,128)S(1)}, u32[]{:S(2)}, u32[]{:S(2)}) collective-permute-start(f32[128,128]{1,0:T(8,128)S(1)} %bitcast.13), channel_id=1, source_target_pairs={{0,4},{4,0},{1,5},{5,1},{2,6},{6,2},{3,7},{7,3},{8,12},{12,8},{9,1... | collective-permute-start | bytes 196616 | tf_op jit(solution)/shard_map/ppermute | solution.py:642
  20.6 13.7 %all-to-all-done.1.data = f32[32,16,256]{2,1,0:T(8,128)S(1)} async-done(((f32[32,16,256]{2,1,0:T(8,128)}), f32[32,16,256]{2,1,0:T(8,128)S(1)}, u32[]{:S(2)}, u32[]{:S(2)}) %all-to-all-start.1) | async-done | bytes 524320 | tf_op jit(solution)/shard_map/all_to_all | solution.py:700
  34.3 3.6 %planes.1 = f32[32,16,256]{2,1,0:T(8,128)} custom-call(s32[1]{0:T(128)} %bitcast.rank, f32[32,16,256]{2,1,0:T(8,128)S(1)} %all-to-all-done.1.data, bf16[512,256]{1,0:T(8,128)(2,1)} %constant.34.x_any, bf16[512,256]{1,0:T(8,128)(2,1)} %constant.35.xt_any, bf16[2,512,512]{2,1,0:T(8,128)(2,1)} %constant.33.clone.y_any), custom_call_target="tpu_custom_call" | custom-call | tf_op jit(solution)/shard_map/planes/pallas_call | solution.py:713
  37.9 3.4 %all-to-all-start.2 = ((f32[32,16,256]{2,1,0:T(8,128)}), f32[32,16,256]{2,1,0:T(8,128)S(1)}, u32[]{:S(2)}, u32[]{:S(2)}) async-start(f32[32,16,256]{2,1,0:T(8,128)} %planes.1), calls=%async_computation.2 | async-start | bytes 1048576 | tf_op jit(solution)/shard_map/all_to_all | solution.py:716
  41.3 0.0 collective-permute-done
  41.3 1.7 %collective-permute-start.1 = (f32[256,128]{1,0:T(8,128)S(1)}, f32[256,128]{1,0:T(8,128)S(1)}, u32[]{:S(2)}, u32[]{:S(2)}) collective-permute-start(f32[256,128]{1,0:T(8,128)S(1)} %pad_maximum_fusion.mid), channel_id=1, source_target_pairs={{0,1},{1,2},{2,3},{3,8},{8,9},{9,10},{10,11},{11,16},{16,17},{17,1... | collective-permute-start | bytes 393224 | tf_op jit(solution)/shard_map/ppermute | solution.py:642
  43.0 0.0 collective-permute-start.2
  43.0 3.8 %collective-permute-done.1.low = f32[256,128]{1,0:T(8,128)S(1)} collective-permute-done((f32[256,128]{1,0:T(8,128)S(1)}, f32[256,128]{1,0:T(8,128)S(1)}, u32[]{:S(2)}, u32[]{:S(2)}) %collective-permute-start.1) | collective-permute-done | bytes 131104 | tf_op jit(solution)/shard_map/ppermute | solution.py:642
  46.8 3.3 %collective-permute-done.2.high = f32[256,128]{1,0:T(8,128)S(1)} collective-permute-done((f32[256,128]{1,0:T(8,128)S(1)}, f32[256,128]{1,0:T(8,128)S(1)}, u32[]{:S(2)}, u32[]{:S(2)}) %collective-permute-start.2) | collective-permute-done | bytes 131104 | tf_op jit(solution)/shard_map/ppermute | solution.py:642
  50.1 12.6 %density.1 = (f32[2,16,128]{2,1,0:T(8,128)S(1)}, f32[32,128]{1,0:T(8,128)S(1)}) custom-call(f32[256,128]{1,0:T(8,128)S(1)} %collective-permute-done.1.low, f32[256,128]{1,0:T(8,128)S(1)} %pad_maximum_fusion.mid, f32[256,128]{1,0:T(8,128)S(1)} %collective-permute-done.2.high, f32[2]{0:T(128)} %electrons.3, f32[2]{0:T(128)} %embed.1), custom_call_target="tpu_custom_call" | custom-call | flops 566231040 | bytes 393216 | tf_op jit(solution)/shard_map/density/pallas_call | solution.py:707
  62.7 1.0 collective-permute-start.3
  63.7 1.7 %collective-permute-done.3 = f32[32,128]{1,0:T(8,128)S(1)} collective-permute-done((f32[32,128]{1,0:T(8,128)S(1)}, f32[32,128]{1,0:T(8,128)S(1)}, u32[]{:S(2)}, u32[]{:S(2)}) %collective-permute-start.3) | collective-permute-done | bytes 16416 | tf_op jit(solution)/shard_map/ppermute | solution.py:642
  65.4 0.7 collective-permute-start.4
  66.1 7.5 %collective-permute-start.5 = (f32[64,128]{1,0:T(8,128)S(1)}, f32[64,128]{1,0:T(8,128)S(1)}, u32[]{:S(2)}, u32[]{:S(2)}) collective-permute-start(f32[64,128]{1,0:T(8,128)S(1)} %pad_maximum_fusion.2.slope_mid), channel_id=1, source_target_pairs={{1,0},{2,1},{3,2},{8,3},{9,8},{10,9},{11,10},{16,11},{17,16},{18,1... | collective-permute-start | bytes 98312 | tf_op jit(solution)/shard_map/ppermute | solution.py:642
  73.7 0.5 collective-permute-done.4.slope_low
  74.1 0.4 collective-permute-done.5.slope_high
  74.5 30.7 %force.1.short = f32[3,2,16,128]{3,2,1,0:T(8,128)S(1)} custom-call(f32[256,128]{1,0:T(8,128)S(1)} %collective-permute-done.1.low, f32[256,128]{1,0:T(8,128)S(1)} %pad_maximum_fusion.mid, f32[256,128]{1,0:T(8,128)S(1)} %collective-permute-done.2.high, f32[64,128]{1,0:T(8,128)S(1)} %collective-permute-done.4.slope_low, ...), custom_call_target="tpu_custom_call" | custom-call | flops 1415577600 | bytes 393216 | tf_op jit(solution)/shard_map/force/pallas_call | solution.py:722
  105.3 0.0 all-to-all-done.2.data
  105.3 4.7 %sample.1 = f32[4,2,4,4,128]{4,3,2,1,0:T(4,128)S(1)} custom-call(f32[32,16,256]{2,1,0:T(8,128)S(1)} %all-to-all-done.2.data, f32[4,2,7,4,128]{4,3,2,1,0:T(4,128)S(1)} %all_to_all.20.atoms, f32[3,2,16,128]{3,2,1,0:T(8,128)S(1)} %force.1.short, f32[2,16,128]{2,1,0:T(8,128)S(1)} %get-tuple-element.5.dens, f32[2]{0:T(128)} %table.3, ...), custom_call_target="tpu_custom_call" | custom-call | tf_op jit(solution)/shard_map/sample/pallas_call | solution.py:723
  110.0 10.6 %all_to_all.21 = f32[4,2,4,4,128]{4,3,2,1,0:T(4,128)S(1)} all-to-all(f32[4,2,4,4,128]{4,3,2,1,0:T(4,128)S(1)} %sample.1), channel_id=1, replica_groups=mesh['gx'=4,'gy'=2,'gz'=4] {'gz'}, dimensions={0} | all-to-all | bytes 131072 | tf_op jit(solution)/shard_map/all_to_all | solution.py:726
  120.6 0.6 slice_bitcast_fusion
  121.2 0.6 slice_bitcast_fusion.1
  (9 shorter events, 0.1 us)
Async XLA Ops:
  0.6 0.9 copy-start.1
  0.6 0.9 copy-start.2
  0.7 0.9 copy-start
  13.4 20.9 %all-to-all-start.1 = ((f32[32,16,256]{2,1,0:T(8,128)}), f32[32,16,256]{2,1,0:T(8,128)S(1)}, u32[]{:S(2)}, u32[]{:S(2)}) async-start(f32[32,16,256]{2,1,0:T(8,128)} %spread.1), calls=%async_computation.1 | async-start | bytes 1048576 | tf_op jit(solution)/shard_map/all_to_all | solution.py:700
  19.1 22.1 %collective-permute-start = (f32[128,128]{1,0:T(8,128)S(1)}, f32[128,128]{1,0:T(8,128)S(1)}, u32[]{:S(2)}, u32[]{:S(2)}) collective-permute-start(f32[128,128]{1,0:T(8,128)S(1)} %bitcast.13), channel_id=1, source_target_pairs={{0,4},{4,0},{1,5},{5,1},{2,6},{6,2},{3,7},{7,3},{8,12},{12,8},{9,1... | collective-permute-start | bytes 196616 | tf_op jit(solution)/shard_map/ppermute | solution.py:642
  37.9 67.4 %all-to-all-start.2 = ((f32[32,16,256]{2,1,0:T(8,128)}), f32[32,16,256]{2,1,0:T(8,128)S(1)}, u32[]{:S(2)}, u32[]{:S(2)}) async-start(f32[32,16,256]{2,1,0:T(8,128)} %planes.1), calls=%async_computation.2 | async-start | bytes 1048576 | tf_op jit(solution)/shard_map/all_to_all | solution.py:716
  41.3 5.5 %collective-permute-start.1 = (f32[256,128]{1,0:T(8,128)S(1)}, f32[256,128]{1,0:T(8,128)S(1)}, u32[]{:S(2)}, u32[]{:S(2)}) collective-permute-start(f32[256,128]{1,0:T(8,128)S(1)} %pad_maximum_fusion.mid), channel_id=1, source_target_pairs={{0,1},{1,2},{2,3},{3,8},{8,9},{9,10},{10,11},{11,16},{16,17},{17,1... | collective-permute-start | bytes 393224 | tf_op jit(solution)/shard_map/ppermute | solution.py:642
  43.0 7.1 %collective-permute-start.2 = (f32[256,128]{1,0:T(8,128)S(1)}, f32[256,128]{1,0:T(8,128)S(1)}, u32[]{:S(2)}, u32[]{:S(2)}) collective-permute-start(f32[256,128]{1,0:T(8,128)S(1)} %pad_maximum_fusion.mid), channel_id=1, source_target_pairs={{1,0},{2,1},{3,2},{8,3},{9,8},{10,9},{11,10},{16,11},{17,16},{18,1... | collective-permute-start | bytes 393224 | tf_op jit(solution)/shard_map/ppermute | solution.py:642
  62.7 2.7 %collective-permute-start.3 = (f32[32,128]{1,0:T(8,128)S(1)}, f32[32,128]{1,0:T(8,128)S(1)}, u32[]{:S(2)}, u32[]{:S(2)}) collective-permute-start(f32[32,128]{1,0:T(8,128)S(1)} %get-tuple-element.4), channel_id=1, source_target_pairs={{0,4},{4,0},{1,5},{5,1},{2,6},{6,2},{3,7},{7,3},{8,12},{12,8},{9,1... | collective-permute-start | bytes 49160 | tf_op jit(solution)/shard_map/ppermute | solution.py:642
  65.4 8.7 %collective-permute-start.4 = (f32[64,128]{1,0:T(8,128)S(1)}, f32[64,128]{1,0:T(8,128)S(1)}, u32[]{:S(2)}, u32[]{:S(2)}) collective-permute-start(f32[64,128]{1,0:T(8,128)S(1)} %pad_maximum_fusion.2.slope_mid), channel_id=1, source_target_pairs={{0,1},{1,2},{2,3},{3,8},{8,9},{9,10},{10,11},{11,16},{16,17},{17,1... | collective-permute-start | bytes 98312 | tf_op jit(solution)/shard_map/ppermute | solution.py:642
  66.1 8.4 %collective-permute-start.5 = (f32[64,128]{1,0:T(8,128)S(1)}, f32[64,128]{1,0:T(8,128)S(1)}, u32[]{:S(2)}, u32[]{:S(2)}) collective-permute-start(f32[64,128]{1,0:T(8,128)S(1)} %pad_maximum_fusion.2.slope_mid), channel_id=1, source_target_pairs={{1,0},{2,1},{3,2},{8,3},{9,8},{10,9},{11,10},{16,11},{17,16},{18,1... | collective-permute-start | bytes 98312 | tf_op jit(solution)/shard_map/ppermute | solution.py:642

commit v5 on v4

--- a/solution.py
+++ b/solution.py
@@ -122,7 +122,7 @@
     tiles = lz // 128
     reach = columns // tiles
 
-    def kernel(atoms, table, basis_any, out, plane, line, basis_ref, sem):
+    def kernel(atoms, table, basis_any, out_any, plane, line, basis_ref, out, sem, sends):
         fetch = pltpu.make_async_copy(basis_any, basis_ref, sem)
         fetch.start()
         line[...] = jnp.zeros(line.shape, BF16)
@@ -157,8 +157,12 @@
         if not relayout:
             for cy in range(cells_y):
                 out[pl.ds(cy * rows, rows), :] = pieces[cy]
+            copy = pltpu.make_async_copy(out, out_any, sends.at[0])
+            copy.start()
+            copy.wait()
             return
         chunks = 128 // modes
+        copies = []
         for tile in range(tiles):
             for group in range(yl // chunks):
                 parts = []
@@ -169,6 +173,11 @@
                     )
                 for chunk, value in enumerate(chunk_transpose(parts, modes)):
                     out[tile * chunks + chunk, :, pl.ds(group * 128, 128)] = value
+            there = pl.ds(tile * chunks, chunks)
+            copies.append(pltpu.make_async_copy(out.at[there], out_any.at[there], sends.at[tile]))
+            copies[-1].start()
+        for copy in copies:
+            copy.wait()
 
     if relayout:
         shape = (devices, PPC, yl * modes)
@@ -176,14 +185,16 @@
         shape = (cells_y * rows, lz)
     return pl.pallas_call(
         kernel,
-        out_shape=pltpu.VMEM(shape, F32),
+        out_shape=jax.ShapeDtypeStruct(shape, F32),
         in_specs=[VMEM, SMEM, ANY],
-        out_specs=VMEM,
+        out_specs=ANY,
         scratch_shapes=[
             pltpu.VMEM((tiles, 2 * rows, reach * slots), BF16),
             pltpu.VMEM((tiles, 256, reach * slots), BF16),
             pltpu.VMEM((2, lz, lz), BF16),
+            pltpu.VMEM(shape, F32),
             pltpu.SemaphoreType.DMA(()),
+            pltpu.SemaphoreType.DMA((tiles,)),
         ],
         compiler_params=PARAMS,
         name="spread",
@@ -198,7 +209,9 @@
     def wave_square(indices, length):
         return jnp.square(signed_modes(indices, length).astype(F32) * (2.0 * math.pi / length))
 
-    def kernel(rank, data, x_any, xt_any, y_any, out, grid, x_ref, xt_ref, y_ref, sems):
+    def kernel(
+        rank, data, x_any, xt_any, y_any, out_any, grid, x_ref, xt_ref, y_ref, out, sems, sends
+    ):
         fetches = [
             pltpu.make_async_copy(source, target, sems.at[index])
             for index, (source, target) in enumerate(
@@ -225,26 +238,35 @@
         value = dot3(stack2(value), (y_ref[0], y_ref[1]), NT) * green
         value = dot3(stack2(value), (y_ref[0], y_ref[1]), NN)
         fetches[2].wait()
-        value = dot3(xt_ref[...], split2(value), NN)
-        for a in range(gx):
-            for b in range(gy):
+        copies = []
+        for b in range(gy):
+            part = dot3(xt_ref[...], split2(value[:, b * lanes : (b + 1) * lanes]), NN)
+            for a in range(gx):
+                first = (a * gy + b) * gz
                 for c in range(gz):
                     start = (a * gz + c) * PPC
-                    out[(a * gy + b) * gz + c] = value[
-                        start : start + PPC, b * lanes : (b + 1) * lanes
-                    ]
+                    out[first + c] = part[start : start + PPC]
+                there = pl.ds(first, gz)
+                copies.append(
+                    pltpu.make_async_copy(out.at[there], out_any.at[there], sends.at[len(copies)])
+                )
+                copies[-1].start()
+        for copy in copies:
+            copy.wait()
 
     return pl.pallas_call(
         kernel,
-        out_shape=pltpu.VMEM((gx * gy * gz, PPC, lanes), F32),
+        out_shape=jax.ShapeDtypeStruct((gx * gy * gz, PPC, lanes), F32),
         in_specs=[SMEM, VMEM, ANY, ANY, ANY],
-        out_specs=VMEM,
+        out_specs=ANY,
         scratch_shapes=[
             pltpu.VMEM((lx, width), F32),
             pltpu.VMEM((2 * lx, lx), BF16),
             pltpu.VMEM((2 * lx, lx), BF16),
             pltpu.VMEM((2, width, width), BF16),
+            pltpu.VMEM((gx * gy * gz, PPC, lanes), F32),
             pltpu.SemaphoreType.DMA((3,)),
+            pltpu.SemaphoreType.DMA((gx * gy,)),
         ],
         compiler_params=PARAMS,
         name="planes",
@@ -348,6 +370,33 @@
     )
 
 
+def make_finish(shape):
+    cells_x, cells_y, _, cells_z, slots = shape
+
+    def kernel(result, forces, density, sems):
+        copies = [
+            pltpu.make_async_copy(result.at[:, :, pl.ds(0, 3)], forces, sems.at[0]),
+            pltpu.make_async_copy(result.at[:, :, 3], density, sems.at[1]),
+        ]
+        for copy in copies:
+            copy.start()
+        for copy in copies:
+            copy.wait()
+
+    return pl.pallas_call(
+        kernel,
+        out_shape=(
+            jax.ShapeDtypeStruct((cells_x, cells_y, 3, cells_z, slots), F32),
+            jax.ShapeDtypeStruct((cells_x, cells_y, cells_z, slots), F32),
+        ),
+        in_specs=[VMEM],
+        out_specs=(ANY, ANY),
+        scratch_shapes=[pltpu.SemaphoreType.DMA((2,))],
+        compiler_params=PARAMS,
+        name="finish",
+    )
+
+
 RIGHT = ((0, 0), (1, 0), (1, 0), (2, 0))
 LEFT = ((0, 1), (0, 1), (1, 2), (0, 2))
 
@@ -571,10 +620,12 @@
                     if len(pair) > 1:
                         rhs = [jnp.concatenate(rhs, axis=1)]
                         rhs_extra = [jnp.concatenate(rhs_extra, axis=1)]
-                    weight = jnp.maximum(dot(lhs, rhs[0], NN), 0.0)
+                    bare = dot(lhs, rhs[0], NN)
+                    value = bare * dot(lhs_extra, rhs_extra[0], NN) - 2.0
+                    weight = jnp.maximum(bare, 0.0)
                     if dz == 1 and index == 8:
                         weight = jnp.where(same, 0.0, weight)
-                    value = (weight * dot(lhs_extra, rhs_extra[0], NN) - 2.0) * weight
+                    value = value * weight
                     there = [
                         [place[pl.ds(cell * 8 + d, 1), :] for d in range(3)] for cell in pair
                     ]
@@ -600,7 +651,7 @@
                 sums[d] = jnp.where(lane == n, column, sums[d])
             return carry
 
-        lax.fori_loop(0, own, one_cell, 0, unroll=4)
+        lax.fori_loop(0, own, one_cell, 0, unroll=8)
         rows = [sums[d].T for d in range(4)]
         for y in range(cells_y):
             pos = row_positions(mid, 1, y + 1, sy, nz)
@@ -724,7 +775,8 @@
         near_core(lines), near_core(atoms), near_core(short), near_core(density), species_charge, z_pair
     )
     result = lax.all_to_all(result, "gz", split_axis=0, concat_axis=0, tiled=True)
-    return (result[:, :, 0:3].transpose(0, 1, 3, 2, 4), result[:, :, 3])
+    forces, density = make_finish(result.shape)(near_core(result))
+    return (forces.transpose(0, 1, 3, 2, 4), density)
 
 
 def solution(mesh):

time: 123 us -> 122 us (level)
  local copies, waits for them, and re-layouts: 1.27 us -> 0.04 us
  transfers between devices with their start and end apart: 8 -> 8, of which waited for: 6 -> 6; matrix products, arithmetic and copies ran while one was open for 0% -> 0% of each run, Pallas kernels for 39% -> 38%
where the time goes in v5:
time: 122 us; the launch traced here: 120 us
  Pallas kernels  55.5 us (45%)
  waiting for transfers between devices  23.4 us (19%)
  starting transfers between devices  21.4 us (18%)
  blocking collectives  18 us (15%)
    pallas_call x1, Pallas kernels, on_device(): make_force(cells_y, nz, slots)  29.6 us
    all_to_all x1, waiting for transfers between devices, on_device(): lax.all_to_all(lines, ('gx', 'gy', 'gz'), split_axis=0, concat_axis=0, ti...  13.7 us
    pallas_call x1, Pallas kernels, on_device(): make_density(cells_y, nz, slots)  12.6 us
    all_to_all x1, blocking collectives, on_device(): lax.all_to_all(result, 'gz', split_axis=0, concat_axis=0, tiled=True)  10.6 us
    ppermute x2, starting transfers between devices, shifted(): lax.ppermute(part, axis, down)  7.55 us
    all_to_all x1, blocking collectives, on_device(): atoms = lax.all_to_all(atoms, 'gz', split_axis=0, concat_axis=0, tiled=True)  7.48 us
    ppermute x4, waiting for transfers between devices, shifted(): lax.ppermute(part, axis, up)  5.93 us
    all_to_all x1, starting transfers between devices, on_device(): lax.all_to_all(lines, ('gx', 'gy', 'gz'), split_axis=0, concat_axis=0, ti...  5.67 us
  transfers between devices with their start and end apart: 8, of which 6 were waited for; matrix products, arithmetic and copies ran while one was open for 0% of the time, Pallas kernels for 38%

profile of v5, /device:TPU:1, one launch (start us, length us, event | category | flops | bytes accessed | tf_op | source)
XLA Modules:
  0.0 120.3 jit_solution(13442519058767359355)
XLA Ops:
  0.6 0.0 copy-start.1
  0.6 0.0 copy-start.2
  0.7 0.0 copy-start
  0.7 0.8 convert_bitcast_fusion
  1.5 0.0 copy-done.1
  1.5 0.0 copy-done.2
  1.5 0.1 select_bitcast_fusion
  1.6 0.0 copy-done
  1.6 7.5 %all_to_all.20.atoms = f32[4,2,7,4,128]{4,3,2,1,0:T(4,128)S(1)} all-to-all(f32[4,2,7,4,128]{4,3,2,1,0:T(4,128)S(1)} %pad_maximum_fusion.1), channel_id=1, replica_groups=mesh['gx'=4,'gy'=2,'gz'=4] {'gz'}, dimensions={0} | all-to-all | bytes 229376 | tf_op jit(solution)/shard_map/all_to_all | solution.py:742
  9.1 4.3 %spread.1 = f32[32,16,256]{2,1,0:T(8,128)} custom-call(f32[4,2,7,4,128]{4,3,2,1,0:T(4,128)S(1)} %all_to_all.20.atoms, f32[2]{0:T(128)} %table.3, bf16[2,256,256]{2,1,0:T(8,128)(2,1)} %constant.31.clone.basis_any), custom_call_target="tpu_custom_call" | custom-call | tf_op jit(solution)/shard_map/spread/pallas_call | solution.py:747
  13.4 5.7 %all-to-all-start.1 = ((f32[32,16,256]{2,1,0:T(8,128)}), f32[32,16,256]{2,1,0:T(8,128)S(1)}, u32[]{:S(2)}, u32[]{:S(2)}) async-start(f32[32,16,256]{2,1,0:T(8,128)} %spread.1), calls=%async_computation.1 | async-start | bytes 1048576 | tf_op jit(solution)/shard_map/all_to_all | solution.py:751
  19.1 1.4 %collective-permute-start = (f32[128,128]{1,0:T(8,128)S(1)}, f32[128,128]{1,0:T(8,128)S(1)}, u32[]{:S(2)}, u32[]{:S(2)}) collective-permute-start(f32[128,128]{1,0:T(8,128)S(1)} %bitcast.10), channel_id=1, source_target_pairs={{0,4},{4,0},{1,5},{5,1},{2,6},{6,2},{3,7},{7,3},{8,12},{12,8},{9,1... | collective-permute-start | bytes 196616 | tf_op jit(solution)/shard_map/ppermute | solution.py:693
  20.6 13.7 %all-to-all-done.1.data = f32[32,16,256]{2,1,0:T(8,128)S(1)} async-done(((f32[32,16,256]{2,1,0:T(8,128)}), f32[32,16,256]{2,1,0:T(8,128)S(1)}, u32[]{:S(2)}, u32[]{:S(2)}) %all-to-all-start.1) | async-done | bytes 524320 | tf_op jit(solution)/shard_map/all_to_all | solution.py:751
  34.3 3.6 %planes.1 = f32[32,16,256]{2,1,0:T(8,128)} custom-call(s32[1]{0:T(128)} %bitcast.rank, f32[32,16,256]{2,1,0:T(8,128)S(1)} %all-to-all-done.1.data, bf16[512,256]{1,0:T(8,128)(2,1)} %constant.34.x_any, bf16[512,256]{1,0:T(8,128)(2,1)} %constant.35.xt_any, bf16[2,512,512]{2,1,0:T(8,128)(2,1)} %constant.33.clone.y_any), custom_call_target="tpu_custom_call" | custom-call | tf_op jit(solution)/shard_map/planes/pallas_call | solution.py:764
  37.9 3.4 %all-to-all-start.2 = ((f32[32,16,256]{2,1,0:T(8,128)}), f32[32,16,256]{2,1,0:T(8,128)S(1)}, u32[]{:S(2)}, u32[]{:S(2)}) async-start(f32[32,16,256]{2,1,0:T(8,128)} %planes.1), calls=%async_computation.2 | async-start | bytes 1048576 | tf_op jit(solution)/shard_map/all_to_all | solution.py:767
  41.3 0.0 collective-permute-done
  41.3 1.7 %collective-permute-start.1 = (f32[256,128]{1,0:T(8,128)S(1)}, f32[256,128]{1,0:T(8,128)S(1)}, u32[]{:S(2)}, u32[]{:S(2)}) collective-permute-start(f32[256,128]{1,0:T(8,128)S(1)} %pad_maximum_fusion.mid), channel_id=1, source_target_pairs={{0,1},{1,2},{2,3},{3,8},{8,9},{9,10},{10,11},{11,16},{16,17},{17,1... | collective-permute-start | bytes 393224 | tf_op jit(solution)/shard_map/ppermute | solution.py:693
  43.0 0.0 collective-permute-start.2
  43.0 3.8 %collective-permute-done.1.low = f32[256,128]{1,0:T(8,128)S(1)} collective-permute-done((f32[256,128]{1,0:T(8,128)S(1)}, f32[256,128]{1,0:T(8,128)S(1)}, u32[]{:S(2)}, u32[]{:S(2)}) %collective-permute-start.1) | collective-permute-done | bytes 131104 | tf_op jit(solution)/shard_map/ppermute | solution.py:693
  46.8 3.3 %collective-permute-done.2.high = f32[256,128]{1,0:T(8,128)S(1)} collective-permute-done((f32[256,128]{1,0:T(8,128)S(1)}, f32[256,128]{1,0:T(8,128)S(1)}, u32[]{:S(2)}, u32[]{:S(2)}) %collective-permute-start.2) | collective-permute-done | bytes 131104 | tf_op jit(solution)/shard_map/ppermute | solution.py:693
  50.1 12.6 %density.1 = (f32[2,16,128]{2,1,0:T(8,128)S(1)}, f32[32,128]{1,0:T(8,128)S(1)}) custom-call(f32[256,128]{1,0:T(8,128)S(1)} %collective-permute-done.1.low, f32[256,128]{1,0:T(8,128)S(1)} %pad_maximum_fusion.mid, f32[256,128]{1,0:T(8,128)S(1)} %collective-permute-done.2.high, f32[2]{0:T(128)} %electrons.3, f32[2]{0:T(128)} %embed.1), custom_call_target="tpu_custom_call" | custom-call | flops 566231040 | bytes 393216 | tf_op jit(solution)/shard_map/density/pallas_call | solution.py:758
  62.7 1.0 collective-permute-start.3
  63.7 1.7 %collective-permute-done.3 = f32[32,128]{1,0:T(8,128)S(1)} collective-permute-done((f32[32,128]{1,0:T(8,128)S(1)}, f32[32,128]{1,0:T(8,128)S(1)}, u32[]{:S(2)}, u32[]{:S(2)}) %collective-permute-start.3) | collective-permute-done | bytes 16416 | tf_op jit(solution)/shard_map/ppermute | solution.py:693
  65.4 0.7 collective-permute-start.4
  66.1 7.5 %collective-permute-start.5 = (f32[64,128]{1,0:T(8,128)S(1)}, f32[64,128]{1,0:T(8,128)S(1)}, u32[]{:S(2)}, u32[]{:S(2)}) collective-permute-start(f32[64,128]{1,0:T(8,128)S(1)} %pad_maximum_fusion.2.slope_mid), channel_id=1, source_target_pairs={{1,0},{2,1},{3,2},{8,3},{9,8},{10,9},{11,10},{16,11},{17,16},{18,1... | collective-permute-start | bytes 98312 | tf_op jit(solution)/shard_map/ppermute | solution.py:693
  73.7 0.5 collective-permute-done.4.slope_low
  74.1 0.4 collective-permute-done.5.slope_high
  74.5 29.6 %force.1.short = f32[3,2,16,128]{3,2,1,0:T(8,128)S(1)} custom-call(f32[256,128]{1,0:T(8,128)S(1)} %collective-permute-done.1.low, f32[256,128]{1,0:T(8,128)S(1)} %pad_maximum_fusion.mid, f32[256,128]{1,0:T(8,128)S(1)} %collective-permute-done.2.high, f32[64,128]{1,0:T(8,128)S(1)} %collective-permute-done.4.slope_low, ...), custom_call_target="tpu_custom_call" | custom-call | flops 1415577600 | bytes 393216 | tf_op jit(solution)/shard_map/force/pallas_call | solution.py:773
  104.1 0.0 all-to-all-done.2.data
  104.2 4.7 %sample.1 = f32[4,2,4,4,128]{4,3,2,1,0:T(4,128)S(1)} custom-call(f32[32,16,256]{2,1,0:T(8,128)S(1)} %all-to-all-done.2.data, f32[4,2,7,4,128]{4,3,2,1,0:T(4,128)S(1)} %all_to_all.20.atoms, f32[3,2,16,128]{3,2,1,0:T(8,128)S(1)} %force.1.short, f32[2,16,128]{2,1,0:T(8,128)S(1)} %get-tuple-element.7.dens, f32[2]{0:T(128)} %table.3, ...), custom_call_target="tpu_custom_call" | custom-call | tf_op jit(solution)/shard_map/sample/pallas_call | solution.py:774
  108.9 10.6 %all_to_all.21.result = f32[4,2,4,4,128]{4,3,2,1,0:T(4,128)S(1)} all-to-all(f32[4,2,4,4,128]{4,3,2,1,0:T(4,128)S(1)} %sample.1), channel_id=1, replica_groups=mesh['gx'=4,'gy'=2,'gz'=4] {'gz'}, dimensions={0} | all-to-all | bytes 131072 | tf_op jit(solution)/shard_map/all_to_all | solution.py:777
  119.5 0.6 finish.1
  (9 shorter events, 0.1 us)
Async XLA Ops:
  0.6 0.9 copy-start.1
  0.6 0.9 copy-start.2
  0.7 0.9 copy-start
  13.4 20.9 %all-to-all-start.1 = ((f32[32,16,256]{2,1,0:T(8,128)}), f32[32,16,256]{2,1,0:T(8,128)S(1)}, u32[]{:S(2)}, u32[]{:S(2)}) async-start(f32[32,16,256]{2,1,0:T(8,128)} %spread.1), calls=%async_computation.1 | async-start | bytes 1048576 | tf_op jit(solution)/shard_map/all_to_all | solution.py:751
  19.1 22.1 %collective-permute-start = (f32[128,128]{1,0:T(8,128)S(1)}, f32[128,128]{1,0:T(8,128)S(1)}, u32[]{:S(2)}, u32[]{:S(2)}) collective-permute-start(f32[128,128]{1,0:T(8,128)S(1)} %bitcast.10), channel_id=1, source_target_pairs={{0,4},{4,0},{1,5},{5,1},{2,6},{6,2},{3,7},{7,3},{8,12},{12,8},{9,1... | collective-permute-start | bytes 196616 | tf_op jit(solution)/shard_map/ppermute | solution.py:693
  37.9 66.2 %all-to-all-start.2 = ((f32[32,16,256]{2,1,0:T(8,128)}), f32[32,16,256]{2,1,0:T(8,128)S(1)}, u32[]{:S(2)}, u32[]{:S(2)}) async-start(f32[32,16,256]{2,1,0:T(8,128)} %planes.1), calls=%async_computation.2 | async-start | bytes 1048576 | tf_op jit(solution)/shard_map/all_to_all | solution.py:767
  41.3 5.5 %collective-permute-start.1 = (f32[256,128]{1,0:T(8,128)S(1)}, f32[256,128]{1,0:T(8,128)S(1)}, u32[]{:S(2)}, u32[]{:S(2)}) collective-permute-start(f32[256,128]{1,0:T(8,128)S(1)} %pad_maximum_fusion.mid), channel_id=1, source_target_pairs={{0,1},{1,2},{2,3},{3,8},{8,9},{9,10},{10,11},{11,16},{16,17},{17,1... | collective-permute-start | bytes 393224 | tf_op jit(solution)/shard_map/ppermute | solution.py:693
  43.0 7.1 %collective-permute-start.2 = (f32[256,128]{1,0:T(8,128)S(1)}, f32[256,128]{1,0:T(8,128)S(1)}, u32[]{:S(2)}, u32[]{:S(2)}) collective-permute-start(f32[256,128]{1,0:T(8,128)S(1)} %pad_maximum_fusion.mid), channel_id=1, source_target_pairs={{1,0},{2,1},{3,2},{8,3},{9,8},{10,9},{11,10},{16,11},{17,16},{18,1... | collective-permute-start | bytes 393224 | tf_op jit(solution)/shard_map/ppermute | solution.py:693
  62.7 2.7 %collective-permute-start.3 = (f32[32,128]{1,0:T(8,128)S(1)}, f32[32,128]{1,0:T(8,128)S(1)}, u32[]{:S(2)}, u32[]{:S(2)}) collective-permute-start(f32[32,128]{1,0:T(8,128)S(1)} %get-tuple-element.6), channel_id=1, source_target_pairs={{0,4},{4,0},{1,5},{5,1},{2,6},{6,2},{3,7},{7,3},{8,12},{12,8},{9,1... | collective-permute-start | bytes 49160 | tf_op jit(solution)/shard_map/ppermute | solution.py:693
  65.4 8.8 %collective-permute-start.4 = (f32[64,128]{1,0:T(8,128)S(1)}, f32[64,128]{1,0:T(8,128)S(1)}, u32[]{:S(2)}, u32[]{:S(2)}) collective-permute-start(f32[64,128]{1,0:T(8,128)S(1)} %pad_maximum_fusion.2.slope_mid), channel_id=1, source_target_pairs={{0,1},{1,2},{2,3},{3,8},{8,9},{9,10},{10,11},{11,16},{16,17},{17,1... | collective-permute-start | bytes 98312 | tf_op jit(solution)/shard_map/ppermute | solution.py:693
  66.1 8.4 %collective-permute-start.5 = (f32[64,128]{1,0:T(8,128)S(1)}, f32[64,128]{1,0:T(8,128)S(1)}, u32[]{:S(2)}, u32[]{:S(2)}) collective-permute-start(f32[64,128]{1,0:T(8,128)S(1)} %pad_maximum_fusion.2.slope_mid), channel_id=1, source_target_pairs={{1,0},{2,1},{3,2},{8,3},{9,8},{10,9},{11,10},{16,11},{17,16},{18,1... | collective-permute-start | bytes 98312 | tf_op jit(solution)/shard_map/ppermute | solution.py:693

commit v6 on v5

--- a/solution.py
+++ b/solution.py
@@ -210,12 +210,12 @@
         return jnp.square(signed_modes(indices, length).astype(F32) * (2.0 * math.pi / length))
 
     def kernel(
-        rank, data, x_any, xt_any, y_any, out_any, grid, x_ref, xt_ref, y_ref, out, sems, sends
+        rank, data, x_any, xt_any, y_ref, out_any, grid, x_ref, xt_ref, out, sems, sends
     ):
         fetches = [
             pltpu.make_async_copy(source, target, sems.at[index])
             for index, (source, target) in enumerate(
-                ((x_any, x_ref), (y_any, y_ref), (xt_any, xt_ref))
+                ((x_any, x_ref), (xt_any, xt_ref))
             )
         ]
         for fetch in fetches:
@@ -234,10 +234,9 @@
         green = jnp.where(squared == 0.0, 0.0, factor / jnp.where(squared == 0.0, 1.0, squared))
         fetches[0].wait()
         value = dot3(x_ref[...], split2(grid[...]), NN)
-        fetches[1].wait()
         value = dot3(stack2(value), (y_ref[0], y_ref[1]), NT) * green
         value = dot3(stack2(value), (y_ref[0], y_ref[1]), NN)
-        fetches[2].wait()
+        fetches[1].wait()
         copies = []
         for b in range(gy):
             part = dot3(xt_ref[...], split2(value[:, b * lanes : (b + 1) * lanes]), NN)
@@ -257,15 +256,14 @@
     return pl.pallas_call(
         kernel,
         out_shape=jax.ShapeDtypeStruct((gx * gy * gz, PPC, lanes), F32),
-        in_specs=[SMEM, VMEM, ANY, ANY, ANY],
+        in_specs=[SMEM, VMEM, ANY, ANY, VMEM],
         out_specs=ANY,
         scratch_shapes=[
             pltpu.VMEM((lx, width), F32),
             pltpu.VMEM((2 * lx, lx), BF16),
             pltpu.VMEM((2 * lx, lx), BF16),
-            pltpu.VMEM((2, width, width), BF16),
             pltpu.VMEM((gx * gy * gz, PPC, lanes), F32),
-            pltpu.SemaphoreType.DMA((3,)),
+            pltpu.SemaphoreType.DMA((2,)),
             pltpu.SemaphoreType.DMA((gx * gy,)),
         ],
         compiler_params=PARAMS,
@@ -762,7 +760,7 @@
 
     rank = lax.axis_index(("gx", "gy", "gz")).astype(jnp.int32).reshape(1)
     planes = make_planes(gx, gy, gz, yl * modes, lx, ly, lz)(
-        rank, near_core(planes), x_pair.reshape(2 * lx, lx), xt_pair.reshape(2 * lx, lx), y_pair
+        rank, near_core(planes), x_pair.reshape(2 * lx, lx), xt_pair.reshape(2 * lx, lx), near_core(y_pair)
     )
     lines = lax.all_to_all(planes, ("gx", "gy", "gz"), split_axis=0, concat_axis=0, tiled=True)
     if not relayout:

time: 122 us -> 122 us (level)
  no operation moved by 1% of the time
where the time goes in v6:
time: 122 us; the launch traced here: 120 us
  Pallas kernels  55.5 us (45%)
  waiting for transfers between devices  23.4 us (19%)
  starting transfers between devices  21.4 us (18%)
  blocking collectives  18 us (15%)
    pallas_call x1, Pallas kernels, on_device(): make_force(cells_y, nz, slots)  29.6 us
    all_to_all x1, waiting for transfers between devices, on_device(): lax.all_to_all(lines, ('gx', 'gy', 'gz'), split_axis=0, concat_axis=0, ti...  13.7 us
    pallas_call x1, Pallas kernels, on_device(): make_density(cells_y, nz, slots)  12.6 us
    all_to_all x1, blocking collectives, on_device(): lax.all_to_all(result, 'gz', split_axis=0, concat_axis=0, tiled=True)  10.6 us
    ppermute x2, starting transfers between devices, shifted(): lax.ppermute(part, axis, down)  7.54 us
    all_to_all x1, blocking collectives, on_device(): atoms = lax.all_to_all(atoms, 'gz', split_axis=0, concat_axis=0, tiled=True)  7.48 us
    ppermute x4, waiting for transfers between devices, shifted(): lax.ppermute(part, axis, up)  5.93 us
    all_to_all x1, starting transfers between devices, on_device(): lax.all_to_all(lines, ('gx', 'gy', 'gz'), split_axis=0, concat_axis=0, ti...  5.67 us
  transfers between devices with their start and end apart: 8, of which 6 were waited for; matrix products, arithmetic and copies ran while one was open for 0% of the time, Pallas kernels for 38%

profile of v6, /device:TPU:1, one launch (start us, length us, event | category | flops | bytes accessed | tf_op | source)
XLA Modules:
  0.0 120.2 jit_solution(17651623109260366228)
XLA Ops:
  0.6 0.0 copy-start.2
  0.6 0.0 copy-start.3
  0.7 0.0 copy-start.1
  0.7 0.8 convert_bitcast_fusion
  1.5 0.0 copy-done.2
  1.5 0.0 copy-done.3
  1.5 0.1 select_bitcast_fusion
  1.6 0.0 copy-done.1
  1.6 7.5 %all_to_all.20.atoms = f32[4,2,7,4,128]{4,3,2,1,0:T(4,128)S(1)} all-to-all(f32[4,2,7,4,128]{4,3,2,1,0:T(4,128)S(1)} %pad_maximum_fusion.1), channel_id=1, replica_groups=mesh['gx'=4,'gy'=2,'gz'=4] {'gz'}, dimensions={0} | all-to-all | bytes 229376 | tf_op jit(solution)/shard_map/all_to_all | solution.py:740
  9.1 0.0 copy-start
  9.1 4.4 %spread.1 = f32[32,16,256]{2,1,0:T(8,128)} custom-call(f32[4,2,7,4,128]{4,3,2,1,0:T(4,128)S(1)} %all_to_all.20.atoms, f32[2]{0:T(128)} %table.3, bf16[2,256,256]{2,1,0:T(8,128)(2,1)} %constant.31.clone.basis_any), custom_call_target="tpu_custom_call" | custom-call | tf_op jit(solution)/shard_map/spread/pallas_call | solution.py:745
  13.5 5.7 %all-to-all-start.1 = ((f32[32,16,256]{2,1,0:T(8,128)}), f32[32,16,256]{2,1,0:T(8,128)S(1)}, u32[]{:S(2)}, u32[]{:S(2)}) async-start(f32[32,16,256]{2,1,0:T(8,128)} %spread.1), calls=%async_computation.1 | async-start | bytes 1048576 | tf_op jit(solution)/shard_map/all_to_all | solution.py:749
  19.3 1.4 %collective-permute-start = (f32[128,128]{1,0:T(8,128)S(1)}, f32[128,128]{1,0:T(8,128)S(1)}, u32[]{:S(2)}, u32[]{:S(2)}) collective-permute-start(f32[128,128]{1,0:T(8,128)S(1)} %bitcast.10), channel_id=1, source_target_pairs={{0,4},{4,0},{1,5},{5,1},{2,6},{6,2},{3,7},{7,3},{8,12},{12,8},{9,1... | collective-permute-start | bytes 196616 | tf_op jit(solution)/shard_map/ppermute | solution.py:691
  20.7 13.7 %all-to-all-done.1.data = f32[32,16,256]{2,1,0:T(8,128)S(1)} async-done(((f32[32,16,256]{2,1,0:T(8,128)}), f32[32,16,256]{2,1,0:T(8,128)S(1)}, u32[]{:S(2)}, u32[]{:S(2)}) %all-to-all-start.1) | async-done | bytes 524320 | tf_op jit(solution)/shard_map/all_to_all | solution.py:749
  34.4 0.0 copy-done
  34.4 3.5 %planes.1 = f32[32,16,256]{2,1,0:T(8,128)} custom-call(s32[1]{0:T(128)} %bitcast.rank, f32[32,16,256]{2,1,0:T(8,128)S(1)} %all-to-all-done.1.data, bf16[512,256]{1,0:T(8,128)(2,1)} %constant.34.x_any, bf16[512,256]{1,0:T(8,128)(2,1)} %constant.35.xt_any, bf16[2,512,512]{2,1,0:T(8,128)(2,1)S(1)} %copy-done), custom_call_target="tpu_custom_call" | custom-call | tf_op jit(solution)/shard_map/planes/pallas_call | solution.py:762
  37.9 3.4 %all-to-all-start.2 = ((f32[32,16,256]{2,1,0:T(8,128)}), f32[32,16,256]{2,1,0:T(8,128)S(1)}, u32[]{:S(2)}, u32[]{:S(2)}) async-start(f32[32,16,256]{2,1,0:T(8,128)} %planes.1), calls=%async_computation.2 | async-start | bytes 1048576 | tf_op jit(solution)/shard_map/all_to_all | solution.py:765
  41.3 0.0 collective-permute-done
  41.3 1.7 %collective-permute-start.1 = (f32[256,128]{1,0:T(8,128)S(1)}, f32[256,128]{1,0:T(8,128)S(1)}, u32[]{:S(2)}, u32[]{:S(2)}) collective-permute-start(f32[256,128]{1,0:T(8,128)S(1)} %pad_maximum_fusion.mid), channel_id=1, source_target_pairs={{0,1},{1,2},{2,3},{3,8},{8,9},{9,10},{10,11},{11,16},{16,17},{17,1... | collective-permute-start | bytes 393224 | tf_op jit(solution)/shard_map/ppermute | solution.py:691
  43.0 0.0 collective-permute-start.2
  43.0 3.8 %collective-permute-done.1.low = f32[256,128]{1,0:T(8,128)S(1)} collective-permute-done((f32[256,128]{1,0:T(8,128)S(1)}, f32[256,128]{1,0:T(8,128)S(1)}, u32[]{:S(2)}, u32[]{:S(2)}) %collective-permute-start.1) | collective-permute-done | bytes 131104 | tf_op jit(solution)/shard_map/ppermute | solution.py:691
  46.8 3.3 %collective-permute-done.2.high = f32[256,128]{1,0:T(8,128)S(1)} collective-permute-done((f32[256,128]{1,0:T(8,128)S(1)}, f32[256,128]{1,0:T(8,128)S(1)}, u32[]{:S(2)}, u32[]{:S(2)}) %collective-permute-start.2) | collective-permute-done | bytes 131104 | tf_op jit(solution)/shard_map/ppermute | solution.py:691
  50.1 12.6 %density.1 = (f32[2,16,128]{2,1,0:T(8,128)S(1)}, f32[32,128]{1,0:T(8,128)S(1)}) custom-call(f32[256,128]{1,0:T(8,128)S(1)} %collective-permute-done.1.low, f32[256,128]{1,0:T(8,128)S(1)} %pad_maximum_fusion.mid, f32[256,128]{1,0:T(8,128)S(1)} %collective-permute-done.2.high, f32[2]{0:T(128)} %electrons.3, f32[2]{0:T(128)} %embed.1), custom_call_target="tpu_custom_call" | custom-call | flops 566231040 | bytes 393216 | tf_op jit(solution)/shard_map/density/pallas_call | solution.py:756
  62.7 1.0 collective-permute-start.3
  63.7 1.7 %collective-permute-done.3 = f32[32,128]{1,0:T(8,128)S(1)} collective-permute-done((f32[32,128]{1,0:T(8,128)S(1)}, f32[32,128]{1,0:T(8,128)S(1)}, u32[]{:S(2)}, u32[]{:S(2)}) %collective-permute-start.3) | collective-permute-done | bytes 16416 | tf_op jit(solution)/shard_map/ppermute | solution.py:691
  65.4 0.7 collective-permute-start.4
  66.1 7.5 %collective-permute-start.5 = (f32[64,128]{1,0:T(8,128)S(1)}, f32[64,128]{1,0:T(8,128)S(1)}, u32[]{:S(2)}, u32[]{:S(2)}) collective-permute-start(f32[64,128]{1,0:T(8,128)S(1)} %pad_maximum_fusion.2.slope_mid), channel_id=1, source_target_pairs={{1,0},{2,1},{3,2},{8,3},{9,8},{10,9},{11,10},{16,11},{17,16},{18,1... | collective-permute-start | bytes 98312 | tf_op jit(solution)/shard_map/ppermute | solution.py:691
  73.7 0.5 collective-permute-done.4.slope_low
  74.1 0.4 collective-permute-done.5.slope_high
  74.5 29.6 %force.1.short = f32[3,2,16,128]{3,2,1,0:T(8,128)S(1)} custom-call(f32[256,128]{1,0:T(8,128)S(1)} %collective-permute-done.1.low, f32[256,128]{1,0:T(8,128)S(1)} %pad_maximum_fusion.mid, f32[256,128]{1,0:T(8,128)S(1)} %collective-permute-done.2.high, f32[64,128]{1,0:T(8,128)S(1)} %collective-permute-done.4.slope_low, ...), custom_call_target="tpu_custom_call" | custom-call | flops 1415577600 | bytes 393216 | tf_op jit(solution)/shard_map/force/pallas_call | solution.py:771
  104.1 0.0 all-to-all-done.2.data
  104.1 4.7 %sample.1 = f32[4,2,4,4,128]{4,3,2,1,0:T(4,128)S(1)} custom-call(f32[32,16,256]{2,1,0:T(8,128)S(1)} %all-to-all-done.2.data, f32[4,2,7,4,128]{4,3,2,1,0:T(4,128)S(1)} %all_to_all.20.atoms, f32[3,2,16,128]{3,2,1,0:T(8,128)S(1)} %force.1.short, f32[2,16,128]{2,1,0:T(8,128)S(1)} %get-tuple-element.7.dens, f32[2]{0:T(128)} %table.3, ...), custom_call_target="tpu_custom_call" | custom-call | tf_op jit(solution)/shard_map/sample/pallas_call | solution.py:772
  108.9 10.6 %all_to_all.21.result = f32[4,2,4,4,128]{4,3,2,1,0:T(4,128)S(1)} all-to-all(f32[4,2,4,4,128]{4,3,2,1,0:T(4,128)S(1)} %sample.1), channel_id=1, replica_groups=mesh['gx'=4,'gy'=2,'gz'=4] {'gz'}, dimensions={0} | all-to-all | bytes 131072 | tf_op jit(solution)/shard_map/all_to_all | solution.py:775
  119.4 0.6 finish.1
  (9 shorter events, 0.1 us)
Async XLA Ops:
  0.6 0.9 copy-start.2
  0.6 0.9 copy-start.3
  0.7 0.9 copy-start.1
  9.1 25.3 %copy-start = (bf16[2,512,512]{2,1,0:T(8,128)(2,1)S(1)}, bf16[2,512,512]{2,1,0:T(8,128)(2,1)}, u32[]{:S(2)}) copy-start(bf16[2,512,512]{2,1,0:T(8,128)(2,1)} %constant.33.clone.y_ref) | copy-start | bytes 3145732
  13.5 20.9 %all-to-all-start.1 = ((f32[32,16,256]{2,1,0:T(8,128)}), f32[32,16,256]{2,1,0:T(8,128)S(1)}, u32[]{:S(2)}, u32[]{:S(2)}) async-start(f32[32,16,256]{2,1,0:T(8,128)} %spread.1), calls=%async_computation.1 | async-start | bytes 1048576 | tf_op jit(solution)/shard_map/all_to_all | solution.py:749
  19.3 22.0 %collective-permute-start = (f32[128,128]{1,0:T(8,128)S(1)}, f32[128,128]{1,0:T(8,128)S(1)}, u32[]{:S(2)}, u32[]{:S(2)}) collective-permute-start(f32[128,128]{1,0:T(8,128)S(1)} %bitcast.10), channel_id=1, source_target_pairs={{0,4},{4,0},{1,5},{5,1},{2,6},{6,2},{3,7},{7,3},{8,12},{12,8},{9,1... | collective-permute-start | bytes 196616 | tf_op jit(solution)/shard_map/ppermute | solution.py:691
  37.9 66.2 %all-to-all-start.2 = ((f32[32,16,256]{2,1,0:T(8,128)}), f32[32,16,256]{2,1,0:T(8,128)S(1)}, u32[]{:S(2)}, u32[]{:S(2)}) async-start(f32[32,16,256]{2,1,0:T(8,128)} %planes.1), calls=%async_computation.2 | async-start | bytes 1048576 | tf_op jit(solution)/shard_map/all_to_all | solution.py:765
  41.3 5.5 %collective-permute-start.1 = (f32[256,128]{1,0:T(8,128)S(1)}, f32[256,128]{1,0:T(8,128)S(1)}, u32[]{:S(2)}, u32[]{:S(2)}) collective-permute-start(f32[256,128]{1,0:T(8,128)S(1)} %pad_maximum_fusion.mid), channel_id=1, source_target_pairs={{0,1},{1,2},{2,3},{3,8},{8,9},{9,10},{10,11},{11,16},{16,17},{17,1... | collective-permute-start | bytes 393224 | tf_op jit(solution)/shard_map/ppermute | solution.py:691
  43.0 7.1 %collective-permute-start.2 = (f32[256,128]{1,0:T(8,128)S(1)}, f32[256,128]{1,0:T(8,128)S(1)}, u32[]{:S(2)}, u32[]{:S(2)}) collective-permute-start(f32[256,128]{1,0:T(8,128)S(1)} %pad_maximum_fusion.mid), channel_id=1, source_target_pairs={{1,0},{2,1},{3,2},{8,3},{9,8},{10,9},{11,10},{16,11},{17,16},{18,1... | collective-permute-start | bytes 393224 | tf_op jit(solution)/shard_map/ppermute | solution.py:691
  62.7 2.7 %collective-permute-start.3 = (f32[32,128]{1,0:T(8,128)S(1)}, f32[32,128]{1,0:T(8,128)S(1)}, u32[]{:S(2)}, u32[]{:S(2)}) collective-permute-start(f32[32,128]{1,0:T(8,128)S(1)} %get-tuple-element.6), channel_id=1, source_target_pairs={{0,4},{4,0},{1,5},{5,1},{2,6},{6,2},{3,7},{7,3},{8,12},{12,8},{9,1... | collective-permute-start | bytes 49160 | tf_op jit(solution)/shard_map/ppermute | solution.py:691
  65.4 8.7 %collective-permute-start.4 = (f32[64,128]{1,0:T(8,128)S(1)}, f32[64,128]{1,0:T(8,128)S(1)}, u32[]{:S(2)}, u32[]{:S(2)}) collective-permute-start(f32[64,128]{1,0:T(8,128)S(1)} %pad_maximum_fusion.2.slope_mid), channel_id=1, source_target_pairs={{0,1},{1,2},{2,3},{3,8},{8,9},{9,10},{10,11},{11,16},{16,17},{17,1... | collective-permute-start | bytes 98312 | tf_op jit(solution)/shard_map/ppermute | solution.py:691
  66.1 8.4 %collective-permute-start.5 = (f32[64,128]{1,0:T(8,128)S(1)}, f32[64,128]{1,0:T(8,128)S(1)}, u32[]{:S(2)}, u32[]{:S(2)}) collective-permute-start(f32[64,128]{1,0:T(8,128)S(1)} %pad_maximum_fusion.2.slope_mid), channel_id=1, source_target_pairs={{1,0},{2,1},{3,2},{8,3},{9,8},{10,9},{11,10},{16,11},{17,16},{18,1... | collective-permute-start | bytes 98312 | tf_op jit(solution)/shard_map/ppermute | solution.py:691
